TPU v7x, 1024 devices: a whole 4x8x16 slice. The times are simulated.
1024 devices in a mesh: dp: 4 (over x), cp: 16 (over z), tensor: 16 (over y, core).
Axes of the slice: x: 4, y: 8, z: 16, core: 2. Of those that a mesh axis runs over, the one named last changes fastest.
Arguments:
- x_in: bfloat16 [8192, 16384], P('tensor', ('dp', 'cp')), parts along dimension 1, may hold values from -6 to 6
- z_gate: bfloat16 [8192, 16384], P('tensor', ('dp', 'cp')), parts along dimension 1, may hold values from -6 to 6
- bc_in: bfloat16 [8, 256, 16384], P(None, None, ('dp', 'cp')), parts along dimension 2, may hold values from -6 to 6
- dt_raw: bfloat16 [128, 16384], P('tensor', ('dp', 'cp')), parts along dimension 1, may hold values from -3 to 13
- conv_x_w: float32 [8192, 4], P('tensor'), may hold values from -3 to 3
- conv_x_b: float32 [8192], P('tensor'), may hold values from -1.7 to 0.3
- conv_bc_w: float32 [8, 256, 4], replicated, may hold values from -3 to 3
- conv_bc_b: float32 [8, 256], replicated, may hold values from -1.7 to 0.3
- dt_bias: float32 [128], P('tensor'), may hold values from -10 to -1.5
- a_log: float32 [128], P('tensor'), may hold values from -4.6 to -2
- d_skip: float32 [128], P('tensor'), may hold values from 0.5 to 2
Outputs:
- y_out: bfloat16 [8192, 16384], P('tensor', ('dp', 'cp')), parts along dimension 1
There are 4 independent parts, one for each index of `dp`. A program takes and returns all parts, laid end to end along the dimension named above; an argument that names none is the same for every part. Nothing has to cross between parts.
All inputs are finite; a program needn't handle non-finite values.
Results may differ from a plain program's by a relative error of at most 0.0085.
Values may be sent and summed in bfloat16 or wider, within the bound.
No kernel may reach another device: no remote copies, remote signals or barrier semaphores. Data moves between devices by JAX's collectives and lax.ppermute only.
A program may use at most 32 MiB of HBM per device.

v0:
```python
import jax
import jax.numpy as jnp
from jax import lax
from jax.experimental import pallas as pl
from jax.experimental.pallas import tpu as pltpu
from jax.sharding import Mesh, PartitionSpec as P


HEADS = 128
GROUPS = 8
GROUP_HEADS = HEADS // GROUPS
LO = 4
META = 16

F32 = jnp.float32
BF16 = jnp.bfloat16


def dot(a, b, ca, cb):
    return lax.dot_general(a, b, (((ca,), (cb,)), ((), ())), preferred_element_type=F32)


def silu(v):
    return v / (1.0 + jnp.exp(-v))


def log1p(u):
    return jnp.where(u < 1e-3, u * (1.0 - u * (0.5 - u * (1.0 / 3.0))), jnp.log(1.0 + u))


def softplus(v):
    return jnp.maximum(v, 0.0) + log1p(jnp.exp(-jnp.abs(v)))


def picks(first_lane):
    rows = lax.broadcasted_iota(jnp.int32, (8, 128), 0)
    lanes = lax.broadcasted_iota(jnp.int32, (8, 128), 1)
    return jnp.where(jnp.logical_and(lanes == rows + first_lane, rows < 3), 1.0, 0.0).astype(BF16)


def load_kernel(
    group, bc, bw, x, dt, xw, xb, bb, bias, a_log, skip, last, first, x_out, bc_out, dt_out, x_taps, bc_taps, per_head
):
    channels = x.shape[0]
    heads = dt.shape[0]
    begin, finish = picks(0), picks(125)
    series, mine = x[...], bc[0]
    last[:, :channels] = dot(finish, series[:, 128:], 1, 1).astype(BF16)
    last[:, channels:] = dot(finish, mine[:, 128:], 1, 1).astype(BF16)
    first[:, :channels] = dot(begin, series[:, :128], 1, 1).astype(BF16)
    first[:, channels:] = dot(begin, mine[:, :128], 1, 1).astype(BF16)
    x_out[...] = series
    bc_out[...] = mine
    dt_out[...] = dt[...]
    x_taps[:4, :] = xw[...]
    x_taps[4:, :] = jnp.broadcast_to(xb[...], (4, channels))
    bc_taps[:4, :] = bw[0]
    bc_taps[4:, :] = jnp.broadcast_to(chosen(bb[...], group[0]), (4, mine.shape[0]))
    for i, row in enumerate((bias, a_log, skip)):
        per_head[i] = jnp.broadcast_to(column(row[...]), (heads, 128))


def filtered(series, taps):
    lanes = lax.broadcasted_iota(jnp.int32, (series.shape[0], 128), 1)
    first, second = series[:, :128].astype(F32), series[:, 128:].astype(F32)
    a = taps[:, 4:5] + taps[:, 3:4] * first
    b = taps[:, 4:5] + taps[:, 3:4] * second
    for back in (1, 2, 3):
        moved = pltpu.roll(first, back, 1)
        tap = taps[:, 3 - back : 4 - back]
        a = a + tap * moved
        b = b + tap * jnp.where(lanes < back, moved, pltpu.roll(second, back, 1))
    return jnp.concatenate([silu(a), silu(b)], axis=1).astype(BF16)


def column(row):
    size = row.shape[1]
    same = lax.broadcasted_iota(jnp.int32, (size, size), 0) == lax.broadcasted_iota(jnp.int32, (size, size), 1)
    return jnp.sum(jnp.where(same, row, 0.0), axis=1, keepdims=True)


def chosen(table, group):
    rows = lax.broadcasted_iota(jnp.int32, table.shape, 0)
    return jnp.sum(jnp.where(rows == group, table, 0.0), axis=0, keepdims=True)


def split(value):
    high = value.astype(BF16)
    return high, (value - high.astype(F32)).astype(BF16)


def state_kernel(x, bc, dt, x_taps, bc_taps, per_head, fresh, tails, gains, xc, bcc, cum_out, less_out):
    channels = x.shape[0]
    heads = dt.shape[0]
    width = channels // heads
    states = bc.shape[0] // 2

    delta = softplus(dt[...].astype(F32) + per_head[0][:, :1])
    scaled = delta * -jnp.exp(per_head[1][:, :1])
    high = scaled.astype(BF16)
    mid, low = split(scaled - high.astype(F32))
    size = scaled.shape[1]
    upto = jnp.where(
        lax.broadcasted_iota(jnp.int32, (size, size), 0) <= lax.broadcasted_iota(jnp.int32, (size, size), 1), 1.0, 0.0
    ).astype(BF16)
    cum = dot(low, upto, 1, 0) + dot(mid, upto, 1, 0) + dot(high, upto, 1, 0)
    cum_out[...] = cum
    less_out[...] = cum - jnp.log(delta)
    end = cum[:, size - 1 :]
    gain = delta * jnp.exp(end - cum)
    total_high, total_low = split(jnp.exp(end))
    total_high, total_low = total_high.astype(F32), total_low.astype(F32)

    spread = jnp.where(
        lax.broadcasted_iota(jnp.int32, (heads, channels), 1) // width
        == lax.broadcasted_iota(jnp.int32, (heads, channels), 0),
        1.0,
        0.0,
    ).astype(BF16)
    gain_high, gain_low = split(gain[:, :128])
    gains[...] = (dot(gain_high, spread, 0, 0) + dot(gain_low, spread, 0, 0))[:8]

    bcc[...] = filtered(bc[...], bc_taps[...].T)
    b_rows = bcc[:states, :]
    x_cols = x_taps[...].T
    late = jnp.where(lax.broadcasted_iota(jnp.int32, gain.shape, 1) < 3, 0.0, gain)
    meta = lax.broadcasted_iota(jnp.int32, (META, 128), 0)
    per = heads // LO
    for quarter in range(LO):
        tail = jnp.zeros((META, 128), F32)
        for j in range(per):
            h = quarter * per + j
            at = pl.ds(h * width, width)
            values = filtered(x[at, :], x_cols[h * width : (h + 1) * width])
            xc[at, :] = values
            weighted = (values.astype(F32) * late[h : h + 1]).astype(BF16)
            fresh[at, :] = dot(weighted, b_rows, 1, 1)
            tail = jnp.where(meta == 2 * j, total_high[h : h + 1], tail)
            tail = jnp.where(meta == 2 * j + 1, total_low[h : h + 1], tail)
        tails[quarter] = tail.astype(BF16)


def early(rims, first, taps):
    rows = lax.broadcasted_iota(jnp.int32, rims.shape, 0)
    series = jnp.where(rows < 3, rims, pltpu.roll(first, 3, 0))
    total = taps[4:5] + taps[0:1] * series
    for k in (1, 2, 3):
        total = total + taps[k : k + 1] * pltpu.roll(series, 8 - k, 0)
    return jnp.where(rows < 3, silu(total), 0.0).astype(BF16)


def rim_kernel(rims, first, x_taps, bc_taps, fresh, tails, gains, pay, begun):
    channels = fresh.shape[0]
    states = fresh.shape[1]
    quarter = channels // LO
    r, f = rims[...].astype(F32), first[...].astype(F32)
    x_rows = early(r[:, :channels], f[:, :channels], x_taps[...])
    bc_rows = early(r[:, channels:], f[:, channels:], bc_taps[...])
    begun[:, :channels] = x_rows
    begun[:, channels:] = bc_rows
    weighted = (x_rows.astype(F32) * gains[...]).astype(BF16)
    state = fresh[...] + dot(weighted, bc_rows[:, :states], 0, 0)
    for q in range(LO):
        pay[q, :quarter, :] = state[q * quarter : (q + 1) * quarter].astype(BF16)
        pay[q, quarter:, :] = tails[q]


def unpack(block, per):
    size = block.shape[0] - META
    width = size // per
    tail = block[size:].astype(F32)
    decays = jnp.concatenate(
        [jnp.broadcast_to(tail[2 * j : 2 * j + 1] + tail[2 * j + 1 : 2 * j + 2], (width, 128)) for j in range(per)], axis=0
    )
    return block[:size].astype(F32), decays


def packed(state, decay, out, per):
    size = out.shape[0] - META
    width = size // per
    out[:size, :] = state.astype(BF16)
    meta = lax.broadcasted_iota(jnp.int32, (META, 128), 0)
    tail = jnp.zeros((META, 128), F32)
    for j in range(per):
        d = decay[j * width : j * width + 1]
        high = d.astype(BF16).astype(F32)
        tail = jnp.where(meta == 2 * j, high, tail)
        tail = jnp.where(meta == 2 * j + 1, d - high, tail)
    out[size:, :] = tail.astype(BF16)


def group_kernel(got, kept, out, *, per):
    kept[...] = got[...]
    state, decay = unpack(got[0], per)
    for r in range(1, LO):
        fresh, d = unpack(got[r], per)
        state = fresh + d * state
        decay = decay * d
    packed(state, decay, out, per)


def join_kernel(earlier, later, out, *, per):
    before, decay_before = unpack(earlier[...], per)
    after, decay = unpack(later[...], per)
    packed(after + decay * before, decay * decay_before, out, per)


def entering_kernel(got, *refs, per):
    *given, out = refs
    if given:
        near, next_one, over, between = given
        last, last_decay = unpack(between[...], per)
        state = last + last_decay * unpack(over[...], per)[0]
        state = state + unpack(near[...], per)[0] + unpack(next_one[...], per)[0]
    else:
        state = jnp.zeros(out.shape[1:], F32)
    out[0] = state.astype(BF16)
    for r in range(1, LO):
        fresh, d = unpack(got[r - 1], per)
        state = fresh + d * state
        out[r] = state.astype(BF16)


def copy_kernel(*refs):
    half = len(refs) // 2
    for source, target in zip(refs[:half], refs[half:]):
        target[...] = source[...]


def blank_kernel(*refs):
    for ref in refs:
        ref[...] = jnp.zeros(ref.shape, ref.dtype)


def intra_kernel(xc, bcc, begun, cum_in, less_in, per_head, out, c_out):
    heads = cum_in.shape[0]
    channels = xc.shape[0]
    width = channels // heads
    states = bcc.shape[0] // 2
    cum, less = cum_in[...], less_in[...]
    less_cols = jnp.concatenate([less[:, :128].T, less[:, 128:].T], axis=0)
    skips = per_head[2][:, :1]
    placed = dot(begun[...], picks(0), 0, 0).astype(BF16)

    def mended(values, rows):
        lanes = lax.broadcasted_iota(jnp.int32, rows.shape, 1)
        return jnp.concatenate([jnp.where(lanes < 3, rows, values[:, :128]), values[:, 128:]], axis=1)

    both = mended(bcc[...], placed[channels:])
    c_out[...] = both[states:]
    gram = dot(both[:states], both[states:], 0, 0)
    keep = lax.broadcasted_iota(jnp.int32, (128, 128), 0) <= lax.broadcasted_iota(jnp.int32, (128, 128), 1)
    for h in range(heads):
        at = pl.ds(h * width, width)
        values = mended(xc[at, :], placed[h * width : (h + 1) * width])
        row = cum[h : h + 1]
        col = less_cols[:, h : h + 1]

        def mix(s, t, masked):
            spread = row[:, t : t + 128] - col[s : s + 128]
            if masked:
                spread = jnp.where(keep, spread, -1e30)
            return (gram[s : s + 128, t : t + 128] * jnp.exp(spread)).astype(BF16)

        near = dot(values[:, :128], mix(0, 0, True), 1, 0)
        late = dot(values, jnp.concatenate([mix(0, 128, False), mix(128, 128, True)], axis=0), 1, 0)
        out[at, :] = jnp.concatenate([near, late], axis=1) + skips[h : h + 1] * values.astype(F32)


def output_kernel(inner, c_rows, cum, state, z, out):
    heads = cum.shape[0]
    width = inner.shape[0] // heads
    grown = jnp.exp(cum[...])
    for h in range(heads):
        at = pl.ds(h * width, width)
        y = inner[at, :] + grown[h : h + 1] * dot(state[at, :], c_rows[...], 1, 0)
        y = y.astype(BF16).astype(F32)
        out[at, :] = (y * silu(z[at, :].astype(F32))).astype(BF16)


def shape(*dims, dtype=F32):
    return pltpu.VMEM(dims, dtype)


VMEM = pl.BlockSpec(memory_space=pltpu.VMEM)


def run(kernel, outs, *args):
    args = [pltpu.with_memory_space_constraint(a, pltpu.VMEM) for a in args]
    return pl.pallas_call(kernel, out_shape=outs, in_specs=[VMEM] * len(args), out_specs=[VMEM] * len(outs))(*args)


def local(x_in, z_gate, bc_in, dt_raw, conv_x_w, conv_x_b, conv_bc_w, conv_bc_b, dt_bias, a_log, d_skip):
    heads, length = dt_raw.shape
    channels = x_in.shape[0]
    rows = bc_in.shape[1]
    states = rows // 2
    per = heads // LO
    quarter = channels // LO
    group = (lax.axis_index("tensor") // (GROUP_HEADS // heads)).astype(jnp.int32).reshape(1)
    far = lax.axis_index("far")
    cp = ("far", "near")

    strip = shape(8, channels + rows, dtype=BF16)
    block_shape = shape(quarter + META, states, dtype=BF16)
    kept_shape = shape(LO, quarter + META, states, dtype=BF16)
    series = shape(channels, length, dtype=BF16)
    taps = jnp.swapaxes(conv_bc_w, 1, 2)
    small = [dt_raw, conv_x_w.T, conv_x_b[None], conv_bc_b, dt_bias[None], a_log[None], d_skip[None]]
    last, first, x, bc, dt, x_taps, bc_taps, per_head = pl.pallas_call(
        load_kernel,
        grid_spec=pltpu.PrefetchScalarGridSpec(
            num_scalar_prefetch=1,
            grid=(1,),
            in_specs=[pl.BlockSpec((1,) + a.shape[1:], lambda i, g: (g[0], 0, 0)) for a in (bc_in, taps)]
            + [pl.BlockSpec(a.shape, lambda i, g: (0, 0)) for a in [x_in] + small],
            out_specs=[VMEM] * 8,
        ),
        out_shape=[
            strip,
            strip,
            series,
            shape(rows, length, dtype=BF16),
            shape(heads, length, dtype=BF16),
            shape(8, channels),
            shape(8, rows),
            shape(3, heads, 128),
        ],
        name="load",
    )(group, bc_in, taps, x_in, *small)
    count = lax.axis_size(cp)
    rims = lax.ppermute(last, cp, [(i, i + 1) for i in range(count - 1)])
    fresh, tails, gains, xc, bcc, cum, less = run(
        state_kernel,
        [
            shape(channels, states),
            shape(LO, META, 128, dtype=BF16),
            shape(8, channels),
            series,
            shape(rows, length, dtype=BF16),
            shape(heads, length),
            shape(heads, length),
        ],
        x,
        bc,
        dt,
        x_taps,
        bc_taps,
        per_head,
    )
    pay, begun = run(rim_kernel, [kept_shape, strip], rims, first, x_taps, bc_taps, fresh, tails, gains)

    def gather():
        got = lax.all_to_all(pay, "near", 0, 0, tiled=True)
        return tuple(run(lambda *refs: group_kernel(*refs, per=per), [kept_shape, block_shape], got))

    def blank(*outs):
        return tuple(run(blank_kernel, list(outs)))

    def inside():
        return run(
            intra_kernel,
            [shape(channels, length), shape(states, length, dtype=BF16)],
            xc,
            bcc,
            begun,
            cum,
            less,
            per_head,
        )

    def finish(target, inner, c_rows, kept, *given):
        (entering,) = run(
            lambda *refs: entering_kernel(*refs, per=per), [shape(LO, quarter, states, dtype=BF16)], kept, *given
        )
        state = lax.all_to_all(entering, "near", 0, 0, tiled=True).reshape(channels, states)
        return run(output_kernel, [target], inner, c_rows, cum, state, z_gate)[0]

    def sent(block, source, target):
        pairs = [(source * LO + i, target * LO + i) for i in range(LO)]
        return lax.ppermute(block, cp, pairs)

    def first_branch(kept, block):
        return blank(kept_shape, block_shape) + (finish(series, *inside(), kept),)

    def second_branch(kept, block):
        return gather() + blank(series)

    kept, block = lax.cond(far == 0, gather, lambda: blank(kept_shape, block_shape))
    near = sent(block, 0, 1)
    kept, block, begin = lax.switch(
        jnp.minimum(far, 2),
        [first_branch, second_branch, lambda kept, block: blank(kept_shape, block_shape, series)],
        kept,
        block,
    )
    (joined,) = run(lambda *refs: join_kernel(*refs, per=per), [block_shape], near, block)
    next_one = sent(joined, 1, 2)
    over = sent(joined, 1, 3)
    kept, block = lax.cond(
        far >= 2,
        lambda kept, block: gather(),
        lambda kept, block: tuple(run(copy_kernel, [kept_shape, block_shape], kept, block)),
        kept,
        block,
    )
    between = sent(block, 2, 3)
    inner, c_rows = inside()
    out = jax.ShapeDtypeStruct((channels, length), BF16)
    return lax.cond(
        far == 0,
        lambda begin, *unused: run(copy_kernel, [out], begin)[0],
        lambda begin, *given: finish(out, *given),
        begin,
        inner,
        c_rows,
        kept,
        near,
        next_one,
        over,
        between,
    )


def solution(mesh):
    dp, cp, tensor = mesh.devices.shape
    finer = Mesh(mesh.devices.reshape(dp, cp // LO, LO, tensor), ("dp", "far", "near", "tensor"))
    along = ("dp", "far", "near")
    return jax.shard_map(
        local,
        mesh=finer,
        in_specs=(
            P("tensor", along),
            P("tensor", along),
            P(None, None, along),
            P("tensor", along),
            P("tensor", None),
            P("tensor"),
            P(),
            P(),
            P("tensor"),
            P("tensor"),
            P("tensor"),
        ),
        out_specs=P("tensor", along),
        check_vma=False,
    )
```

profile of v0, /device:TPU:308, one launch (start us, length us, event | category | flops | bytes accessed | tf_op | source)
XLA Modules:
  0.0 48.3 jit_solution(16019236304009761088)
XLA Ops:
  0.0 1.3 %load.1 = (bf16[8,768]{1,0:T(8,128)(2,1)S(1)}, bf16[8,768]{1,0:T(8,128)(2,1)S(1)}, bf16[512,256]{1,0:T(8,128)(2,1)S(1)}, bf16[256,256]{1,0:T(8,128)(2,1)S(1)}, b...) custom-call(s32[1]{0:T(128)} %bitcast.2.group, ...), custom_call_target="tpu_custom_call" | custom-call | tf_op jit(solution)/shard_map/load/pallas_call | solution.py:310
  1.3 4.3 %collective-permute-start = (bf16[8,768]{1,0:T(8,128)(2,1)S(1)}, bf16[8,768]{1,0:T(8,128)(2,1)S(1)}, u32[]{:S(2)}, u32[]{:S(2)}) collective-permute-start(bf16[8,768]{1,0:T(8,128)(2,1)S(1)} %get-tuple-element.113), channel_id=1, source_target_pairs={{0,16},{16,32},{32,48},{48,64},{64,80},{80,96},{96,112},{112,128},... | collective-permute-start | bytes 36872 | tf_op jit(solution)/shard_map/ppermute | solution.py:332
  5.6 1.6 %shard_map.111 = (f32[512,128]{1,0:T(8,128)S(1)}, bf16[4,16,128]{2,1,0:T(8,128)(2,1)S(1)}, f32[8,512]{1,0:T(8,128)S(1)}, bf16[512,256]{1,0:T(8,128)(2,1)S(1)}, b...) custom-call(bf16[512,256]{1,0:T(8,128)(2,1)S(1)} %get-tuple-element.105.x, ...), custom_call_target="tpu_custom_call" | custom-call | tf_op jit(solution)/shard_map/pallas_call | solution.py:290
  7.2 0.9 %collective-permute-done.rims = bf16[8,768]{1,0:T(8,128)(2,1)S(1)} collective-permute-done((bf16[8,768]{1,0:T(8,128)(2,1)S(1)}, bf16[8,768]{1,0:T(8,128)(2,1)S(1)}, u32[]{:S(2)}, u32[]{:S(2)}) %collective-permute-start) | collective-permute-done | bytes 12320 | tf_op jit(solution)/shard_map/ppermute | solution.py:332
  8.1 0.3 shard_map.112
  8.4 0.0 copy-start
  8.4 1.4 %collective-permute-start.1 = (bf16[144,128]{1,0:T(8,128)(2,1)S(1)}, bf16[144,128]{1,0:T(8,128)(2,1)S(1)}, u32[]{:S(2)}, u32[]{:S(2)}) collective-permute-start(bf16[144,128]{1,0:T(8,128)(2,1)S(1)} %get-tuple-element.126), channel_id=1, source_target_pairs={{0,64},{16,80},{32,96},{48,112},{1,65},{17,81},{33,97},{49,113},{2... | collective-permute-start | bytes 110600 | tf_op jit(solution)/shard_map/ppermute | solution.py:381
  9.9 0.0 copy-done
  9.9 13.7 %conditional.5 = ((bf16[4,144,128]{2,1,0:T(8,128)(2,1)S(1)}, bf16[144,128]{1,0:T(8,128)(2,1)S(1)}, bf16[512,256]{1,0:T(8,128)(2,1)S(1)})) conditional(s32[]{:T(128)} %clamp.3, (bf16[512,256]{1,0:T(8,128)(2,1)S(1)}, bf16[256,256]{1,0:T(8,128)(2,1)S(1)}, bf16[8,768]{1,0:T(8,128)(2,1)S(1)}, f32[8,256]{1,0:T(8,128)S(1)}, ...), branch_computations={%region_2.3_spmd, %region_3.4_spmd, %region_4.5_spmd} | conditional | bytes 442432 | solution.py:391
  9.9 7.6 %all-to-all-start.2 = ((bf16[4,144,128]{2,1,0:T(8,128)(2,1)S(1)}), bf16[4,144,128]{2,1,0:T(8,128)(2,1)S(1)}, u32[]{:S(2)}, u32[]{:S(2)}) async-start(bf16[4,144,128]{2,1,0:T(8,128)(2,1)S(1)} %param.3), calls=%async_computation.2 | async-start | bytes 294912 | tf_op jit(solution)/shard_map/cond/branch_1_fun/all_to_all | solution.py:354
  17.5 6.0 %all-to-all-done.2.refs_0_ = bf16[4,144,128]{2,1,0:T(8,128)(2,1)S(1)} async-done(((bf16[4,144,128]{2,1,0:T(8,128)(2,1)S(1)}), bf16[4,144,128]{2,1,0:T(8,128)(2,1)S(1)}, u32[]{:S(2)}, u32[]{:S(2)}) %all-to-all-start.2) | async-done | bytes 147488 | tf_op jit(solution)/shard_map/cond/branch_1_fun/all_to_all | solution.py:354
  23.7 0.7 %collective-permute-start.4 = (bf16[144,128]{1,0:T(8,128)(2,1)S(1)}, bf16[144,128]{1,0:T(8,128)(2,1)S(1)}, u32[]{:S(2)}, u32[]{:S(2)}) collective-permute-start(bf16[144,128]{1,0:T(8,128)(2,1)S(1)} %get-tuple-element.127), channel_id=1, source_target_pairs={{128,192},{144,208},{160,224},{176,240},{129,193},{145,209},{161,2... | collective-permute-start | bytes 110600 | tf_op jit(solution)/shard_map/ppermute | solution.py:381
  24.3 0.0 collective-permute-done.1.refs_0_
  24.4 10.8 %collective-permute-start.3 = (bf16[144,128]{1,0:T(8,128)(2,1)S(1)}, bf16[144,128]{1,0:T(8,128)(2,1)S(1)}, u32[]{:S(2)}, u32[]{:S(2)}) collective-permute-start(bf16[144,128]{1,0:T(8,128)(2,1)S(1)} %shard_map.113), channel_id=1, source_target_pairs={{64,192},{80,208},{96,224},{112,240},{65,193},{81,209},{97,225},{1... | collective-permute-start | bytes 110600 | tf_op jit(solution)/shard_map/ppermute | solution.py:381
  35.2 1.8 %collective-permute-start.2 = (bf16[144,128]{1,0:T(8,128)(2,1)S(1)}, bf16[144,128]{1,0:T(8,128)(2,1)S(1)}, u32[]{:S(2)}, u32[]{:S(2)}) collective-permute-start(bf16[144,128]{1,0:T(8,128)(2,1)S(1)} %shard_map.113), channel_id=1, source_target_pairs={{64,128},{80,144},{96,160},{112,176},{65,129},{81,145},{97,161},{1... | collective-permute-start | bytes 110600 | tf_op jit(solution)/shard_map/ppermute | solution.py:381
  37.0 0.8 %shard_map.114 = (f32[512,256]{1,0:T(8,128)S(1)}, bf16[128,256]{1,0:T(8,128)(2,1)S(1)}) custom-call(bf16[512,256]{1,0:T(8,128)(2,1)S(1)} %get-tuple-element.111.xc, bf16[256,256]{1,0:T(8,128)(2,1)S(1)} %get-tuple-element.112.bcc, bf16[8,768]{1,0:T(8,128)(2,1)S(1)} %get-tuple-element.118.begun, f32[8,256]{1,0:T(8,128)S(1)} %get-tuple-element.119.cum_in, ...), custom_call_target="tpu_custom_call" | custom-call | tf_op jit(solution)/shard_map/pallas_call | solution.py:290
  37.8 0.0 collective-permute-done.4
  37.8 0.0 collective-permute-done.3
  37.9 1.0 %collective-permute-done.2 = bf16[144,128]{1,0:T(8,128)(2,1)S(1)} collective-permute-done((bf16[144,128]{1,0:T(8,128)(2,1)S(1)}, bf16[144,128]{1,0:T(8,128)(2,1)S(1)}, u32[]{:S(2)}, u32[]{:S(2)}) %collective-permute-start.2) | collective-permute-done | bytes 36896 | tf_op jit(solution)/shard_map/ppermute | solution.py:381
  38.9 8.7 %conditional.7 = (bf16[512,256]{1,0:T(8,128)(2,1)S(1)}) conditional(s32[]{:T(128)} %convert_element_type.7, (bf16[4,144,128]{2,1,0:T(8,128)(2,1)S(1)}, bf16[144,128]{1,0:T(8,128)(2,1)S(1)}, bf16[144,128]{1,0:T(8,128)(2,1)S(1)}, bf16[144,128]{1,0:T(8,128)(2,1)S(1)}, bf16[144,128]{1,0:T(8,128)(2,1)S(1)}, /*index=5*/f32[512,256]{1,0:T(8,128)S(1)}, ...), branch_computations={%region_7.8_spmd, %region_8.9_spmd} | conditional | bytes 262152 | solution.py:410
  38.9 8.3 %all_to_all.22 = bf16[4,128,128]{2,1,0:T(8,128)(2,1)S(1)} all-to-all(bf16[4,128,128]{2,1,0:T(8,128)(2,1)S(1)} %branch_0_fun.14), channel_id=1, replica_groups=mesh['dp'=4,'far'=4,'near'=4,'tensor'=16] {'near'}, dimensions={0} | all-to-all | bytes 262144 | tf_op jit(solution)/shard_map/cond/branch_0_fun/all_to_all | solution.py:376
  47.2 0.3 branch_0_fun.15
  47.6 0.0 copy-start.1
  47.6 0.7 %copy-done.1 = bf16[512,256]{1,0:T(8,128)(2,1)} copy-done((bf16[512,256]{1,0:T(8,128)(2,1)}, bf16[512,256]{1,0:T(8,128)(2,1)S(1)}, u32[]{:S(2)}) %copy-start.1) | copy-done | bytes 262168
  (8 shorter events, 0.3 us)
Async XLA Ops:
  1.3 6.8 %collective-permute-start = (bf16[8,768]{1,0:T(8,128)(2,1)S(1)}, bf16[8,768]{1,0:T(8,128)(2,1)S(1)}, u32[]{:S(2)}, u32[]{:S(2)}) collective-permute-start(bf16[8,768]{1,0:T(8,128)(2,1)S(1)} %get-tuple-element.113), channel_id=1, source_target_pairs={{0,16},{16,32},{32,48},{48,64},{64,80},{80,96},{96,112},{112,128},... | collective-permute-start | bytes 36872 | tf_op jit(solution)/shard_map/ppermute | solution.py:332
  8.4 1.5 %copy-start = (bf16[512,256]{1,0:T(8,128)(2,1)S(1)}, bf16[512,256]{1,0:T(8,128)(2,1)}, u32[]{:S(2)}) copy-start(bf16[512,256]{1,0:T(8,128)(2,1)} %param.21) | copy-start | bytes 786436
  8.4 15.9 %collective-permute-start.1 = (bf16[144,128]{1,0:T(8,128)(2,1)S(1)}, bf16[144,128]{1,0:T(8,128)(2,1)S(1)}, u32[]{:S(2)}, u32[]{:S(2)}) collective-permute-start(bf16[144,128]{1,0:T(8,128)(2,1)S(1)} %get-tuple-element.126), channel_id=1, source_target_pairs={{0,64},{16,80},{32,96},{48,112},{1,65},{17,81},{33,97},{49,113},{2... | collective-permute-start | bytes 110600 | tf_op jit(solution)/shard_map/ppermute | solution.py:381
  9.9 13.6 %all-to-all-start.2 = ((bf16[4,144,128]{2,1,0:T(8,128)(2,1)S(1)}), bf16[4,144,128]{2,1,0:T(8,128)(2,1)S(1)}, u32[]{:S(2)}, u32[]{:S(2)}) async-start(bf16[4,144,128]{2,1,0:T(8,128)(2,1)S(1)} %param.3), calls=%async_computation.2 | async-start | bytes 294912 | tf_op jit(solution)/shard_map/cond/branch_1_fun/all_to_all | solution.py:354
  23.7 14.2 %collective-permute-start.4 = (bf16[144,128]{1,0:T(8,128)(2,1)S(1)}, bf16[144,128]{1,0:T(8,128)(2,1)S(1)}, u32[]{:S(2)}, u32[]{:S(2)}) collective-permute-start(bf16[144,128]{1,0:T(8,128)(2,1)S(1)} %get-tuple-element.127), channel_id=1, source_target_pairs={{128,192},{144,208},{160,224},{176,240},{129,193},{145,209},{161,2... | collective-permute-start | bytes 110600 | tf_op jit(solution)/shard_map/ppermute | solution.py:381
  24.4 13.5 %collective-permute-start.3 = (bf16[144,128]{1,0:T(8,128)(2,1)S(1)}, bf16[144,128]{1,0:T(8,128)(2,1)S(1)}, u32[]{:S(2)}, u32[]{:S(2)}) collective-permute-start(bf16[144,128]{1,0:T(8,128)(2,1)S(1)} %shard_map.113), channel_id=1, source_target_pairs={{64,192},{80,208},{96,224},{112,240},{65,193},{81,209},{97,225},{1... | collective-permute-start | bytes 110600 | tf_op jit(solution)/shard_map/ppermute | solution.py:381
  35.2 3.7 %collective-permute-start.2 = (bf16[144,128]{1,0:T(8,128)(2,1)S(1)}, bf16[144,128]{1,0:T(8,128)(2,1)S(1)}, u32[]{:S(2)}, u32[]{:S(2)}) collective-permute-start(bf16[144,128]{1,0:T(8,128)(2,1)S(1)} %shard_map.113), channel_id=1, source_target_pairs={{64,128},{80,144},{96,160},{112,176},{65,129},{81,145},{97,161},{1... | collective-permute-start | bytes 110600 | tf_op jit(solution)/shard_map/ppermute | solution.py:381
  47.6 0.7 %copy-start.1 = (bf16[512,256]{1,0:T(8,128)(2,1)}, bf16[512,256]{1,0:T(8,128)(2,1)S(1)}, u32[]{:S(2)}) copy-start(bf16[512,256]{1,0:T(8,128)(2,1)S(1)} %get-tuple-element.179) | copy-start | bytes 786436
where the time goes:
time: 48.6 us; the launch traced here: 48.3 us
  starting transfers between devices  26.6 us (55%)
  blocking collectives  8.31 us (17%)
  waiting for transfers between devices  7.91 us (16%)
  Pallas kernels  4.49 us (9%)
  local copies, waits for them, and re-layouts  0.7 us (1%)
    ppermute x4, starting transfers between devices, sent(): return lax.ppermute(block, cp, pairs)  14.7 us
    all_to_all x1, blocking collectives, finish(): lax.all_to_all(entering, 'near', 0, 0, tiled=True).reshape(channels, states)  8.31 us
    all_to_all x1, starting transfers between devices, gather(): got = lax.all_to_all(pay, 'near', 0, 0, tiled=True)  7.61 us
    all_to_all x1, waiting for transfers between devices, gather(): got = lax.all_to_all(pay, 'near', 0, 0, tiled=True)  6.01 us
    ppermute x1, starting transfers between devices, local(): rims = lax.ppermute(last, cp, [(i, i + 1) for i in range(count - 1)])  4.29 us
    pallas_call x10, Pallas kernels, run(): pl.pallas_call(kernel, out_shape=outs, in_specs=[VMEM] * len(args), out_s...  3.19 us
    pallas_call x1, Pallas kernels, local(): pl.pallas_call(load_kernel, grid_spec=pltpu.PrefetchScalarGridSpec(num_sc...  1.3 us
    ppermute x4, waiting for transfers between devices, sent(): return lax.ppermute(block, cp, pairs)  1.01 us
  transfers between devices with their start and end apart: 6, of which 3 were waited for; matrix products, arithmetic and copies ran while one was open for 0% of the time, Pallas kernels for 5%

commit v1 on v0

v1 whole, which is shorter than its diff:
```python
import jax
import jax.numpy as jnp
from jax import lax
from jax.experimental import pallas as pl
from jax.experimental.pallas import tpu as pltpu
from jax.sharding import Mesh, PartitionSpec as P


HEADS = 128
GROUPS = 8
GROUP_HEADS = HEADS // GROUPS
LO = 4
META = 32

F32 = jnp.float32
BF16 = jnp.bfloat16


def dot(a, b, ca, cb):
    return lax.dot_general(a, b, (((ca,), (cb,)), ((), ())), preferred_element_type=F32)


def silu(v):
    return v / (1.0 + jnp.exp(-v))


def log1p(u):
    return jnp.where(u < 1e-3, u * (1.0 - u * (0.5 - u * (1.0 / 3.0))), jnp.log(1.0 + u))


def softplus(v):
    return jnp.maximum(v, 0.0) + log1p(jnp.exp(-jnp.abs(v)))


def picks(first_lane):
    rows = lax.broadcasted_iota(jnp.int32, (8, 128), 0)
    lanes = lax.broadcasted_iota(jnp.int32, (8, 128), 1)
    return jnp.where(jnp.logical_and(lanes == rows + first_lane, rows < 3), 1.0, 0.0).astype(BF16)


def load_kernel(
    group, member, bc, bw, x, dt, xw, xb, bb, bias, a_log, skip,
    last, first, x_out, bc_out, dt_out, x_taps, bc_taps, own_taps, per_head,
):
    channels = x.shape[0]
    heads = dt.shape[0]
    begin, finish = picks(0), picks(125)
    series, mine = x[...], bc[0]
    last[:, :channels] = dot(finish, series[:, 128:], 1, 1).astype(BF16)
    last[:, channels:] = dot(finish, mine[:, 128:], 1, 1).astype(BF16)
    first[:, :channels] = dot(begin, series[:, :128], 1, 1).astype(BF16)
    first[:, channels:] = dot(begin, mine[:, :128], 1, 1).astype(BF16)
    x_out[...] = series
    bc_out[...] = mine
    dt_out[...] = dt[...]
    x_taps[:4, :] = xw[...]
    x_taps[4:, :] = jnp.broadcast_to(xb[...], (4, channels))
    own = jnp.zeros(own_taps.shape[1:], F32)
    for q in range(LO):
        own = jnp.where(member[0] == q, x_taps[:, q * 128 : (q + 1) * 128], own)
    own_taps[0] = own
    bc_taps[:4, :] = bw[0]
    bc_taps[4:, :] = jnp.broadcast_to(chosen(bb[...], group[0]), (4, mine.shape[0]))
    own_taps[1] = bc_taps[:, :128]
    for i, row in enumerate((bias, a_log, skip)):
        per_head[i] = jnp.broadcast_to(column(row[...]), (heads, 128))


def filtered(series, taps):
    lanes = lax.broadcasted_iota(jnp.int32, (series.shape[0], 128), 1)
    first, second = series[:, :128].astype(F32), series[:, 128:].astype(F32)
    a = taps[:, 4:5] + taps[:, 3:4] * first
    b = taps[:, 4:5] + taps[:, 3:4] * second
    for back in (1, 2, 3):
        moved = pltpu.roll(first, back, 1)
        tap = taps[:, 3 - back : 4 - back]
        a = a + tap * moved
        b = b + tap * jnp.where(lanes < back, moved, pltpu.roll(second, back, 1))
    return jnp.concatenate([silu(a), silu(b)], axis=1).astype(BF16)


def column(row):
    size = row.shape[1]
    same = lax.broadcasted_iota(jnp.int32, (size, size), 0) == lax.broadcasted_iota(jnp.int32, (size, size), 1)
    return jnp.sum(jnp.where(same, row, 0.0), axis=1, keepdims=True)


def chosen(table, group):
    rows = lax.broadcasted_iota(jnp.int32, table.shape, 0)
    return jnp.sum(jnp.where(rows == group, table, 0.0), axis=0, keepdims=True)


def split(value):
    high = value.astype(BF16)
    return high, (value - high.astype(F32)).astype(BF16)


def state_kernel(x, bc, dt, x_taps, bc_taps, per_head, last, first, pay, xc, bcc, cum_out, less_out):
    channels = x.shape[0]
    heads = dt.shape[0]
    width = channels // heads
    states = bc.shape[0] // 2

    delta = softplus(dt[...].astype(F32) + per_head[0][:, :1])
    scaled = delta * -jnp.exp(per_head[1][:, :1])
    high = scaled.astype(BF16)
    mid, low = split(scaled - high.astype(F32))
    size = scaled.shape[1]
    upto = jnp.where(
        lax.broadcasted_iota(jnp.int32, (size, size), 0) <= lax.broadcasted_iota(jnp.int32, (size, size), 1), 1.0, 0.0
    ).astype(BF16)
    cum = dot(low, upto, 1, 0) + dot(mid, upto, 1, 0) + dot(high, upto, 1, 0)
    cum_out[...] = cum
    less_out[...] = cum - jnp.log(delta)
    end = cum[:, size - 1 :]
    gain = delta * jnp.exp(end - cum)
    total_high, total_low = split(jnp.exp(end))
    total_high, total_low = total_high.astype(F32), total_low.astype(F32)

    spread = jnp.where(
        lax.broadcasted_iota(jnp.int32, (heads, channels), 1) // width
        == lax.broadcasted_iota(jnp.int32, (heads, channels), 0),
        1.0,
        0.0,
    ).astype(BF16)
    gain_high, gain_low = split(gain[:, :128])
    lines = lax.broadcasted_iota(jnp.int32, (8, channels), 0)
    gains = jnp.where(lines < 4, dot(gain_high, spread, 0, 0)[:8], pltpu.roll(dot(gain_low, spread, 0, 0)[:8], 4, 0))
    lines = lax.broadcasted_iota(jnp.int32, last.shape, 0)
    edges = jnp.where(lines < 3, last[...].astype(F32), pltpu.roll(first[...].astype(F32), 3, 0))

    bcc[...] = filtered(bc[...], bc_taps[...].T)
    b_rows = bcc[:states, :]
    x_cols = x_taps[...].T
    late = jnp.where(lax.broadcasted_iota(jnp.int32, gain.shape, 1) < 3, 0.0, gain)
    lines = lax.broadcasted_iota(jnp.int32, (8, 128), 0)
    per = heads // LO
    for quarter in range(LO):
        tail = jnp.zeros((8, 128), F32)
        for j in range(per):
            h = quarter * per + j
            at = pl.ds(h * width, width)
            values = filtered(x[at, :], x_cols[h * width : (h + 1) * width])
            xc[at, :] = values
            weighted = (values.astype(F32) * late[h : h + 1]).astype(BF16)
            pay[quarter, pl.ds(j * width, width), :] = dot(weighted, b_rows, 1, 1).astype(BF16)
            tail = jnp.where(lines == 2 * j, total_high[h : h + 1], tail)
            tail = jnp.where(lines == 2 * j + 1, total_low[h : h + 1], tail)
        here = slice(quarter * 128, (quarter + 1) * 128)
        rows = jnp.concatenate([tail, edges[:, here], edges[:, channels : channels + 128], gains[:, here]], axis=0)
        pay[quarter, pl.ds(per * width, META), :] = rows.astype(BF16)


def early(series, taps):
    rows = lax.broadcasted_iota(jnp.int32, series.shape, 0)
    total = taps[4:5] + taps[0:1] * series
    for k in (1, 2, 3):
        total = total + taps[k : k + 1] * pltpu.roll(series, 8 - k, 0)
    return jnp.where(rows < 3, silu(total), 0.0).astype(BF16)


def rim_state(before, after, taps):
    rows = lax.broadcasted_iota(jnp.int32, (8, 128), 0)
    x_rows = early(jnp.where(rows < 3, before[8:16], after[8:16]), taps[0])
    b_rows = early(jnp.where(rows < 3, before[16:24], after[16:24]), taps[1])
    gains = after[24:32] + pltpu.roll(after[24:32], 4, 0)
    return dot((x_rows.astype(F32) * gains).astype(BF16), b_rows, 0, 0)


def spread_rows(rows, start, per, size):
    width = size // per
    values = [rows[start + 2 * j : start + 2 * j + 1] + rows[start + 2 * j + 1 : start + 2 * j + 2] for j in range(per)]
    return jnp.concatenate([jnp.broadcast_to(v, (width, 128)) for v in values], axis=0)


def unpack(block):
    size = block.shape[0] - META
    return block[:size].astype(F32), block[size:].astype(F32)


def packed_rows(decay, start, rows, per):
    width = decay.shape[0] // per
    lines = lax.broadcasted_iota(jnp.int32, (8, 128), 0)
    for j in range(per):
        d = decay[j * width : j * width + 1]
        high = d.astype(BF16).astype(F32)
        rows = jnp.where(lines == start + 2 * j, high, rows)
        rows = jnp.where(lines == start + 2 * j + 1, d - high, rows)
    return rows


def group_kernel(got, taps, kept, meta, out, *, per, opening):
    size = out.shape[0] - META
    members = [unpack(got[r]) for r in range(LO)]
    lines = lax.broadcasted_iota(jnp.int32, (META, 128), 0)
    state, rows = members[0]
    if opening:
        state = state + rim_state(jnp.zeros_like(rows), rows, taps)
    kept[0] = state
    decay = spread_rows(rows, 0, per, size)
    suffix = jnp.ones_like(decay)
    for r in range(1, LO):
        fresh, now = members[r]
        fresh = fresh + rim_state(members[r - 1][1], now, taps)
        kept[r] = fresh
        d = spread_rows(now, 0, per, size)
        state = fresh + d * state
        decay, suffix = decay * d, suffix * d
    meta[...] = got[:, size:, :]
    out[:size, :] = state.astype(BF16)
    head = packed_rows(suffix, 4, packed_rows(decay, 0, jnp.zeros((8, 128), F32), per), per)
    edge = lax.broadcasted_iota(jnp.int32, (16, 128), 0) % 8 < 3
    edges = jnp.where(edge, members[LO - 1][1][8:24], rows[8:24])
    out[size:, :] = jnp.concatenate([head, edges, rows[24:32]], axis=0).astype(BF16)


def join_kernel(earlier, later, taps, out, *, per):
    size = out.shape[0] - META
    before, rows_before = unpack(earlier[...])
    after, rows = unpack(later[...])
    opening = rim_state(rows_before, rows, taps)
    state = after + spread_rows(rows, 4, per, size) * opening + spread_rows(rows, 0, per, size) * before
    out[:size, :] = state.astype(BF16)
    out[size:, :] = later[size:, :]


def entering_kernel(kept, meta, *refs, per):
    *given, out = refs
    size = kept.shape[1]
    own = meta[0].astype(F32)
    fresh = kept[0]
    state = jnp.zeros(out.shape[1:], F32)
    if given:
        taps, near, next_one, over, between = given
        (near, rows_near), (next_one, rows_next) = unpack(near[...]), unpack(next_one[...])
        (over, rows_over), (between, rows) = unpack(over[...]), unpack(between[...])
        opening = rim_state(rows_over, rows, taps)
        state = between + spread_rows(rows, 4, per, size) * opening + spread_rows(rows, 0, per, size) * over
        state = state + near + next_one
        fresh = fresh + rim_state(rows_near + rows_next + rows, own, taps)
    out[0] = state.astype(BF16)
    for r in range(1, LO):
        state = fresh + spread_rows(meta[r - 1].astype(F32), 0, per, size) * state
        out[r] = state.astype(BF16)
        fresh = kept[r]


def copy_kernel(*refs):
    half = len(refs) // 2
    for source, target in zip(refs[:half], refs[half:]):
        target[...] = source[...]


def blank_kernel(*refs):
    for ref in refs:
        ref[...] = jnp.zeros(ref.shape, ref.dtype)


def intra_kernel(xc, bcc, rims, first, x_taps, bc_taps, cum_in, less_in, per_head, out, c_out):
    heads = cum_in.shape[0]
    channels = xc.shape[0]
    width = channels // heads
    states = bcc.shape[0] // 2
    cum, less = cum_in[...], less_in[...]
    less_cols = jnp.concatenate([less[:, :128].T, less[:, 128:].T], axis=0)
    skips = per_head[2][:, :1]
    lines = lax.broadcasted_iota(jnp.int32, rims.shape, 0)
    edges = jnp.where(lines < 3, rims[...].astype(F32), pltpu.roll(first[...].astype(F32), 3, 0))
    begun = [early(edges[:, :channels], x_taps[...]), early(edges[:, channels:], bc_taps[...])]
    placed = dot(jnp.concatenate(begun, axis=1), picks(0), 0, 0).astype(BF16)

    def mended(values, rows):
        lanes = lax.broadcasted_iota(jnp.int32, rows.shape, 1)
        return jnp.concatenate([jnp.where(lanes < 3, rows, values[:, :128]), values[:, 128:]], axis=1)

    both = mended(bcc[...], placed[channels:])
    c_out[...] = both[states:]
    gram = dot(both[:states], both[states:], 0, 0)
    keep = lax.broadcasted_iota(jnp.int32, (128, 128), 0) <= lax.broadcasted_iota(jnp.int32, (128, 128), 1)
    for h in range(heads):
        at = pl.ds(h * width, width)
        values = mended(xc[at, :], placed[h * width : (h + 1) * width])
        row = cum[h : h + 1]
        col = less_cols[:, h : h + 1]

        def mix(s, t, masked):
            spread = row[:, t : t + 128] - col[s : s + 128]
            if masked:
                spread = jnp.where(keep, spread, -1e30)
            return (gram[s : s + 128, t : t + 128] * jnp.exp(spread)).astype(BF16)

        near = dot(values[:, :128], mix(0, 0, True), 1, 0)
        late = dot(values, jnp.concatenate([mix(0, 128, False), mix(128, 128, True)], axis=0), 1, 0)
        out[at, :] = jnp.concatenate([near, late], axis=1) + skips[h : h + 1] * values.astype(F32)


def output_kernel(inner, c_rows, cum, state, z, out):
    heads = cum.shape[0]
    width = inner.shape[0] // heads
    grown = jnp.exp(cum[...])
    for h in range(heads):
        at = pl.ds(h * width, width)
        y = inner[at, :] + grown[h : h + 1] * dot(state[at, :], c_rows[...], 1, 0)
        y = y.astype(BF16).astype(F32)
        out[at, :] = (y * silu(z[at, :].astype(F32))).astype(BF16)


def shape(*dims, dtype=F32):
    return pltpu.VMEM(dims, dtype)


VMEM = pl.BlockSpec(memory_space=pltpu.VMEM)


def run(kernel, outs, *args):
    args = [pltpu.with_memory_space_constraint(a, pltpu.VMEM) for a in args]
    return pl.pallas_call(kernel, out_shape=outs, in_specs=[VMEM] * len(args), out_specs=[VMEM] * len(outs))(*args)


def local(x_in, z_gate, bc_in, dt_raw, conv_x_w, conv_x_b, conv_bc_w, conv_bc_b, dt_bias, a_log, d_skip):
    heads, length = dt_raw.shape
    channels = x_in.shape[0]
    rows = bc_in.shape[1]
    states = rows // 2
    per = heads // LO
    quarter = channels // LO
    group = (lax.axis_index("tensor") // (GROUP_HEADS // heads)).astype(jnp.int32).reshape(1)
    member = lax.axis_index("near").astype(jnp.int32).reshape(1)
    far = lax.axis_index("far")
    cp = ("far", "near")
    count = lax.axis_size(cp)

    strip = shape(8, channels + rows, dtype=BF16)
    block_shape = shape(quarter + META, states, dtype=BF16)
    kept_shapes = [shape(LO, quarter, states), shape(LO, META, states, dtype=BF16)]
    state_shape = shape(LO, quarter, states, dtype=BF16)
    series = shape(channels, length, dtype=BF16)
    pairs = shape(rows, length, dtype=BF16)
    taps = jnp.swapaxes(conv_bc_w, 1, 2)
    small = [dt_raw, conv_x_w.T, conv_x_b[None], conv_bc_b, dt_bias[None], a_log[None], d_skip[None]]
    outs = [strip, strip, series, pairs, shape(heads, length, dtype=BF16), shape(8, channels), shape(8, rows)]
    outs += [shape(2, 8, 128), shape(3, heads, 128)]
    last, first, x, bc, dt, x_taps, bc_taps, own_taps, per_head = pl.pallas_call(
        load_kernel,
        grid_spec=pltpu.PrefetchScalarGridSpec(
            num_scalar_prefetch=2,
            grid=(1,),
            in_specs=[pl.BlockSpec((1,) + a.shape[1:], lambda i, g, m: (g[0], 0, 0)) for a in (bc_in, taps)]
            + [pl.BlockSpec(a.shape, lambda i, g, m: (0, 0)) for a in [x_in] + small],
            out_specs=[VMEM] * len(outs),
        ),
        out_shape=outs,
        name="load",
    )(group, member, bc_in, taps, x_in, *small)
    pay, xc, bcc, cum, less = run(
        state_kernel,
        [shape(LO, quarter + META, states, dtype=BF16), series, pairs, shape(heads, length), shape(heads, length)],
        x,
        bc,
        dt,
        x_taps,
        bc_taps,
        per_head,
        last,
        first,
    )

    def gather(opening=False):
        got = lax.all_to_all(pay, "near", 0, 0, tiled=True)
        kernel = lambda *refs: group_kernel(*refs, per=per, opening=opening)
        return tuple(run(kernel, kept_shapes + [block_shape], got, own_taps))

    def blank(*outs):
        return tuple(run(blank_kernel, list(outs)))

    def exchange(*given):
        (entering,) = run(lambda *refs: entering_kernel(*refs, per=per), [state_shape], *given)
        return lax.all_to_all(entering, "near", 0, 0, tiled=True)

    def sent(block, source, target):
        route = [(source * LO + i, target * LO + i) for i in range(LO)]
        return lax.ppermute(block, cp, route)

    def kept_on(*arrays):
        return tuple(run(copy_kernel, kept_shapes + [block_shape], *arrays))

    kept = lax.cond(far == 0, lambda: gather(True), lambda: blank(*kept_shapes, block_shape))
    near = sent(kept[2], 0, 1)
    *kept, begin = lax.switch(
        jnp.minimum(far, 2),
        [
            lambda *kept: blank(*kept_shapes, block_shape) + (exchange(*kept[:2]),),
            lambda *kept: gather() + blank(state_shape),
            lambda *kept: blank(*kept_shapes, block_shape, state_shape),
        ],
        *kept,
    )
    (joined,) = run(lambda *refs: join_kernel(*refs, per=per), [block_shape], near, kept[2], own_taps)
    next_one = sent(joined, 1, 2)
    over = sent(joined, 1, 3)
    kept = lax.cond(far >= 2, lambda *kept: gather(), kept_on, *kept)
    between = sent(kept[2], 2, 3)
    rims = lax.ppermute(last, cp, [(i, i + 1) for i in range(count - 1)])
    inner, c_rows = run(
        intra_kernel,
        [shape(channels, length), shape(states, length, dtype=BF16)],
        xc,
        bcc,
        rims,
        first,
        x_taps,
        bc_taps,
        cum,
        less,
        per_head,
    )
    state = lax.cond(
        far == 0,
        lambda begin, *unused: run(copy_kernel, [state_shape], begin)[0],
        lambda begin, *given: exchange(*given),
        begin,
        *kept[:2],
        own_taps,
        near,
        next_one,
        over,
        between,
    ).reshape(channels, states)
    out = jax.ShapeDtypeStruct((channels, length), BF16)
    return run(output_kernel, [out], inner, c_rows, cum, state, z_gate)[0]


def solution(mesh):
    dp, cp, tensor = mesh.devices.shape
    finer = Mesh(mesh.devices.reshape(dp, cp // LO, LO, tensor), ("dp", "far", "near", "tensor"))
    along = ("dp", "far", "near")
    return jax.shard_map(
        local,
        mesh=finer,
        in_specs=(
            P("tensor", along),
            P("tensor", along),
            P(None, None, along),
            P("tensor", along),
            P("tensor", None),
            P("tensor"),
            P(),
            P(),
            P("tensor"),
            P("tensor"),
            P("tensor"),
        ),
        out_specs=P("tensor", along),
        check_vma=False,
    )
```

time: 48.6 us -> 51.7 us (1.064)
  the two profiles are of different devices: /device:TPU:308 before, /device:TPU:300 now
where the time goes in v1:
time: 51.7 us; the launch traced here: 51.3 us
  starting transfers between devices  26.5 us (51%)
  waiting for transfers between devices  10.6 us (21%)
  blocking collectives  8.31 us (16%)
  Pallas kernels  5.68 us (11%)
    ppermute x4, starting transfers between devices, sent(): return lax.ppermute(block, cp, route)  16.8 us
    all_to_all x1, blocking collectives, exchange(): return lax.all_to_all(entering, 'near', 0, 0, tiled=True)  8.31 us
    all_to_all x1, starting transfers between devices, gather(): got = lax.all_to_all(pay, 'near', 0, 0, tiled=True)  7.27 us
    all_to_all x1, waiting for transfers between devices, gather(): got = lax.all_to_all(pay, 'near', 0, 0, tiled=True)  6.19 us
    ppermute x1, waiting for transfers between devices, local(): rims = lax.ppermute(last, cp, [(i, i + 1) for i in range(count - 1)])  4.39 us
    pallas_call x9, Pallas kernels, run(): pl.pallas_call(kernel, out_shape=outs, in_specs=[VMEM] * len(args), out_s...  4.34 us
    ppermute x1, starting transfers between devices, local(): rims = lax.ppermute(last, cp, [(i, i + 1) for i in range(count - 1)])  2.41 us
    pallas_call x1, Pallas kernels, local(): pl.pallas_call(load_kernel, grid_spec=pltpu.PrefetchScalarGridSpec(num_sc...  1.34 us
  transfers between devices with their start and end apart: 6, of which 2 were waited for; matrix products, arithmetic and copies ran while one was open for 0% of the time, Pallas kernels for 3%

profile of v1, /device:TPU:300, one launch (start us, length us, event | category | flops | bytes accessed | tf_op | source)
XLA Modules:
  0.0 51.3 jit_solution(2129068427805573463)
XLA Ops:
  0.0 1.3 %load.1 = (bf16[8,768]{1,0:T(8,128)(2,1)S(1)}, bf16[8,768]{1,0:T(8,128)(2,1)S(1)}, bf16[512,256]{1,0:T(8,128)(2,1)S(1)}, bf16[256,256]{1,0:T(8,128)(2,1)S(1)}, b...) custom-call(s32[1]{0:T(128)} %bitcast.2.group, ...), custom_call_target="tpu_custom_call" | custom-call | tf_op jit(solution)/shard_map/load/pallas_call | solution.py:343
  1.3 1.7 %shard_map.109 = (bf16[4,160,128]{2,1,0:T(8,128)(2,1)S(1)}, bf16[512,256]{1,0:T(8,128)(2,1)S(1)}, bf16[256,256]{1,0:T(8,128)(2,1)S(1)}, f32[8,256]{1,0:T(8,128)S(1)}, f32[8,256]{1,0:T(8,128)S(1)}) custom-call(bf16[512,256]{1,0:T(8,128)(2,1)S(1)} %get-tuple-element.101.x, bf16[256,256]{1,0:T(8,128)(2,1)S(1)} %get-tuple-element.102.bc, ...), custom_call_target="tpu_custom_call" | custom-call | tf_op jit(solution)/shard_map/pallas_call | solution.py:317
  3.0 0.1 conditional.4
  3.1 1.3 %collective-permute-start.1 = (bf16[160,128]{1,0:T(8,128)(2,1)S(1)}, bf16[160,128]{1,0:T(8,128)(2,1)S(1)}, u32[]{:S(2)}, u32[]{:S(2)}) collective-permute-start(bf16[160,128]{1,0:T(8,128)(2,1)S(1)} %get-tuple-element.124), channel_id=1, source_target_pairs={{0,64},{16,80},{32,96},{48,112},{1,65},{17,81},{33,97},{49,113},{2... | collective-permute-start | bytes 122888 | tf_op jit(solution)/shard_map/ppermute | solution.py:382
  4.4 13.8 %conditional.5 = ((f32[4,128,128]{2,1,0:T(8,128)S(1)}, bf16[4,32,128]{2,1,0:T(8,128)(2,1)S(1)}, bf16[160,128]{1,0:T(8,128)(2,1)S(1)}, bf16[4,128,128]{2,1,0:T(8,128)(2,1)S(1)})) conditional(s32[]{:T(128)} %clamp.3, (f32[4,128,128]{2,1,0:T(8,128)S(1)}, bf16[4,32,128]{2,1,0:T(8,128)(2,1)S(1)}) %tuple.44, ...), branch_computations={%region_2.3_spmd, %region_3.4_spmd, %region_4.5_spmd} | conditional | bytes 491592 | solution.py:389
  4.4 7.3 %all-to-all-start.2 = ((bf16[4,160,128]{2,1,0:T(8,128)(2,1)S(1)}), bf16[4,160,128]{2,1,0:T(8,128)(2,1)S(1)}, u32[]{:S(2)}, u32[]{:S(2)}) async-start(bf16[4,160,128]{2,1,0:T(8,128)(2,1)S(1)} %get-tuple-element.58), calls=%async_computation.2 | async-start | bytes 327680 | tf_op jit(solution)/shard_map/cond/branch_1_fun/all_to_all | solution.py:369
  11.7 6.2 %all-to-all-done.2.refs_0_ = bf16[4,160,128]{2,1,0:T(8,128)(2,1)S(1)} async-done(((bf16[4,160,128]{2,1,0:T(8,128)(2,1)S(1)}), bf16[4,160,128]{2,1,0:T(8,128)(2,1)S(1)}, u32[]{:S(2)}, u32[]{:S(2)}) %all-to-all-start.2) | async-done | bytes 163872 | tf_op jit(solution)/shard_map/cond/branch_1_fun/all_to_all | solution.py:369
  17.9 0.2 branch_1_fun.6
  18.2 0.7 %collective-permute-start.4 = (bf16[160,128]{1,0:T(8,128)(2,1)S(1)}, bf16[160,128]{1,0:T(8,128)(2,1)S(1)}, u32[]{:S(2)}, u32[]{:S(2)}) collective-permute-start(bf16[160,128]{1,0:T(8,128)(2,1)S(1)} %get-tuple-element.125), channel_id=1, source_target_pairs={{128,192},{144,208},{160,224},{176,240},{129,193},{145,209},{161,2... | collective-permute-start | bytes 122888 | tf_op jit(solution)/shard_map/ppermute | solution.py:382
  18.9 0.0 collective-permute-done.1.refs_0_
  18.9 0.2 shard_map.111
  19.1 13.6 %collective-permute-start.2 = (bf16[160,128]{1,0:T(8,128)(2,1)S(1)}, bf16[160,128]{1,0:T(8,128)(2,1)S(1)}, u32[]{:S(2)}, u32[]{:S(2)}) collective-permute-start(bf16[160,128]{1,0:T(8,128)(2,1)S(1)} %shard_map.111), channel_id=1, source_target_pairs={{64,128},{80,144},{96,160},{112,176},{65,129},{81,145},{97,161},{1... | collective-permute-start | bytes 122888 | tf_op jit(solution)/shard_map/ppermute | solution.py:382
  32.7 1.3 %collective-permute-start.3 = (bf16[160,128]{1,0:T(8,128)(2,1)S(1)}, bf16[160,128]{1,0:T(8,128)(2,1)S(1)}, u32[]{:S(2)}, u32[]{:S(2)}) collective-permute-start(bf16[160,128]{1,0:T(8,128)(2,1)S(1)} %shard_map.111), channel_id=1, source_target_pairs={{64,192},{80,208},{96,224},{112,240},{65,193},{81,209},{97,225},{1... | collective-permute-start | bytes 122888 | tf_op jit(solution)/shard_map/ppermute | solution.py:382
  34.0 2.4 %collective-permute-start = (bf16[8,768]{1,0:T(8,128)(2,1)S(1)}, bf16[8,768]{1,0:T(8,128)(2,1)S(1)}, u32[]{:S(2)}, u32[]{:S(2)}) collective-permute-start(bf16[8,768]{1,0:T(8,128)(2,1)S(1)} %get-tuple-element.107.last), channel_id=1, source_target_pairs={{0,16},{16,32},{32,48},{48,64},{64,80},{80,96},{96,112},{112,128},... | collective-permute-start | bytes 36872 | tf_op jit(solution)/shard_map/ppermute | solution.py:403
  36.4 4.4 %collective-permute-done.rims = bf16[8,768]{1,0:T(8,128)(2,1)S(1)} collective-permute-done((bf16[8,768]{1,0:T(8,128)(2,1)S(1)}, bf16[8,768]{1,0:T(8,128)(2,1)S(1)}, u32[]{:S(2)}, u32[]{:S(2)}) %collective-permute-start) | collective-permute-done | bytes 12320 | tf_op jit(solution)/shard_map/ppermute | solution.py:403
  40.8 0.8 %shard_map.110 = (f32[512,256]{1,0:T(8,128)S(1)}, bf16[128,256]{1,0:T(8,128)(2,1)S(1)}) custom-call(bf16[512,256]{1,0:T(8,128)(2,1)S(1)} %get-tuple-element.109.xc, bf16[256,256]{1,0:T(8,128)(2,1)S(1)} %get-tuple-element.110.bcc, bf16[8,768]{1,0:T(8,128)(2,1)S(1)} %collective-permute-done.rims, bf16[8,768]{1,0:T(8,128)(2,1)S(1)} %get-tuple-element.108.first, ...), custom_call_target="tpu_custom_call" | custom-call | tf_op jit(solution)/shard_map/pallas_call | solution.py:317
  41.7 0.0 collective-permute-done.4
  41.7 0.0 collective-permute-done.2
  41.7 0.0 collective-permute-done.3
  41.7 0.0 copy-start
  41.7 8.6 %conditional.7 = (bf16[512,128]{1,0:T(8,128)(2,1)S(1)}) conditional(s32[]{:T(128)} %convert_element_type.7, (f32[4,128,128]{2,1,0:T(8,128)S(1)}, bf16[4,32,128]{2,1,0:T(8,128)(2,1)S(1)}, f32[2,8,128]{2,1,0:T(8,128)S(1)}, bf16[160,128]{1,0:T(8,128)(2,1)S(1)}, bf16[160,128]{1,0:T(8,128)(2,1)S(1)}, /*index=5*/bf16[160,128]{1,0:T(8,128)(2,1)S(1)}, ...), branch_computations={%region_7.8_spmd, %region_8.9_spmd} | conditional | bytes 262152 | solution.py:417
  41.7 0.2 branch_0_fun.9
  42.0 8.3 %all_to_all.22 = bf16[4,128,128]{2,1,0:T(8,128)(2,1)S(1)} all-to-all(bf16[4,128,128]{2,1,0:T(8,128)(2,1)S(1)} %branch_0_fun.9), channel_id=1, replica_groups=mesh['dp'=4,'far'=4,'near'=4,'tensor'=16] {'near'}, dimensions={0} | all-to-all | bytes 262144 | tf_op jit(solution)/shard_map/cond/branch_0_fun/all_to_all | solution.py:378
  50.3 0.0 copy-done
  50.3 1.0 %shard_map.112 = bf16[512,256]{1,0:T(8,128)(2,1)} custom-call(f32[512,256]{1,0:T(8,128)S(1)} %get-tuple-element.113.inner, bf16[128,256]{1,0:T(8,128)(2,1)S(1)} %get-tuple-element.114.c_rows, f32[8,256]{1,0:T(8,128)S(1)} %get-tuple-element.111.cum_in.cum, bf16[512,128]{1,0:T(8,128)(2,1)S(1)} %get-tuple-element.154.state, bf16[512,256]{1,0:T(8,128)(2,1)S(1)} %copy-done), custom_call_target="tpu_custom_call" | custom-call | tf_op jit(solution)/shard_map/pallas_call | solution.py:317
  (4 shorter events, 0.1 us)
Async XLA Ops:
  3.1 15.8 %collective-permute-start.1 = (bf16[160,128]{1,0:T(8,128)(2,1)S(1)}, bf16[160,128]{1,0:T(8,128)(2,1)S(1)}, u32[]{:S(2)}, u32[]{:S(2)}) collective-permute-start(bf16[160,128]{1,0:T(8,128)(2,1)S(1)} %get-tuple-element.124), channel_id=1, source_target_pairs={{0,64},{16,80},{32,96},{48,112},{1,65},{17,81},{33,97},{49,113},{2... | collective-permute-start | bytes 122888 | tf_op jit(solution)/shard_map/ppermute | solution.py:382
  4.4 13.5 %all-to-all-start.2 = ((bf16[4,160,128]{2,1,0:T(8,128)(2,1)S(1)}), bf16[4,160,128]{2,1,0:T(8,128)(2,1)S(1)}, u32[]{:S(2)}, u32[]{:S(2)}) async-start(bf16[4,160,128]{2,1,0:T(8,128)(2,1)S(1)} %get-tuple-element.58), calls=%async_computation.2 | async-start | bytes 327680 | tf_op jit(solution)/shard_map/cond/branch_1_fun/all_to_all | solution.py:369
  18.2 23.4 %collective-permute-start.4 = (bf16[160,128]{1,0:T(8,128)(2,1)S(1)}, bf16[160,128]{1,0:T(8,128)(2,1)S(1)}, u32[]{:S(2)}, u32[]{:S(2)}) collective-permute-start(bf16[160,128]{1,0:T(8,128)(2,1)S(1)} %get-tuple-element.125), channel_id=1, source_target_pairs={{128,192},{144,208},{160,224},{176,240},{129,193},{145,209},{161,2... | collective-permute-start | bytes 122888 | tf_op jit(solution)/shard_map/ppermute | solution.py:382
  19.1 22.6 %collective-permute-start.2 = (bf16[160,128]{1,0:T(8,128)(2,1)S(1)}, bf16[160,128]{1,0:T(8,128)(2,1)S(1)}, u32[]{:S(2)}, u32[]{:S(2)}) collective-permute-start(bf16[160,128]{1,0:T(8,128)(2,1)S(1)} %shard_map.111), channel_id=1, source_target_pairs={{64,128},{80,144},{96,160},{112,176},{65,129},{81,145},{97,161},{1... | collective-permute-start | bytes 122888 | tf_op jit(solution)/shard_map/ppermute | solution.py:382
  32.7 9.0 %collective-permute-start.3 = (bf16[160,128]{1,0:T(8,128)(2,1)S(1)}, bf16[160,128]{1,0:T(8,128)(2,1)S(1)}, u32[]{:S(2)}, u32[]{:S(2)}) collective-permute-start(bf16[160,128]{1,0:T(8,128)(2,1)S(1)} %shard_map.111), channel_id=1, source_target_pairs={{64,192},{80,208},{96,224},{112,240},{65,193},{81,209},{97,225},{1... | collective-permute-start | bytes 122888 | tf_op jit(solution)/shard_map/ppermute | solution.py:382
  34.0 6.8 %collective-permute-start = (bf16[8,768]{1,0:T(8,128)(2,1)S(1)}, bf16[8,768]{1,0:T(8,128)(2,1)S(1)}, u32[]{:S(2)}, u32[]{:S(2)}) collective-permute-start(bf16[8,768]{1,0:T(8,128)(2,1)S(1)} %get-tuple-element.107.last), channel_id=1, source_target_pairs={{0,16},{16,32},{32,48},{48,64},{64,80},{80,96},{96,112},{112,128},... | collective-permute-start | bytes 36872 | tf_op jit(solution)/shard_map/ppermute | solution.py:403
  41.7 8.6 %copy-start = (bf16[512,256]{1,0:T(8,128)(2,1)S(1)}, bf16[512,256]{1,0:T(8,128)(2,1)}, u32[]{:S(2)}) copy-start(bf16[512,256]{1,0:T(8,128)(2,1)} %z.1) | copy-start | bytes 786436

commit v2 on v1

--- a/solution.py
+++ b/solution.py
@@ -95,7 +95,11 @@
     return high, (value - high.astype(F32)).astype(BF16)
 
 
-def state_kernel(x, bc, dt, x_taps, bc_taps, per_head, last, first, pay, xc, bcc, cum_out, less_out):
+def state_kernel(
+    z, x, bc, dt, x_taps, bc_taps, per_head, last, first, pay, xc, bcc, cum_out, less_out, z_out, done
+):
+    fetch = pltpu.make_async_copy(z, z_out, done)
+    fetch.start()
     channels = x.shape[0]
     heads = dt.shape[0]
     width = channels // heads
@@ -149,6 +153,7 @@
         here = slice(quarter * 128, (quarter + 1) * 128)
         rows = jnp.concatenate([tail, edges[:, here], edges[:, channels : channels + 128], gains[:, here]], axis=0)
         pay[quarter, pl.ds(per * width, META), :] = rows.astype(BF16)
+    fetch.wait()
 
 
 def early(series, taps):
@@ -189,7 +194,8 @@
     return rows
 
 
-def group_kernel(got, taps, kept, meta, out, *, per, opening):
+def group_kernel(got, taps, kept, meta, out, *blanks, per, opening):
+    blank_kernel(*blanks)
     size = out.shape[0] - META
     members = [unpack(got[r]) for r in range(LO)]
     lines = lax.broadcasted_iota(jnp.int32, (META, 128), 0)
@@ -224,8 +230,9 @@
     out[size:, :] = later[size:, :]
 
 
-def entering_kernel(kept, meta, *refs, per):
-    *given, out = refs
+def entering_kernel(kept, meta, *refs, per, blanks):
+    blank_kernel(*refs[len(refs) - blanks :])
+    *given, out = refs[: len(refs) - blanks]
     size = kept.shape[1]
     own = meta[0].astype(F32)
     fresh = kept[0]
@@ -256,7 +263,7 @@
         ref[...] = jnp.zeros(ref.shape, ref.dtype)
 
 
-def intra_kernel(xc, bcc, rims, first, x_taps, bc_taps, cum_in, less_in, per_head, out, c_out):
+def intra_kernel(xc, bcc, rims, rims_high, first, x_taps, bc_taps, cum_in, less_in, per_head, out, c_out):
     heads = cum_in.shape[0]
     channels = xc.shape[0]
     width = channels // heads
@@ -265,7 +272,8 @@
     less_cols = jnp.concatenate([less[:, :128].T, less[:, 128:].T], axis=0)
     skips = per_head[2][:, :1]
     lines = lax.broadcasted_iota(jnp.int32, rims.shape, 0)
-    edges = jnp.where(lines < 3, rims[...].astype(F32), pltpu.roll(first[...].astype(F32), 3, 0))
+    given = rims[...].astype(F32) + rims_high[...].astype(F32)
+    edges = jnp.where(lines < 3, given, pltpu.roll(first[...].astype(F32), 3, 0))
     begun = [early(edges[:, :channels], x_taps[...]), early(edges[:, channels:], bc_taps[...])]
     placed = dot(jnp.concatenate(begun, axis=1), picks(0), 0, 0).astype(BF16)
 
@@ -294,15 +302,23 @@
         out[at, :] = jnp.concatenate([near, late], axis=1) + skips[h : h + 1] * values.astype(F32)
 
 
-def output_kernel(inner, c_rows, cum, state, z, out):
+def output_kernel(inner, c_rows, cum, state, z, out, held, done):
     heads = cum.shape[0]
     width = inner.shape[0] // heads
+    per = heads // LO
     grown = jnp.exp(cum[...])
+    copies = []
     for h in range(heads):
         at = pl.ds(h * width, width)
         y = inner[at, :] + grown[h : h + 1] * dot(state[at, :], c_rows[...], 1, 0)
         y = y.astype(BF16).astype(F32)
-        out[at, :] = (y * silu(z[at, :].astype(F32))).astype(BF16)
+        held[at, :] = (y * silu(z[at, :].astype(F32))).astype(BF16)
+        if h % per == per - 1:
+            part = pl.ds((h + 1 - per) * width, per * width)
+            copies.append(pltpu.make_async_copy(held.at[part], out.at[part], done.at[h // per]))
+            copies[-1].start()
+    for copy in copies:
+        copy.wait()
 
 
 def shape(*dims, dtype=F32):
@@ -352,61 +368,65 @@
         out_shape=outs,
         name="load",
     )(group, member, bc_in, taps, x_in, *small)
-    pay, xc, bcc, cum, less = run(
+    inputs = [pltpu.with_memory_space_constraint(a, pltpu.VMEM) for a in (x, bc, dt, x_taps, bc_taps, per_head, last, first)]
+    outs = [shape(LO, quarter + META, states, dtype=BF16), series, pairs]
+    outs += [shape(heads, length), shape(heads, length), series]
+    pay, xc, bcc, cum, less, z = pl.pallas_call(
         state_kernel,
-        [shape(LO, quarter + META, states, dtype=BF16), series, pairs, shape(heads, length), shape(heads, length)],
-        x,
-        bc,
-        dt,
-        x_taps,
-        bc_taps,
-        per_head,
-        last,
-        first,
-    )
-
-    def gather(opening=False):
+        out_shape=outs,
+        in_specs=[pl.BlockSpec(memory_space=pl.ANY)] + [VMEM] * len(inputs),
+        out_specs=[VMEM] * len(outs),
+        scratch_shapes=[pltpu.SemaphoreType.DMA],
+        name="states",
+    )(z_gate, *inputs)
+
+    def gather(*blanks, opening=False):
         got = lax.all_to_all(pay, "near", 0, 0, tiled=True)
         kernel = lambda *refs: group_kernel(*refs, per=per, opening=opening)
-        return tuple(run(kernel, kept_shapes + [block_shape], got, own_taps))
+        return tuple(run(kernel, kept_shapes + [block_shape, *blanks], got, own_taps))
 
     def blank(*outs):
         return tuple(run(blank_kernel, list(outs)))
 
-    def exchange(*given):
-        (entering,) = run(lambda *refs: entering_kernel(*refs, per=per), [state_shape], *given)
-        return lax.all_to_all(entering, "near", 0, 0, tiled=True)
+    def exchange(*given, blanks=()):
+        kernel = lambda *refs: entering_kernel(*refs, per=per, blanks=len(blanks))
+        entering, *rest = run(kernel, [state_shape, *blanks], *given)
+        return tuple(rest) + (lax.all_to_all(entering, "near", 0, 0, tiled=True),)
 
     def sent(block, source, target):
         route = [(source * LO + i, target * LO + i) for i in range(LO)]
         return lax.ppermute(block, cp, route)
 
     def kept_on(*arrays):
-        return tuple(run(copy_kernel, kept_shapes + [block_shape], *arrays))
-
-    kept = lax.cond(far == 0, lambda: gather(True), lambda: blank(*kept_shapes, block_shape))
+        return tuple(run(copy_kernel, [shape(*a.shape, dtype=a.dtype) for a in arrays], *arrays))
+
+    kept = lax.cond(far == 0, lambda: gather(opening=True), lambda: blank(*kept_shapes, block_shape))
     near = sent(kept[2], 0, 1)
+    rims_low = lax.ppermute(last, cp, [(i, i + 1) for i in range(2 * LO - 1)])
     *kept, begin = lax.switch(
         jnp.minimum(far, 2),
         [
-            lambda *kept: blank(*kept_shapes, block_shape) + (exchange(*kept[:2]),),
-            lambda *kept: gather() + blank(state_shape),
+            lambda *kept: exchange(*kept[:2], blanks=(*kept_shapes, block_shape)),
+            lambda *kept: gather(state_shape),
             lambda *kept: blank(*kept_shapes, block_shape, state_shape),
         ],
         *kept,
     )
     (joined,) = run(lambda *refs: join_kernel(*refs, per=per), [block_shape], near, kept[2], own_taps)
+    over = sent(joined, 1, 3)
     next_one = sent(joined, 1, 2)
-    over = sent(joined, 1, 3)
-    kept = lax.cond(far >= 2, lambda *kept: gather(), kept_on, *kept)
+    kept = lax.cond(far == 2, lambda *kept: gather(), kept_on, *kept)
     between = sent(kept[2], 2, 3)
-    rims = lax.ppermute(last, cp, [(i, i + 1) for i in range(count - 1)])
+    kept = lax.cond(far == 3, lambda *kept: gather()[:2], kept_on, *kept[:2])
+    *kept, last = lax.optimization_barrier((*kept, last))
+    rims_high = lax.ppermute(last, cp, [(i, i + 1) for i in range(2 * LO - 1, count - 1)])
     inner, c_rows = run(
         intra_kernel,
         [shape(channels, length), shape(states, length, dtype=BF16)],
         xc,
         bcc,
-        rims,
+        rims_low,
+        rims_high,
         first,
         x_taps,
         bc_taps,
@@ -414,20 +434,27 @@
         less,
         per_head,
     )
-    state = lax.cond(
+    (state,) = lax.cond(
         far == 0,
-        lambda begin, *unused: run(copy_kernel, [state_shape], begin)[0],
+        lambda begin, *unused: tuple(run(copy_kernel, [state_shape], begin)),
         lambda begin, *given: exchange(*given),
         begin,
-        *kept[:2],
+        *kept,
         own_taps,
         near,
         next_one,
         over,
         between,
-    ).reshape(channels, states)
-    out = jax.ShapeDtypeStruct((channels, length), BF16)
-    return run(output_kernel, [out], inner, c_rows, cum, state, z_gate)[0]
+    )
+    inputs = [inner, c_rows, cum, state.reshape(channels, states), z]
+    return pl.pallas_call(
+        output_kernel,
+        out_shape=jax.ShapeDtypeStruct((channels, length), BF16),
+        in_specs=[VMEM] * len(inputs),
+        out_specs=pl.BlockSpec(memory_space=pl.ANY),
+        scratch_shapes=[pltpu.VMEM((channels, length), BF16), pltpu.SemaphoreType.DMA((LO,))],
+        name="gated",
+    )(*[pltpu.with_memory_space_constraint(a, pltpu.VMEM) for a in inputs])
 
 
 def solution(mesh):

time: 51.7 us -> 47.7 us (0.923)
  the two profiles are of different devices: /device:TPU:300 before, /device:TPU:256 now
where the time goes in v2:
time: 47.7 us; the launch traced here: 47.4 us
  blocking collectives  22.3 us (47%)
  waiting for transfers between devices  10.4 us (22%)
  starting transfers between devices  8.7 us (18%)
  Pallas kernels  5.74 us (12%)
    all_to_all x1, blocking collectives, gather(): got = lax.all_to_all(pay, 'near', 0, 0, tiled=True)  14 us
    all_to_all x1, blocking collectives, exchange(): return tuple(rest) + (lax.all_to_all(entering, 'near', 0, 0, tiled=True),)  8.31 us
    ppermute x4, waiting for transfers between devices, sent(): return lax.ppermute(block, cp, route)  5.88 us
    ppermute x4, starting transfers between devices, sent(): return lax.ppermute(block, cp, route)  5.63 us
    ppermute x1, waiting for transfers between devices, local(): rims_low = lax.ppermute(last, cp, [(i, i + 1) for i in range(2 * LO - 1)])  4.5 us
    ppermute x1, starting transfers between devices, local(): rims_low = lax.ppermute(last, cp, [(i, i + 1) for i in range(2 * LO - 1)])  2.41 us
    pallas_call x1, Pallas kernels, local(): pl.pallas_call(state_kernel, out_shape=outs, in_specs=[pl.BlockSpec(memor...  1.81 us
    pallas_call x7, Pallas kernels, run(): pl.pallas_call(kernel, out_shape=outs, in_specs=[VMEM] * len(args), out_s...  1.6 us
  transfers between devices with their start and end apart: 6, of which 2 were waited for; matrix products, arithmetic and copies ran while one was open for 0% of the time, Pallas kernels for 3%

profile of v2, /device:TPU:256, one launch (start us, length us, event | category | flops | bytes accessed | tf_op | source)
XLA Modules:
  0.0 47.4 jit_solution(17160027538063070867)
XLA Ops:
  0.0 1.3 %load.1 = (bf16[8,768]{1,0:T(8,128)(2,1)S(1)}, bf16[8,768]{1,0:T(8,128)(2,1)S(1)}, bf16[512,256]{1,0:T(8,128)(2,1)S(1)}, bf16[256,256]{1,0:T(8,128)(2,1)S(1)}, b...) custom-call(s32[1]{0:T(128)} %bitcast.2.group, ...), custom_call_target="tpu_custom_call" | custom-call | tf_op jit(solution)/shard_map/load/pallas_call | solution.py:359
  1.3 1.8 %states.1 = (bf16[4,160,128]{2,1,0:T(8,128)(2,1)S(1)}, bf16[512,256]{1,0:T(8,128)(2,1)S(1)}, bf16[256,256]{1,0:T(8,128)(2,1)S(1)}, f32[8,256]{1,0:T(8,128)S(1)},...) custom-call(bf16[512,256]{1,0:T(8,128)(2,1)} %z.1, bf16[512,256]{1,0:T(8,128)(2,1)S(1)} %get-tuple-element.123.x, ...), custom_call_target="tpu_custom_call" | custom-call | tf_op jit(solution)/shard_map/states/pallas_call | solution.py:374
  3.2 0.1 conditional.5
  3.2 1.3 %collective-permute-start.2 = (bf16[160,128]{1,0:T(8,128)(2,1)S(1)}, bf16[160,128]{1,0:T(8,128)(2,1)S(1)}, u32[]{:S(2)}, u32[]{:S(2)}) collective-permute-start(bf16[160,128]{1,0:T(8,128)(2,1)S(1)} %get-tuple-element.151), channel_id=1, source_target_pairs={{0,64},{16,80},{32,96},{48,112},{1,65},{17,81},{33,97},{49,113},{2... | collective-permute-start | bytes 122888 | tf_op jit(solution)/shard_map/ppermute | solution.py:398
  4.5 14.3 %conditional.6 = ((f32[4,128,128]{2,1,0:T(8,128)S(1)}, bf16[4,32,128]{2,1,0:T(8,128)(2,1)S(1)}, bf16[160,128]{1,0:T(8,128)(2,1)S(1)}, bf16[4,128,128]{2,1,0:T(8,128)(2,1)S(1)})) conditional(s32[]{:T(128)} %clamp.3, (f32[4,128,128]{2,1,0:T(8,128)S(1)}, bf16[4,32,128]{2,1,0:T(8,128)(2,1)S(1)}) %tuple.51, ...), branch_computations={%region_2.3_spmd, %region_3.4_spmd, %region_4.5_spmd} | conditional | bytes 327688 | solution.py:406
  4.5 14.0 %all_to_all.26.refs_0_ = bf16[4,160,128]{2,1,0:T(8,128)(2,1)S(1)} all-to-all(bf16[4,160,128]{2,1,0:T(8,128)(2,1)S(1)} %get-tuple-element.71), channel_id=1, replica_groups=mesh['dp'=4,'far'=4,'near'=4,'tensor'=16] {'near'}, dimensions={0} | all-to-all | bytes 327680 | tf_op jit(solution)/shard_map/cond/branch_1_fun/all_to_all | solution.py:384
  18.6 0.2 branch_1_fun.6
  18.9 0.7 %collective-permute-start.5 = (bf16[160,128]{1,0:T(8,128)(2,1)S(1)}, bf16[160,128]{1,0:T(8,128)(2,1)S(1)}, u32[]{:S(2)}, u32[]{:S(2)}) collective-permute-start(bf16[160,128]{1,0:T(8,128)(2,1)S(1)} %get-tuple-element.152), channel_id=1, source_target_pairs={{128,192},{144,208},{160,224},{176,240},{129,193},{145,209},{161,2... | collective-permute-start | bytes 122888 | tf_op jit(solution)/shard_map/ppermute | solution.py:398
  19.5 5.9 %collective-permute-done.2.refs_0_ = bf16[160,128]{1,0:T(8,128)(2,1)S(1)} collective-permute-done((bf16[160,128]{1,0:T(8,128)(2,1)S(1)}, bf16[160,128]{1,0:T(8,128)(2,1)S(1)}, u32[]{:S(2)}, u32[]{:S(2)}) %collective-permute-start.2) | collective-permute-done | bytes 40992 | tf_op jit(solution)/shard_map/ppermute | solution.py:398
  25.4 0.2 shard_map.110
  25.6 2.4 %collective-permute-start.3 = (bf16[160,128]{1,0:T(8,128)(2,1)S(1)}, bf16[160,128]{1,0:T(8,128)(2,1)S(1)}, u32[]{:S(2)}, u32[]{:S(2)}) collective-permute-start(bf16[160,128]{1,0:T(8,128)(2,1)S(1)} %shard_map.110), channel_id=1, source_target_pairs={{64,128},{80,144},{96,160},{112,176},{65,129},{81,145},{97,161},{1... | collective-permute-start | bytes 122888 | tf_op jit(solution)/shard_map/ppermute | solution.py:398
  28.0 1.3 %collective-permute-start.4 = (bf16[160,128]{1,0:T(8,128)(2,1)S(1)}, bf16[160,128]{1,0:T(8,128)(2,1)S(1)}, u32[]{:S(2)}, u32[]{:S(2)}) collective-permute-start(bf16[160,128]{1,0:T(8,128)(2,1)S(1)} %shard_map.110), channel_id=1, source_target_pairs={{64,192},{80,208},{96,224},{112,240},{65,193},{81,209},{97,225},{1... | collective-permute-start | bytes 122888 | tf_op jit(solution)/shard_map/ppermute | solution.py:398
  29.4 0.7 %collective-permute-start.1 = (bf16[8,768]{1,0:T(8,128)(2,1)S(1)}, bf16[8,768]{1,0:T(8,128)(2,1)S(1)}, u32[]{:S(2)}, u32[]{:S(2)}) collective-permute-start(bf16[8,768]{1,0:T(8,128)(2,1)S(1)} %get-tuple-element.144.last), channel_id=1, source_target_pairs={{112,128},{128,144},{144,160},{160,176},{176,192},{192,208},{208,2... | collective-permute-start | bytes 36872 | tf_op jit(solution)/shard_map/ppermute | solution.py:422
  30.0 2.4 %collective-permute-start = (bf16[8,768]{1,0:T(8,128)(2,1)S(1)}, bf16[8,768]{1,0:T(8,128)(2,1)S(1)}, u32[]{:S(2)}, u32[]{:S(2)}) collective-permute-start(bf16[8,768]{1,0:T(8,128)(2,1)S(1)} %get-tuple-element.144.last), channel_id=1, source_target_pairs={{0,16},{16,32},{32,48},{48,64},{64,80},{80,96},{96,112},{1,17},{17... | collective-permute-start | bytes 36872 | tf_op jit(solution)/shard_map/ppermute | solution.py:405
  32.5 0.0 collective-permute-done.1.rims_high
  32.5 4.5 %collective-permute-done.rims = bf16[8,768]{1,0:T(8,128)(2,1)S(1)} collective-permute-done((bf16[8,768]{1,0:T(8,128)(2,1)S(1)}, bf16[8,768]{1,0:T(8,128)(2,1)S(1)}, u32[]{:S(2)}, u32[]{:S(2)}) %collective-permute-start) | collective-permute-done | bytes 12320 | tf_op jit(solution)/shard_map/ppermute | solution.py:405
  37.0 0.8 %shard_map.109 = (f32[512,256]{1,0:T(8,128)S(1)}, bf16[128,256]{1,0:T(8,128)(2,1)S(1)}) custom-call(bf16[512,256]{1,0:T(8,128)(2,1)S(1)} %get-tuple-element.131.xc, bf16[256,256]{1,0:T(8,128)(2,1)S(1)} %get-tuple-element.132.bcc, bf16[8,768]{1,0:T(8,128)(2,1)S(1)} %collective-permute-done.rims, bf16[8,768]{1,0:T(8,128)(2,1)S(1)} %collective-permute-done.1.rims_high, ...), custom_call_target="tpu_custom_call" | custom-call | tf_op jit(solution)/shard_map/pallas_call | solution.py:333
  37.8 0.0 collective-permute-done.5
  37.8 0.0 collective-permute-done.3
  37.8 0.0 collective-permute-done.4
  37.8 8.6 %conditional.9 = (bf16[512,128]{1,0:T(8,128)(2,1)S(1)}) conditional(s32[]{:T(128)} %convert_element_type.12, (f32[4,128,128]{2,1,0:T(8,128)S(1)}, bf16[4,32,128]{2,1,0:T(8,128)(2,1)S(1)}, f32[2,8,128]{2,1,0:T(8,128)S(1)}, bf16[160,128]{1,0:T(8,128)(2,1)S(1)}, bf16[160,128]{1,0:T(8,128)(2,1)S(1)}, /*index=5*/bf16[160,128]{1,0:T(8,128)(2,1)S(1)}, ...), branch_computations={%region_9.10_spmd, %region_10.11_spmd} | conditional | bytes 262152 | solution.py:437
  37.9 0.2 branch_0_fun.9
  38.1 8.3 %all_to_all.29 = bf16[4,128,128]{2,1,0:T(8,128)(2,1)S(1)} all-to-all(bf16[4,128,128]{2,1,0:T(8,128)(2,1)S(1)} %branch_0_fun.9), channel_id=1, replica_groups=mesh['dp'=4,'far'=4,'near'=4,'tensor'=16] {'near'}, dimensions={0} | all-to-all | bytes 262144 | tf_op jit(solution)/shard_map/cond/branch_0_fun/all_to_all | solution.py:394
  46.4 1.0 %gated.1 = bf16[512,256]{1,0:T(8,128)(2,1)} custom-call(f32[512,256]{1,0:T(8,128)S(1)} %get-tuple-element.147.inner, bf16[128,256]{1,0:T(8,128)(2,1)S(1)} %get-tuple-element.148.c_rows, f32[8,256]{1,0:T(8,128)S(1)} %get-tuple-element.145.cum_in.cum, bf16[512,128]{1,0:T(8,128)(2,1)S(1)} %get-tuple-element.187.state, bf16[512,256]{1,0:T(8,128)(2,1)S(1)} %get-tuple-element.154.z), custom_call_target="tpu_custom_call" | custom-call | tf_op jit(solution)/shard_map/gated/pallas_call | solution.py:450
  (5 shorter events, 0.2 us)
Async XLA Ops:
  3.2 22.2 %collective-permute-start.2 = (bf16[160,128]{1,0:T(8,128)(2,1)S(1)}, bf16[160,128]{1,0:T(8,128)(2,1)S(1)}, u32[]{:S(2)}, u32[]{:S(2)}) collective-permute-start(bf16[160,128]{1,0:T(8,128)(2,1)S(1)} %get-tuple-element.151), channel_id=1, source_target_pairs={{0,64},{16,80},{32,96},{48,112},{1,65},{17,81},{33,97},{49,113},{2... | collective-permute-start | bytes 122888 | tf_op jit(solution)/shard_map/ppermute | solution.py:398
  18.9 18.9 %collective-permute-start.5 = (bf16[160,128]{1,0:T(8,128)(2,1)S(1)}, bf16[160,128]{1,0:T(8,128)(2,1)S(1)}, u32[]{:S(2)}, u32[]{:S(2)}) collective-permute-start(bf16[160,128]{1,0:T(8,128)(2,1)S(1)} %get-tuple-element.152), channel_id=1, source_target_pairs={{128,192},{144,208},{160,224},{176,240},{129,193},{145,209},{161,2... | collective-permute-start | bytes 122888 | tf_op jit(solution)/shard_map/ppermute | solution.py:398
  25.6 12.2 %collective-permute-start.3 = (bf16[160,128]{1,0:T(8,128)(2,1)S(1)}, bf16[160,128]{1,0:T(8,128)(2,1)S(1)}, u32[]{:S(2)}, u32[]{:S(2)}) collective-permute-start(bf16[160,128]{1,0:T(8,128)(2,1)S(1)} %shard_map.110), channel_id=1, source_target_pairs={{64,128},{80,144},{96,160},{112,176},{65,129},{81,145},{97,161},{1... | collective-permute-start | bytes 122888 | tf_op jit(solution)/shard_map/ppermute | solution.py:398
  28.0 9.8 %collective-permute-start.4 = (bf16[160,128]{1,0:T(8,128)(2,1)S(1)}, bf16[160,128]{1,0:T(8,128)(2,1)S(1)}, u32[]{:S(2)}, u32[]{:S(2)}) collective-permute-start(bf16[160,128]{1,0:T(8,128)(2,1)S(1)} %shard_map.110), channel_id=1, source_target_pairs={{64,192},{80,208},{96,224},{112,240},{65,193},{81,209},{97,225},{1... | collective-permute-start | bytes 122888 | tf_op jit(solution)/shard_map/ppermute | solution.py:398
  29.4 3.1 %collective-permute-start.1 = (bf16[8,768]{1,0:T(8,128)(2,1)S(1)}, bf16[8,768]{1,0:T(8,128)(2,1)S(1)}, u32[]{:S(2)}, u32[]{:S(2)}) collective-permute-start(bf16[8,768]{1,0:T(8,128)(2,1)S(1)} %get-tuple-element.144.last), channel_id=1, source_target_pairs={{112,128},{128,144},{144,160},{160,176},{176,192},{192,208},{208,2... | collective-permute-start | bytes 36872 | tf_op jit(solution)/shard_map/ppermute | solution.py:422
  30.0 6.9 %collective-permute-start = (bf16[8,768]{1,0:T(8,128)(2,1)S(1)}, bf16[8,768]{1,0:T(8,128)(2,1)S(1)}, u32[]{:S(2)}, u32[]{:S(2)}) collective-permute-start(bf16[8,768]{1,0:T(8,128)(2,1)S(1)} %get-tuple-element.144.last), channel_id=1, source_target_pairs={{0,16},{16,32},{32,48},{48,64},{64,80},{80,96},{96,112},{1,17},{17... | collective-permute-start | bytes 36872 | tf_op jit(solution)/shard_map/ppermute | solution.py:405

commit v3 on v2

--- a/solution.py
+++ b/solution.py
@@ -194,9 +194,9 @@
     return rows
 
 
-def group_kernel(got, taps, kept, meta, out, *blanks, per, opening):
-    blank_kernel(*blanks)
-    size = out.shape[0] - META
+def group_kernel(got, taps, kept, meta, *refs, per, opening):
+    blank_kernel(*refs[1:])
+    size = kept.shape[1]
     members = [unpack(got[r]) for r in range(LO)]
     lines = lax.broadcasted_iota(jnp.int32, (META, 128), 0)
     state, rows = members[0]
@@ -213,6 +213,9 @@
         state = fresh + d * state
         decay, suffix = decay * d, suffix * d
     meta[...] = got[:, size:, :]
+    if not refs:
+        return
+    out = refs[0]
     out[:size, :] = state.astype(BF16)
     head = packed_rows(suffix, 4, packed_rows(decay, 0, jnp.zeros((8, 128), F32), per), per)
     edge = lax.broadcasted_iota(jnp.int32, (16, 128), 0) % 8 < 3
@@ -263,7 +266,8 @@
         ref[...] = jnp.zeros(ref.shape, ref.dtype)
 
 
-def intra_kernel(xc, bcc, rims, rims_high, first, x_taps, bc_taps, cum_in, less_in, per_head, out, c_out):
+def intra_kernel(*refs, count):
+    rims, (xc, bcc, first, x_taps, bc_taps, cum_in, less_in, per_head, out, c_out) = refs[:count], refs[count:]
     heads = cum_in.shape[0]
     channels = xc.shape[0]
     width = channels // heads
@@ -271,8 +275,8 @@
     cum, less = cum_in[...], less_in[...]
     less_cols = jnp.concatenate([less[:, :128].T, less[:, 128:].T], axis=0)
     skips = per_head[2][:, :1]
-    lines = lax.broadcasted_iota(jnp.int32, rims.shape, 0)
-    given = rims[...].astype(F32) + rims_high[...].astype(F32)
+    lines = lax.broadcasted_iota(jnp.int32, first.shape, 0)
+    given = sum(r[...].astype(F32) for r in rims)
     edges = jnp.where(lines < 3, given, pltpu.roll(first[...].astype(F32), 3, 0))
     begun = [early(edges[:, :channels], x_taps[...]), early(edges[:, channels:], bc_taps[...])]
     placed = dot(jnp.concatenate(begun, axis=1), picks(0), 0, 0).astype(BF16)
@@ -380,10 +384,10 @@
         name="states",
     )(z_gate, *inputs)
 
-    def gather(*blanks, opening=False):
+    def gather(*rest, opening=False):
         got = lax.all_to_all(pay, "near", 0, 0, tiled=True)
         kernel = lambda *refs: group_kernel(*refs, per=per, opening=opening)
-        return tuple(run(kernel, kept_shapes + [block_shape, *blanks], got, own_taps))
+        return tuple(run(kernel, [*kept_shapes, *rest], got, own_taps))
 
     def blank(*outs):
         return tuple(run(blank_kernel, list(outs)))
@@ -400,52 +404,63 @@
     def kept_on(*arrays):
         return tuple(run(copy_kernel, [shape(*a.shape, dtype=a.dtype) for a in arrays], *arrays))
 
-    kept = lax.cond(far == 0, lambda: gather(opening=True), lambda: blank(*kept_shapes, block_shape))
-    near = sent(kept[2], 0, 1)
-    rims_low = lax.ppermute(last, cp, [(i, i + 1) for i in range(2 * LO - 1)])
-    *kept, begin = lax.switch(
-        jnp.minimum(far, 2),
-        [
+    def inside(*rims):
+        outs = [shape(channels, length), shape(states, length, dtype=BF16)]
+        args = (first, x_taps, bc_taps, cum, less, per_head)
+        kernel = lambda *refs: intra_kernel(*refs, count=len(rims))
+        return tuple(run(kernel, outs, *rims, xc, bcc, *args))
+
+    def shifted(begin, end):
+        return lax.ppermute(kept_on(last)[0], cp, [(i, i + 1) for i in range(begin, end)])
+
+    inner_shapes = [shape(channels, length), shape(states, length, dtype=BF16)]
+
+    def low_part():
+        kept = lax.cond(
+            far == 0, lambda: gather(block_shape, opening=True), lambda: blank(*kept_shapes, block_shape)
+        )
+        near = sent(kept[2], 0, 1)
+        rims = shifted(0, 2 * LO - 1)
+        *kept, begin = lax.cond(
+            far == 0,
             lambda *kept: exchange(*kept[:2], blanks=(*kept_shapes, block_shape)),
-            lambda *kept: gather(state_shape),
-            lambda *kept: blank(*kept_shapes, block_shape, state_shape),
-        ],
-        *kept,
+            lambda *kept: gather(block_shape, state_shape),
+            *kept,
+        )
+        inner = inside(rims)
+        (joined,) = run(lambda *refs: join_kernel(*refs, per=per), [block_shape], near, kept[2], own_taps)
+        kept, meta, near, begin = kept_on(*kept[:2], near, begin)
+        return (kept, meta, joined, near, begin, *inner)
+
+    def high_part(*kept):
+        rims = shifted(2 * LO, count - 1)
+        kept = lax.cond(far == 2, lambda *kept: gather(block_shape), lambda *kept: blank(*kept_shapes, block_shape), *kept)
+        between = sent(kept[2], 2, 3)
+        kept = lax.cond(far == 3, lambda *kept: gather(), kept_on, *kept[:2])
+        return kept_on(*kept, between, rims)
+
+    def later_part(kept, meta, joined, near, begin, *inner):
+        (joined,) = kept_on(joined)
+        over = sent(joined, 1, 3)
+        next_one = sent(joined, 1, 2)
+        rims_mid = shifted(2 * LO - 1, 2 * LO)
+        *kept, between, rims = lax.cond(
+            far >= 2, high_part, lambda *kept: kept_on(*kept) + blank(block_shape, strip), kept, meta
+        )
+        inner = lax.cond(
+            far >= 2, lambda rims, rims_mid, *inner: inside(rims, rims_mid),
+            lambda rims, rims_mid, *inner: kept_on(*inner), rims, rims_mid, *inner
+        )
+        between, *inner = lax.optimization_barrier((between, *inner))
+        (state,) = exchange(*kept_on(*kept), own_taps, near, next_one, over, between)
+        return (state, *inner)
+
+    parts = lax.cond(
+        far < 2, low_part, lambda: blank(*kept_shapes, block_shape, block_shape, state_shape, *inner_shapes)
     )
-    (joined,) = run(lambda *refs: join_kernel(*refs, per=per), [block_shape], near, kept[2], own_taps)
-    over = sent(joined, 1, 3)
-    next_one = sent(joined, 1, 2)
-    kept = lax.cond(far == 2, lambda *kept: gather(), kept_on, *kept)
-    between = sent(kept[2], 2, 3)
-    kept = lax.cond(far == 3, lambda *kept: gather()[:2], kept_on, *kept[:2])
-    *kept, last = lax.optimization_barrier((*kept, last))
-    rims_high = lax.ppermute(last, cp, [(i, i + 1) for i in range(2 * LO - 1, count - 1)])
-    inner, c_rows = run(
-        intra_kernel,
-        [shape(channels, length), shape(states, length, dtype=BF16)],
-        xc,
-        bcc,
-        rims_low,
-        rims_high,
-        first,
-        x_taps,
-        bc_taps,
-        cum,
-        less,
-        per_head,
-    )
-    (state,) = lax.cond(
-        far == 0,
-        lambda begin, *unused: tuple(run(copy_kernel, [state_shape], begin)),
-        lambda begin, *given: exchange(*given),
-        begin,
-        *kept,
-        own_taps,
-        near,
-        next_one,
-        over,
-        between,
-    )
+    parts = list(parts)
+    parts[2], parts[4] = kept_on(parts[2], parts[4])
+    state, inner, c_rows = lax.cond(far == 0, lambda *parts: kept_on(*parts[4:]), later_part, *parts)
     inputs = [inner, c_rows, cum, state.reshape(channels, states), z]
     return pl.pallas_call(
         output_kernel,

time: 47.7 us -> 45 us (0.943)
  waiting for transfers between devices: 10.4 us -> 4.01 us
  local copies, waits for them, and re-layouts: 0 us -> 4.97 us
  blocking collectives: 22.3 us -> 20.7 us
    ppermute x4 -> x3, waiting for transfers between devices: 5.88 us -> 0.31 us  [sent(): return lax.ppermute(block, cp, route)]
    unnamed x0 -> x8, local copies, waits for them, and re-layouts: none -> 2.95 us
    cond x0 -> x6, local copies, waits for them, and re-layouts: none -> 2.01 us
    all_to_all x1, blocking collectives: 14 us -> 12 us  [gather(): got = lax.all_to_all(pay, 'near', 0, 0, tiled=True)]
    ppermute x2, starting transfers between devices: 3.07 us -> 4.94 us  [shifted(): lax.ppermute(kept_on(last)[0], cp, [(i, i + 1) for i in range(begin, end)])]
    ppermute x4 -> x3, starting transfers between devices: 5.63 us -> 3.86 us  [sent(): return lax.ppermute(block, cp, route)]
    ppermute x2, waiting for transfers between devices: 4.51 us -> 3.69 us  [shifted(): lax.ppermute(kept_on(last)[0], cp, [(i, i + 1) for i in range(begin, end)])]
    pallas_call x7 -> x14, Pallas kernels: 1.6 us -> 1.68 us  [run(): pl.pallas_call(kernel, out_shape=outs, in_specs=[VMEM] * len(args), out_s...]
  transfers between devices with their start and end apart: 6 -> 5, of which waited for: 2 -> 2; matrix products, arithmetic and copies ran while one was open for 0% -> 0% of each run, Pallas kernels for 3% -> 3%
where the time goes in v3:
time: 45 us; the launch traced here: 44.5 us
  blocking collectives  20.7 us (46%)
  starting transfers between devices  8.81 us (20%)
  Pallas kernels  5.81 us (13%)
  local copies, waits for them, and re-layouts  4.97 us (11%)
  waiting for transfers between devices  4.01 us (9%)
    all_to_all x1, blocking collectives, gather(): got = lax.all_to_all(pay, 'near', 0, 0, tiled=True)  12 us
    all_to_all x1, blocking collectives, exchange(): return tuple(rest) + (lax.all_to_all(entering, 'near', 0, 0, tiled=True),)  8.63 us
    ppermute x2, starting transfers between devices, shifted(): lax.ppermute(kept_on(last)[0], cp, [(i, i + 1) for i in range(begin, end)])  4.94 us
    ppermute x3, starting transfers between devices, sent(): return lax.ppermute(block, cp, route)  3.86 us
    ppermute x2, waiting for transfers between devices, shifted(): lax.ppermute(kept_on(last)[0], cp, [(i, i + 1) for i in range(begin, end)])  3.69 us
    unnamed x8, local copies, waits for them, and re-layouts  2.95 us
    cond x6, local copies, waits for them, and re-layouts  2.01 us
    pallas_call x1, Pallas kernels, local(): pl.pallas_call(state_kernel, out_shape=outs, in_specs=[pl.BlockSpec(memor...  1.81 us
  transfers between devices with their start and end apart: 5, of which 2 were waited for; matrix products, arithmetic and copies ran while one was open for 0% of the time, Pallas kernels for 3%

profile of v3, /device:TPU:256, one launch (start us, length us, event | category | flops | bytes accessed | tf_op | source)
XLA Modules:
  0.0 44.5 jit_solution(4300862587216511573)
XLA Ops:
  0.0 1.3 %load.1 = (bf16[8,768]{1,0:T(8,128)(2,1)S(1)}, bf16[8,768]{1,0:T(8,128)(2,1)S(1)}, bf16[512,256]{1,0:T(8,128)(2,1)S(1)}, bf16[256,256]{1,0:T(8,128)(2,1)S(1)}, b...) custom-call(s32[1]{0:T(128)} %bitcast.2.group, ...), custom_call_target="tpu_custom_call" | custom-call | tf_op jit(solution)/shard_map/load/pallas_call | solution.py:363
  1.3 1.8 %states.1 = (bf16[4,160,128]{2,1,0:T(8,128)(2,1)S(1)}, bf16[512,256]{1,0:T(8,128)(2,1)S(1)}, bf16[256,256]{1,0:T(8,128)(2,1)S(1)}, f32[8,256]{1,0:T(8,128)S(1)},...) custom-call(bf16[512,256]{1,0:T(8,128)(2,1)} %z.1, bf16[512,256]{1,0:T(8,128)(2,1)S(1)} %get-tuple-element.265.x, ...), custom_call_target="tpu_custom_call" | custom-call | tf_op jit(solution)/shard_map/states/pallas_call | solution.py:378
  3.2 24.0 %conditional.8 = ((f32[4,128,128]{2,1,0:T(8,128)S(1)}, bf16[4,32,128]{2,1,0:T(8,128)(2,1)}, bf16[160,128]{1,0:T(8,128)(2,1)S(1)}, bf16[160,128]{1,0:T(8,128)(2,1...) conditional(s32[]{:T(128)} %convert_element_type.21, () %tuple.61, ...), branch_computations={%region_0.1_spmd, %region_1.6_spmd} | conditional | flops 2 | bytes 1523974 | solution.py:458
  3.2 1.3 %collective-permute-start = (bf16[160,128]{1,0:T(8,128)(2,1)S(1)}, bf16[160,128]{1,0:T(8,128)(2,1)S(1)}, u32[]{:S(2)}, u32[]{:S(2)}) collective-permute-start(bf16[160,128]{1,0:T(8,128)(2,1)S(1)} %get-tuple-element.152), channel_id=1, source_target_pairs={{0,64},{16,80},{32,96},{48,112},{1,65},{17,81},{33,97},{49,113},{2... | collective-permute-start | bytes 122888 | tf_op jit(solution)/shard_map/cond/branch_1_fun/ppermute | solution.py:402
  4.6 4.3 %collective-permute-start.1 = (bf16[8,768]{1,0:T(8,128)(2,1)S(1)}, bf16[8,768]{1,0:T(8,128)(2,1)S(1)}, u32[]{:S(2)}, u32[]{:S(2)}) collective-permute-start(bf16[8,768]{1,0:T(8,128)(2,1)S(1)} %branch_1_fun.16), channel_id=1, source_target_pairs={{0,16},{16,32},{32,48},{48,64},{64,80},{80,96},{96,112},{1,17},{17... | collective-permute-start | bytes 36872 | tf_op jit(solution)/shard_map/cond/branch_1_fun/ppermute | solution.py:414
  8.8 12.3 %conditional.1 = ((f32[4,128,128]{2,1,0:T(8,128)S(1)}, bf16[4,32,128]{2,1,0:T(8,128)(2,1)S(1)}, bf16[160,128]{1,0:T(8,128)(2,1)S(1)}, bf16[4,128,128]{2,1,0:T(8,128)(2,1)S(1)})) conditional(s32[]{:T(128)} %convert_element_type.5, (bf16[4,160,128]{2,1,0:T(8,128)(2,1)S(1)}, f32[2,8,128]{2,1,0:T(8,128)S(1)}) %tuple.40, (f32[4,128,128]{2,1,0:T(8,128)S(1)}, ...), branch_computations={%region_4.4_spmd, %region_5.5_spmd} | conditional | bytes 327688 | solution.py:424
  8.9 12.0 %all_to_all.25.refs_0_ = bf16[4,160,128]{2,1,0:T(8,128)(2,1)S(1)} all-to-all(bf16[4,160,128]{2,1,0:T(8,128)(2,1)S(1)} %get-tuple-element.137), channel_id=1, replica_groups=mesh['dp'=4,'far'=4,'near'=4,'tensor'=16] {'near'}, dimensions={0} | all-to-all | bytes 327680 | tf_op jit(solution)/shard_map/cond/branch_1_fun/cond/branch_0_fun/all_to_all | solution.py:388
  20.9 0.2 branch_0_fun.14
  21.1 3.7 %collective-permute-done.1.refs_0_ = bf16[8,768]{1,0:T(8,128)(2,1)S(1)} collective-permute-done((bf16[8,768]{1,0:T(8,128)(2,1)S(1)}, bf16[8,768]{1,0:T(8,128)(2,1)S(1)}, u32[]{:S(2)}, u32[]{:S(2)}) %collective-permute-start.1) | collective-permute-done | bytes 12320 | tf_op jit(solution)/shard_map/cond/branch_1_fun/ppermute | solution.py:414
  24.8 0.8 %branch_1_fun.17 = (f32[512,256]{1,0:T(8,128)S(1)}, bf16[128,256]{1,0:T(8,128)(2,1)S(1)}) custom-call(bf16[8,768]{1,0:T(8,128)(2,1)S(1)} %collective-permute-done.1.refs_0_, bf16[512,256]{1,0:T(8,128)(2,1)S(1)} %get-tuple-element.160.refs_1_, bf16[256,256]{1,0:T(8,128)(2,1)S(1)} %get-tuple-element.161.refs_2_, ...), custom_call_target="tpu_custom_call" | custom-call | tf_op jit(solution)/shard_map/cond/branch_1_fun/pallas_call | solution.py:337
  25.6 0.0 collective-permute-done.refs_2_.refs_0_
  25.6 0.2 branch_1_fun.15
  25.9 0.0 copy-start.1
  25.9 0.6 %copy-done.1 = bf16[4,128,128]{2,1,0:T(8,128)(2,1)} copy-done((bf16[4,128,128]{2,1,0:T(8,128)(2,1)}, bf16[4,128,128]{2,1,0:T(8,128)(2,1)S(1)}, u32[]{:S(2)}) %copy-start.1) | copy-done | bytes 131096 | tf_op jit(solution)/shard_map/cond
  26.6 0.6 %copy-done.8 = bf16[4,32,128]{2,1,0:T(8,128)(2,1)} copy-done((bf16[4,32,128]{2,1,0:T(8,128)(2,1)}, bf16[4,32,128]{2,1,0:T(8,128)(2,1)S(1)}, u32[]{:S(2)}) %copy-start.8) | copy-done | bytes 32792 | tf_op jit(solution)/shard_map/cond
  27.2 0.6 %copy-done.5 = bf16[160,128]{1,0:T(8,128)(2,1)} copy-done((bf16[160,128]{1,0:T(8,128)(2,1)}, bf16[160,128]{1,0:T(8,128)(2,1)S(1)}, u32[]{:S(2)}) %copy-start.5) | copy-done | bytes 40984
  27.8 0.9 %copy-done.2 = bf16[4,128,128]{2,1,0:T(8,128)(2,1)S(1)} copy-done((bf16[4,128,128]{2,1,0:T(8,128)(2,1)S(1)}, bf16[4,128,128]{2,1,0:T(8,128)(2,1)}, u32[]{:S(2)}) %copy-start.2) | copy-done | bytes 131096
  28.7 0.8 %copy-done.6 = bf16[160,128]{1,0:T(8,128)(2,1)S(1)} copy-done((bf16[160,128]{1,0:T(8,128)(2,1)S(1)}, bf16[160,128]{1,0:T(8,128)(2,1)}, u32[]{:S(2)}) %copy-start.6) | copy-done | bytes 40984
  29.5 0.0 copy-start.3
  29.5 0.6 %copy-done.3 = bf16[4,128,128]{2,1,0:T(8,128)(2,1)} copy-done((bf16[4,128,128]{2,1,0:T(8,128)(2,1)}, bf16[4,128,128]{2,1,0:T(8,128)(2,1)S(1)}, u32[]{:S(2)}) %copy-start.3) | copy-done | bytes 131096
  30.2 13.4 %conditional.9 = (f32[512,256]{1,0:T(8,128)S(1)}, bf16[128,256]{1,0:T(8,128)(2,1)S(1)}, bf16[512,128]{1,0:T(8,128)(2,1)S(1)}) conditional(s32[]{:T(128)} %convert_element_type.20, (s32[]{:T(128)}, f32[4,128,128]{2,1,0:T(8,128)S(1)}, bf16[4,32,128]{2,1,0:T(8,128)(2,1)}, bf16[4,160,128]{2,1,0:T(8,128)(2,1)S(1)}, f32[2,8,128]{2,1,0:T(8,128)S(1)}, ...), branch_computations={%region_6.15_spmd, %region_15.16_spmd} | conditional | flops 6 | bytes 1507802 | solution.py:463
  30.2 1.3 %collective-permute-start.6 = (bf16[160,128]{1,0:T(8,128)(2,1)S(1)}, bf16[160,128]{1,0:T(8,128)(2,1)S(1)}, u32[]{:S(2)}, u32[]{:S(2)}) collective-permute-start(bf16[160,128]{1,0:T(8,128)(2,1)S(1)} %branch_0_fun.22), channel_id=1, source_target_pairs={{64,192},{80,208},{96,224},{112,240},{65,193},{81,209},{97,225},{1... | collective-permute-start | bytes 122888 | tf_op jit(solution)/shard_map/cond/branch_0_fun/ppermute | solution.py:402
  31.5 1.3 %collective-permute-start.5 = (bf16[160,128]{1,0:T(8,128)(2,1)S(1)}, bf16[160,128]{1,0:T(8,128)(2,1)S(1)}, u32[]{:S(2)}, u32[]{:S(2)}) collective-permute-start(bf16[160,128]{1,0:T(8,128)(2,1)S(1)} %branch_0_fun.22), channel_id=1, source_target_pairs={{64,128},{80,144},{96,160},{112,176},{65,129},{81,145},{97,161},{1... | collective-permute-start | bytes 122888 | tf_op jit(solution)/shard_map/cond/branch_0_fun/ppermute | solution.py:402
  32.8 0.7 %collective-permute-start.4 = (bf16[8,768]{1,0:T(8,128)(2,1)S(1)}, bf16[8,768]{1,0:T(8,128)(2,1)S(1)}, u32[]{:S(2)}, u32[]{:S(2)}) collective-permute-start(bf16[8,768]{1,0:T(8,128)(2,1)S(1)} %branch_0_fun.20), channel_id=1, source_target_pairs={{112,128},{113,129},{114,130},{115,131},{116,132},{117,133},{118,1... | collective-permute-start | bytes 36872 | tf_op jit(solution)/shard_map/cond/branch_0_fun/ppermute | solution.py:414
  33.4 0.8 %conditional.4 = ((f32[4,128,128]{2,1,0:T(8,128)S(1)}, bf16[4,32,128]{2,1,0:T(8,128)(2,1)S(1)}, bf16[160,128]{1,0:T(8,128)(2,1)S(1)}, bf16[8,768]{1,0:T(8,128)(2,1)S(1)})) conditional(s32[]{:T(128)} %convert_element_type.17, (f32[4,128,128]{2,1,0:T(8,128)S(1)}, bf16[4,32,128]{2,1,0:T(8,128)(2,1)}) %tuple.50, (s32[]{:T(128)}, ...), branch_computations={%region_7.7_spmd, %region_8.12_spmd} | conditional | flops 4 | bytes 868516 | solution.py:447
  33.5 0.7 %copy-done.9 = bf16[4,32,128]{2,1,0:T(8,128)(2,1)S(1)} copy-done((bf16[4,32,128]{2,1,0:T(8,128)(2,1)S(1)}, bf16[4,32,128]{2,1,0:T(8,128)(2,1)}, u32[]{:S(2)}) %copy-start.9) | copy-done | bytes 32792 | tf_op jit(solution)/shard_map/cond/branch_0_fun/cond
  34.3 0.0 collective-permute-done.4
  34.3 0.1 conditional.5
  34.4 0.3 collective-permute-done.5.refs_4_
  34.7 0.2 branch_0_fun.23
  34.9 8.6 %all_to_all.29 = bf16[4,128,128]{2,1,0:T(8,128)(2,1)S(1)} all-to-all(bf16[4,128,128]{2,1,0:T(8,128)(2,1)S(1)} %branch_0_fun.23), channel_id=1, replica_groups=mesh['dp'=4,'far'=4,'near'=4,'tensor'=16] {'near'}, dimensions={0} | all-to-all | bytes 262144 | tf_op jit(solution)/shard_map/cond/branch_0_fun/all_to_all | solution.py:398
  43.6 1.0 %gated.1 = bf16[512,256]{1,0:T(8,128)(2,1)} custom-call(f32[512,256]{1,0:T(8,128)S(1)} %get-tuple-element.288.inner, bf16[128,256]{1,0:T(8,128)(2,1)S(1)} %get-tuple-element.289.c_rows, f32[8,256]{1,0:T(8,128)S(1)} %get-tuple-element.277.cum, bf16[512,128]{1,0:T(8,128)(2,1)S(1)} %get-tuple-element.290.state, bf16[512,256]{1,0:T(8,128)(2,1)S(1)} %get-tuple-element.291.z), custom_call_target="tpu_custom_call" | custom-call | tf_op jit(solution)/shard_map/gated/pallas_call | solution.py:465
  (17 shorter events, 0.2 us)
Async XLA Ops:
  3.2 22.4 %collective-permute-start = (bf16[160,128]{1,0:T(8,128)(2,1)S(1)}, bf16[160,128]{1,0:T(8,128)(2,1)S(1)}, u32[]{:S(2)}, u32[]{:S(2)}) collective-permute-start(bf16[160,128]{1,0:T(8,128)(2,1)S(1)} %get-tuple-element.152), channel_id=1, source_target_pairs={{0,64},{16,80},{32,96},{48,112},{1,65},{17,81},{33,97},{49,113},{2... | collective-permute-start | bytes 122888 | tf_op jit(solution)/shard_map/cond/branch_1_fun/ppermute | solution.py:402
  4.6 20.3 %collective-permute-start.1 = (bf16[8,768]{1,0:T(8,128)(2,1)S(1)}, bf16[8,768]{1,0:T(8,128)(2,1)S(1)}, u32[]{:S(2)}, u32[]{:S(2)}) collective-permute-start(bf16[8,768]{1,0:T(8,128)(2,1)S(1)} %branch_1_fun.16), channel_id=1, source_target_pairs={{0,16},{16,32},{32,48},{48,64},{64,80},{80,96},{96,112},{1,17},{17... | collective-permute-start | bytes 36872 | tf_op jit(solution)/shard_map/cond/branch_1_fun/ppermute | solution.py:414
  25.9 0.7 %copy-start.1 = (bf16[4,128,128]{2,1,0:T(8,128)(2,1)}, bf16[4,128,128]{2,1,0:T(8,128)(2,1)S(1)}, u32[]{:S(2)}) copy-start(bf16[4,128,128]{2,1,0:T(8,128)(2,1)S(1)} %get-tuple-element.339) | copy-start | bytes 393220 | tf_op jit(solution)/shard_map/cond
  26.6 0.6 %copy-start.8 = (bf16[4,32,128]{2,1,0:T(8,128)(2,1)}, bf16[4,32,128]{2,1,0:T(8,128)(2,1)S(1)}, u32[]{:S(2)}) copy-start(bf16[4,32,128]{2,1,0:T(8,128)(2,1)S(1)} %get-tuple-element.336) | copy-start | bytes 98308 | tf_op jit(solution)/shard_map/cond
  27.2 0.6 %copy-start.5 = (bf16[160,128]{1,0:T(8,128)(2,1)}, bf16[160,128]{1,0:T(8,128)(2,1)S(1)}, u32[]{:S(2)}) copy-start(bf16[160,128]{1,0:T(8,128)(2,1)S(1)} %get-tuple-element.283.refs_0_) | copy-start | bytes 122884
  27.8 0.9 %copy-start.2 = (bf16[4,128,128]{2,1,0:T(8,128)(2,1)S(1)}, bf16[4,128,128]{2,1,0:T(8,128)(2,1)}, u32[]{:S(2)}) copy-start(bf16[4,128,128]{2,1,0:T(8,128)(2,1)} %get-tuple-element.284.refs_1_) | copy-start | bytes 393220
  28.7 0.8 %copy-start.6 = (bf16[160,128]{1,0:T(8,128)(2,1)S(1)}, bf16[160,128]{1,0:T(8,128)(2,1)}, u32[]{:S(2)}) copy-start(bf16[160,128]{1,0:T(8,128)(2,1)} %copy-done.5) | copy-start | bytes 122884
  29.5 0.7 %copy-start.3 = (bf16[4,128,128]{2,1,0:T(8,128)(2,1)}, bf16[4,128,128]{2,1,0:T(8,128)(2,1)S(1)}, u32[]{:S(2)}) copy-start(bf16[4,128,128]{2,1,0:T(8,128)(2,1)S(1)} %get-tuple-element.287) | copy-start | bytes 393220
  30.2 4.2 %collective-permute-start.6 = (bf16[160,128]{1,0:T(8,128)(2,1)S(1)}, bf16[160,128]{1,0:T(8,128)(2,1)S(1)}, u32[]{:S(2)}, u32[]{:S(2)}) collective-permute-start(bf16[160,128]{1,0:T(8,128)(2,1)S(1)} %branch_0_fun.22), channel_id=1, source_target_pairs={{64,192},{80,208},{96,224},{112,240},{65,193},{81,209},{97,225},{1... | collective-permute-start | bytes 122888 | tf_op jit(solution)/shard_map/cond/branch_0_fun/ppermute | solution.py:402
  31.5 3.2 %collective-permute-start.5 = (bf16[160,128]{1,0:T(8,128)(2,1)S(1)}, bf16[160,128]{1,0:T(8,128)(2,1)S(1)}, u32[]{:S(2)}, u32[]{:S(2)}) collective-permute-start(bf16[160,128]{1,0:T(8,128)(2,1)S(1)} %branch_0_fun.22), channel_id=1, source_target_pairs={{64,128},{80,144},{96,160},{112,176},{65,129},{81,145},{97,161},{1... | collective-permute-start | bytes 122888 | tf_op jit(solution)/shard_map/cond/branch_0_fun/ppermute | solution.py:402
  32.8 1.5 %collective-permute-start.4 = (bf16[8,768]{1,0:T(8,128)(2,1)S(1)}, bf16[8,768]{1,0:T(8,128)(2,1)S(1)}, u32[]{:S(2)}, u32[]{:S(2)}) collective-permute-start(bf16[8,768]{1,0:T(8,128)(2,1)S(1)} %branch_0_fun.20), channel_id=1, source_target_pairs={{112,128},{113,129},{114,130},{115,131},{116,132},{117,133},{118,1... | collective-permute-start | bytes 36872 | tf_op jit(solution)/shard_map/cond/branch_0_fun/ppermute | solution.py:414
  33.5 0.8 %copy-start.9 = (bf16[4,32,128]{2,1,0:T(8,128)(2,1)S(1)}, bf16[4,32,128]{2,1,0:T(8,128)(2,1)}, u32[]{:S(2)}) copy-start(bf16[4,32,128]{2,1,0:T(8,128)(2,1)} %get-tuple-element.171.refs_1_) | copy-start | bytes 98308 | tf_op jit(solution)/shard_map/cond/branch_0_fun/cond

commit v4 on v3

--- a/solution.py
+++ b/solution.py
@@ -95,11 +95,7 @@
     return high, (value - high.astype(F32)).astype(BF16)
 
 
-def state_kernel(
-    z, x, bc, dt, x_taps, bc_taps, per_head, last, first, pay, xc, bcc, cum_out, less_out, z_out, done
-):
-    fetch = pltpu.make_async_copy(z, z_out, done)
-    fetch.start()
+def state_kernel(x, bc, dt, x_taps, bc_taps, per_head, last, first, pay, xc, bcc, cum_out, less_out):
     channels = x.shape[0]
     heads = dt.shape[0]
     width = channels // heads
@@ -153,7 +149,6 @@
         here = slice(quarter * 128, (quarter + 1) * 128)
         rows = jnp.concatenate([tail, edges[:, here], edges[:, channels : channels + 128], gains[:, here]], axis=0)
         pay[quarter, pl.ds(per * width, META), :] = rows.astype(BF16)
-    fetch.wait()
 
 
 def early(series, taps):
@@ -261,13 +256,43 @@
         target[...] = source[...]
 
 
+def pack_kernel(kept, begin, meta, joined, near, kept_out, rows):
+    kept_out[...] = kept[...] + begin[...].astype(F32)
+    at = 0
+    for r in range(LO):
+        rows[at : at + META, :] = meta[r]
+        at += META
+    for block in (joined, near):
+        rows[at : at + block.shape[0], :] = block[...]
+        at += block.shape[0]
+
+
+def unpack_kernel(rows, meta, joined, near):
+    at = 0
+    for r in range(LO):
+        meta[r] = rows[at : at + META, :]
+        at += META
+    for block in (joined, near):
+        block[...] = rows[at : at + block.shape[0], :]
+        at += block.shape[0]
+
+
+def begin_kernel(kept, inner, later, state, inner_out, later_out):
+    state[...] = kept[...].astype(BF16)
+    inner_out[...] = inner[...]
+    later_out[...] = later[...]
+
+
 def blank_kernel(*refs):
     for ref in refs:
         ref[...] = jnp.zeros(ref.shape, ref.dtype)
 
 
-def intra_kernel(*refs, count):
-    rims, (xc, bcc, first, x_taps, bc_taps, cum_in, less_in, per_head, out, c_out) = refs[:count], refs[count:]
+def intra_kernel(z, *refs, count):
+    rims, refs = refs[:count], refs[count:]
+    xc, bcc, first, x_taps, bc_taps, cum_in, less_in, per_head, out, later, done = refs
+    fetch = pltpu.make_async_copy(z, later.at[pl.ds(bcc.shape[0] // 2, z.shape[0])], done)
+    fetch.start()
     heads = cum_in.shape[0]
     channels = xc.shape[0]
     width = channels // heads
@@ -286,7 +311,7 @@
         return jnp.concatenate([jnp.where(lanes < 3, rows, values[:, :128]), values[:, 128:]], axis=1)
 
     both = mended(bcc[...], placed[channels:])
-    c_out[...] = both[states:]
+    later[:states, :] = both[states:]
     gram = dot(both[:states], both[states:], 0, 0)
     keep = lax.broadcasted_iota(jnp.int32, (128, 128), 0) <= lax.broadcasted_iota(jnp.int32, (128, 128), 1)
     for h in range(heads):
@@ -304,19 +329,22 @@
         near = dot(values[:, :128], mix(0, 0, True), 1, 0)
         late = dot(values, jnp.concatenate([mix(0, 128, False), mix(128, 128, True)], axis=0), 1, 0)
         out[at, :] = jnp.concatenate([near, late], axis=1) + skips[h : h + 1] * values.astype(F32)
-
-
-def output_kernel(inner, c_rows, cum, state, z, out, held, done):
+    fetch.wait()
+
+
+def output_kernel(inner, later, cum, state, out, held, done):
     heads = cum.shape[0]
     width = inner.shape[0] // heads
     per = heads // LO
+    states = state.shape[1]
+    c_rows = later[:states, :]
     grown = jnp.exp(cum[...])
     copies = []
     for h in range(heads):
         at = pl.ds(h * width, width)
-        y = inner[at, :] + grown[h : h + 1] * dot(state[at, :], c_rows[...], 1, 0)
+        y = inner[at, :] + grown[h : h + 1] * dot(state[at, :], c_rows, 1, 0)
         y = y.astype(BF16).astype(F32)
-        held[at, :] = (y * silu(z[at, :].astype(F32))).astype(BF16)
+        held[at, :] = (y * silu(later[pl.ds(states + h * width, width), :].astype(F32))).astype(BF16)
         if h % per == per - 1:
             part = pl.ds((h + 1 - per) * width, per * width)
             copies.append(pltpu.make_async_copy(held.at[part], out.at[part], done.at[h // per]))
@@ -330,11 +358,14 @@
 
 
 VMEM = pl.BlockSpec(memory_space=pltpu.VMEM)
+GRANT = pltpu.CompilerParams(vmem_limit_bytes=12 << 20)
 
 
 def run(kernel, outs, *args):
     args = [pltpu.with_memory_space_constraint(a, pltpu.VMEM) for a in args]
-    return pl.pallas_call(kernel, out_shape=outs, in_specs=[VMEM] * len(args), out_specs=[VMEM] * len(outs))(*args)
+    return pl.pallas_call(
+        kernel, out_shape=outs, in_specs=[VMEM] * len(args), out_specs=[VMEM] * len(outs), compiler_params=GRANT
+    )(*args)
 
 
 def local(x_in, z_gate, bc_in, dt_raw, conv_x_w, conv_x_b, conv_bc_w, conv_bc_b, dt_bias, a_log, d_skip):
@@ -371,18 +402,11 @@
         ),
         out_shape=outs,
         name="load",
-    )(group, member, bc_in, taps, x_in, *small)
-    inputs = [pltpu.with_memory_space_constraint(a, pltpu.VMEM) for a in (x, bc, dt, x_taps, bc_taps, per_head, last, first)]
+        compiler_params=GRANT,
+    )(group, member, *[pltpu.with_memory_space_constraint(a, pltpu.HBM) for a in (bc_in, taps, x_in, *small)])
     outs = [shape(LO, quarter + META, states, dtype=BF16), series, pairs]
-    outs += [shape(heads, length), shape(heads, length), series]
-    pay, xc, bcc, cum, less, z = pl.pallas_call(
-        state_kernel,
-        out_shape=outs,
-        in_specs=[pl.BlockSpec(memory_space=pl.ANY)] + [VMEM] * len(inputs),
-        out_specs=[VMEM] * len(outs),
-        scratch_shapes=[pltpu.SemaphoreType.DMA],
-        name="states",
-    )(z_gate, *inputs)
+    outs += [shape(heads, length), shape(heads, length)]
+    pay, xc, bcc, cum, less = run(state_kernel, outs, x, bc, dt, x_taps, bc_taps, per_head, last, first)
 
     def gather(*rest, opening=False):
         got = lax.all_to_all(pay, "near", 0, 0, tiled=True)
@@ -405,15 +429,26 @@
         return tuple(run(copy_kernel, [shape(*a.shape, dtype=a.dtype) for a in arrays], *arrays))
 
     def inside(*rims):
-        outs = [shape(channels, length), shape(states, length, dtype=BF16)]
-        args = (first, x_taps, bc_taps, cum, less, per_head)
-        kernel = lambda *refs: intra_kernel(*refs, count=len(rims))
-        return tuple(run(kernel, outs, *rims, xc, bcc, *args))
+        args = [*rims, xc, bcc, first, x_taps, bc_taps, cum, less, per_head]
+        return tuple(
+            pl.pallas_call(
+                lambda *refs: intra_kernel(*refs, count=len(rims)),
+                out_shape=inner_shapes,
+                in_specs=[pl.BlockSpec(memory_space=pl.ANY)] + [VMEM] * len(args),
+                out_specs=[VMEM] * 2,
+                scratch_shapes=[pltpu.SemaphoreType.DMA],
+                name="intra",
+        compiler_params=GRANT,
+            )(pltpu.with_memory_space_constraint(z_gate, pltpu.HBM), *[pltpu.with_memory_space_constraint(a, pltpu.VMEM) for a in args])
+        )
 
     def shifted(begin, end):
         return lax.ppermute(kept_on(last)[0], cp, [(i, i + 1) for i in range(begin, end)])
 
-    inner_shapes = [shape(channels, length), shape(states, length, dtype=BF16)]
+    inner_shapes = [shape(channels, length), shape(states + channels, length, dtype=BF16)]
+
+    packed_rows_count = LO * META + 2 * (quarter + META)
+    packed_shapes = [kept_shapes[0], shape(packed_rows_count, states, dtype=BF16)]
 
     def low_part():
         kept = lax.cond(
@@ -429,8 +464,8 @@
         )
         inner = inside(rims)
         (joined,) = run(lambda *refs: join_kernel(*refs, per=per), [block_shape], near, kept[2], own_taps)
-        kept, meta, near, begin = kept_on(*kept[:2], near, begin)
-        return (kept, meta, joined, near, begin, *inner)
+        packed = run(pack_kernel, packed_shapes, kept[0], begin, kept[1], joined, near)
+        return (*packed, *inner)
 
     def high_part(*kept):
         rims = shifted(2 * LO, count - 1)
@@ -439,8 +474,8 @@
         kept = lax.cond(far == 3, lambda *kept: gather(), kept_on, *kept[:2])
         return kept_on(*kept, between, rims)
 
-    def later_part(kept, meta, joined, near, begin, *inner):
-        (joined,) = kept_on(joined)
+    def later_part(kept, packed, *inner):
+        meta, joined, near = run(unpack_kernel, [kept_shapes[1], block_shape, block_shape], packed)
         over = sent(joined, 1, 3)
         next_one = sent(joined, 1, 2)
         rims_mid = shifted(2 * LO - 1, 2 * LO)
@@ -455,13 +490,14 @@
         (state,) = exchange(*kept_on(*kept), own_taps, near, next_one, over, between)
         return (state, *inner)
 
-    parts = lax.cond(
-        far < 2, low_part, lambda: blank(*kept_shapes, block_shape, block_shape, state_shape, *inner_shapes)
+    parts = lax.cond(far < 2, low_part, lambda: blank(*packed_shapes, *inner_shapes))
+    state, inner, later = lax.cond(
+        far == 0,
+        lambda kept, packed, *inner: tuple(run(begin_kernel, [state_shape, *inner_shapes], kept, *inner)),
+        later_part,
+        *parts,
     )
-    parts = list(parts)
-    parts[2], parts[4] = kept_on(parts[2], parts[4])
-    state, inner, c_rows = lax.cond(far == 0, lambda *parts: kept_on(*parts[4:]), later_part, *parts)
-    inputs = [inner, c_rows, cum, state.reshape(channels, states), z]
+    inputs = [inner, later, cum, state.reshape(channels, states)]
     return pl.pallas_call(
         output_kernel,
         out_shape=jax.ShapeDtypeStruct((channels, length), BF16),
@@ -469,6 +505,7 @@
         out_specs=pl.BlockSpec(memory_space=pl.ANY),
         scratch_shapes=[pltpu.VMEM((channels, length), BF16), pltpu.SemaphoreType.DMA((LO,))],
         name="gated",
+    compiler_params=GRANT,
     )(*[pltpu.with_memory_space_constraint(a, pltpu.VMEM) for a in inputs])
 
 

time: 45 us -> 40.6 us (0.902)
  local copies, waits for them, and re-layouts: 4.97 us -> 0.01 us
  waiting for transfers between devices: 4.01 us -> 4.47 us
    unnamed x8 -> x2, local copies, waits for them, and re-layouts: 2.95 us -> 0.01 us
    cond x6 -> x0, local copies, waits for them, and re-layouts: 2.01 us -> none
    pallas_call x1, Pallas kernels: 1.81 us -> 0.85 us  [inside(): pl.pallas_call(lambda *refs: intra_kernel(*refs, count=len(rims)), out_sh...]
    pallas_call x14 -> x13, Pallas kernels: 1.68 us -> 2.58 us  [run(): pl.pallas_call(kernel, out_shape=outs, in_specs=[VMEM] * len(args), out_s...]
    ppermute x3, waiting for transfers between devices: 0.31 us -> 0.77 us  [sent(): return lax.ppermute(block, cp, route)]
where the time goes in v4:
time: 40.6 us; the launch traced here: 40.4 us
  blocking collectives  21 us (52%)
  starting transfers between devices  8.82 us (22%)
  Pallas kernels  5.74 us (14%)
  waiting for transfers between devices  4.47 us (11%)
    all_to_all x1, blocking collectives, gather(): got = lax.all_to_all(pay, 'near', 0, 0, tiled=True)  12 us
    all_to_all x1, blocking collectives, exchange(): return tuple(rest) + (lax.all_to_all(entering, 'near', 0, 0, tiled=True),)  8.99 us
    ppermute x2, starting transfers between devices, shifted(): lax.ppermute(kept_on(last)[0], cp, [(i, i + 1) for i in range(begin, end)])  4.94 us
    ppermute x3, starting transfers between devices, sent(): return lax.ppermute(block, cp, route)  3.88 us
    ppermute x2, waiting for transfers between devices, shifted(): lax.ppermute(kept_on(last)[0], cp, [(i, i + 1) for i in range(begin, end)])  3.69 us
    pallas_call x13, Pallas kernels, run(): pl.pallas_call(kernel, out_shape=outs, in_specs=[VMEM] * len(args), out_s...  2.58 us
    pallas_call x1, Pallas kernels, local(): pl.pallas_call(load_kernel, grid_spec=pltpu.PrefetchScalarGridSpec(num_sc...  1.34 us
    pallas_call x1, Pallas kernels, local(): pl.pallas_call(output_kernel, out_shape=jax.ShapeDtypeStruct((channels, l...  0.98 us
  transfers between devices with their start and end apart: 5, of which 2 were waited for; matrix products, arithmetic and copies ran while one was open for 0% of the time, Pallas kernels for 3%

profile of v4, /device:TPU:256, one launch (start us, length us, event | category | flops | bytes accessed | tf_op | source)
XLA Modules:
  0.0 40.4 jit_solution(5457375281346615956)
XLA Ops:
  0.0 1.3 %load.1 = (bf16[8,768]{1,0:T(8,128)(2,1)S(1)}, bf16[8,768]{1,0:T(8,128)(2,1)S(1)}, bf16[512,256]{1,0:T(8,128)(2,1)S(1)}, bf16[256,256]{1,0:T(8,128)(2,1)S(1)}, b...) custom-call(s32[1]{0:T(128)} %bitcast.2.group, ...), custom_call_target="tpu_custom_call" | custom-call | tf_op jit(solution)/shard_map/load/pallas_call | solution.py:394
  1.3 0.0 copy-start
  1.3 1.7 %shard_map.109 = (bf16[4,160,128]{2,1,0:T(8,128)(2,1)S(1)}, bf16[512,256]{1,0:T(8,128)(2,1)S(1)}, bf16[256,256]{1,0:T(8,128)(2,1)S(1)}, f32[8,256]{1,0:T(8,128)S(1)}, f32[8,256]{1,0:T(8,128)S(1)}) custom-call(bf16[512,256]{1,0:T(8,128)(2,1)S(1)} %get-tuple-element.263.x, bf16[256,256]{1,0:T(8,128)(2,1)S(1)} %get-tuple-element.264.bc, ...), custom_call_target="tpu_custom_call" | custom-call | tf_op jit(solution)/shard_map/pallas_call | solution.py:366
  3.0 0.0 copy-done
  3.0 22.8 %conditional.8 = ((f32[4,128,128]{2,1,0:T(8,128)S(1)}, bf16[448,128]{1,0:T(8,128)(2,1)S(1)}, f32[512,256]{1,0:T(8,128)S(1)}, bf16[640,256]{1,0:T(8,128)(2,1)S(1)})) conditional(s32[]{:T(128)} %convert_element_type.21, () %tuple.61, (s32[]{:T(128)}, bf16[4,160,128]{2,1,0:T(8,128)(2,1)S(1)}, f32[2,8,128]{2,1,0:T(8,128)S(1)}, ...), branch_computations={%region_0.1_spmd, %region_1.6_spmd} | conditional | flops 2 | bytes 868534 | solution.py:493
  3.1 1.3 %collective-permute-start = (bf16[160,128]{1,0:T(8,128)(2,1)S(1)}, bf16[160,128]{1,0:T(8,128)(2,1)S(1)}, u32[]{:S(2)}, u32[]{:S(2)}) collective-permute-start(bf16[160,128]{1,0:T(8,128)(2,1)S(1)} %get-tuple-element.155), channel_id=1, source_target_pairs={{0,64},{16,80},{32,96},{48,112},{1,65},{17,81},{33,97},{49,113},{2... | collective-permute-start | bytes 122888 | tf_op jit(solution)/shard_map/cond/branch_1_fun/ppermute | solution.py:426
  4.4 4.3 %collective-permute-start.1 = (bf16[8,768]{1,0:T(8,128)(2,1)S(1)}, bf16[8,768]{1,0:T(8,128)(2,1)S(1)}, u32[]{:S(2)}, u32[]{:S(2)}) collective-permute-start(bf16[8,768]{1,0:T(8,128)(2,1)S(1)} %branch_1_fun.14), channel_id=1, source_target_pairs={{0,16},{16,32},{32,48},{48,64},{64,80},{80,96},{96,112},{1,17},{17... | collective-permute-start | bytes 36872 | tf_op jit(solution)/shard_map/cond/branch_1_fun/ppermute | solution.py:446
  8.7 12.3 %conditional.1 = ((f32[4,128,128]{2,1,0:T(8,128)S(1)}, bf16[4,32,128]{2,1,0:T(8,128)(2,1)S(1)}, bf16[160,128]{1,0:T(8,128)(2,1)S(1)}, bf16[4,128,128]{2,1,0:T(8,128)(2,1)S(1)})) conditional(s32[]{:T(128)} %convert_element_type.5, (bf16[4,160,128]{2,1,0:T(8,128)(2,1)S(1)}, f32[2,8,128]{2,1,0:T(8,128)S(1)}) %tuple.40, (f32[4,128,128]{2,1,0:T(8,128)S(1)}, ...), branch_computations={%region_4.4_spmd, %region_5.5_spmd} | conditional | bytes 327688 | solution.py:459
  8.7 12.0 %all_to_all.25.refs_0_ = bf16[4,160,128]{2,1,0:T(8,128)(2,1)S(1)} all-to-all(bf16[4,160,128]{2,1,0:T(8,128)(2,1)S(1)} %get-tuple-element.139), channel_id=1, replica_groups=mesh['dp'=4,'far'=4,'near'=4,'tensor'=16] {'near'}, dimensions={0} | all-to-all | bytes 327680 | tf_op jit(solution)/shard_map/cond/branch_1_fun/cond/branch_0_fun/all_to_all | solution.py:412
  20.8 0.2 branch_0_fun.14
  21.0 3.7 %collective-permute-done.1.refs_1_ = bf16[8,768]{1,0:T(8,128)(2,1)S(1)} collective-permute-done((bf16[8,768]{1,0:T(8,128)(2,1)S(1)}, bf16[8,768]{1,0:T(8,128)(2,1)S(1)}, u32[]{:S(2)}, u32[]{:S(2)}) %collective-permute-start.1) | collective-permute-done | bytes 12320 | tf_op jit(solution)/shard_map/cond/branch_1_fun/ppermute | solution.py:446
  24.7 0.9 %intra.2 = (f32[512,256]{1,0:T(8,128)S(1)}, bf16[640,256]{1,0:T(8,128)(2,1)S(1)}) custom-call(bf16[512,256]{1,0:T(8,128)(2,1)S(1)} %get-tuple-element.159.refs_0_, bf16[8,768]{1,0:T(8,128)(2,1)S(1)} %collective-permute-done.1.refs_1_, bf16[512,256]{1,0:T(8,128)(2,1)S(1)} %get-tuple-element.161.refs_2_, bf16[256,256]{1,0:T(8,128)(2,1)S(1)} %get-tuple-element.162.refs_3_, ...), custom_call_target="tpu_custom_call" | custom-call | tf_op jit(solution)/shard_map/cond/branch_1_fun/intra/pallas_call | solution.py:434
  25.6 0.0 collective-permute-done.refs_0_.near
  25.6 0.2 branch_1_fun.12.joined
  25.9 13.5 %conditional.9 = (f32[512,256]{1,0:T(8,128)S(1)}, bf16[640,256]{1,0:T(8,128)(2,1)S(1)}, bf16[512,128]{1,0:T(8,128)(2,1)S(1)}) conditional(s32[]{:T(128)} %convert_element_type.20, (s32[]{:T(128)}, bf16[448,128]{1,0:T(8,128)(2,1)S(1)}, f32[4,128,128]{2,1,0:T(8,128)S(1)}, bf16[4,160,128]{2,1,0:T(8,128)(2,1)S(1)}, f32[2,8,128]{2,1,0:T(8,128)S(1)}, ...), branch_computations={%region_6.15_spmd, %region_15.16_spmd} | conditional | flops 6 | bytes 2556414 | solution.py:494
  25.9 1.3 %collective-permute-start.6 = (bf16[160,128]{1,0:T(8,128)(2,1)S(1)}, bf16[160,128]{1,0:T(8,128)(2,1)S(1)}, u32[]{:S(2)}, u32[]{:S(2)}) collective-permute-start(bf16[160,128]{1,0:T(8,128)(2,1)S(1)} %get-tuple-element.234), channel_id=1, source_target_pairs={{64,192},{80,208},{96,224},{112,240},{65,193},{81,209},{97,225},{1... | collective-permute-start | bytes 122888 | tf_op jit(solution)/shard_map/cond/branch_0_fun/ppermute | solution.py:426
  27.2 1.3 %collective-permute-start.5 = (bf16[160,128]{1,0:T(8,128)(2,1)S(1)}, bf16[160,128]{1,0:T(8,128)(2,1)S(1)}, u32[]{:S(2)}, u32[]{:S(2)}) collective-permute-start(bf16[160,128]{1,0:T(8,128)(2,1)S(1)} %get-tuple-element.234), channel_id=1, source_target_pairs={{64,128},{80,144},{96,160},{112,176},{65,129},{81,145},{97,161},{1... | collective-permute-start | bytes 122888 | tf_op jit(solution)/shard_map/cond/branch_0_fun/ppermute | solution.py:426
  28.5 0.7 %collective-permute-start.4 = (bf16[8,768]{1,0:T(8,128)(2,1)S(1)}, bf16[8,768]{1,0:T(8,128)(2,1)S(1)}, u32[]{:S(2)}, u32[]{:S(2)}) collective-permute-start(bf16[8,768]{1,0:T(8,128)(2,1)S(1)} %branch_0_fun.21), channel_id=1, source_target_pairs={{112,128},{113,129},{114,130},{115,131},{116,132},{117,133},{118,1... | collective-permute-start | bytes 36872 | tf_op jit(solution)/shard_map/cond/branch_0_fun/ppermute | solution.py:446
  29.2 0.1 conditional.4
  29.3 0.0 collective-permute-done.4
  29.3 0.1 conditional.5
  29.3 0.1 branch_0_fun.19
  29.4 0.0 collective-permute-done.6.refs_5_
  29.4 0.8 %collective-permute-done.5.refs_4_ = bf16[160,128]{1,0:T(8,128)(2,1)S(1)} collective-permute-done((bf16[160,128]{1,0:T(8,128)(2,1)S(1)}, bf16[160,128]{1,0:T(8,128)(2,1)S(1)}, u32[]{:S(2)}, u32[]{:S(2)}) %collective-permute-start.5) | collective-permute-done | bytes 40992 | tf_op jit(solution)/shard_map/cond/branch_0_fun/ppermute | solution.py:426
  30.1 0.2 branch_0_fun.23
  30.4 9.0 %all_to_all.29 = bf16[4,128,128]{2,1,0:T(8,128)(2,1)S(1)} all-to-all(bf16[4,128,128]{2,1,0:T(8,128)(2,1)S(1)} %branch_0_fun.23), channel_id=1, replica_groups=mesh['dp'=4,'far'=4,'near'=4,'tensor'=16] {'near'}, dimensions={0} | all-to-all | bytes 262144 | tf_op jit(solution)/shard_map/cond/branch_0_fun/all_to_all | solution.py:422
  39.4 1.0 %gated.1 = bf16[512,256]{1,0:T(8,128)(2,1)} custom-call(f32[512,256]{1,0:T(8,128)S(1)} %get-tuple-element.281.inner, bf16[640,256]{1,0:T(8,128)(2,1)S(1)} %get-tuple-element.282.later, f32[8,256]{1,0:T(8,128)S(1)} %get-tuple-element.275.cum, bf16[512,128]{1,0:T(8,128)(2,1)S(1)} %get-tuple-element.283.state), custom_call_target="tpu_custom_call" | custom-call | tf_op jit(solution)/shard_map/gated/pallas_call | solution.py:501
  (9 shorter events, 0.2 us)
Async XLA Ops:
  1.3 1.7 %copy-start = (bf16[512,256]{1,0:T(8,128)(2,1)S(1)}, bf16[512,256]{1,0:T(8,128)(2,1)}, u32[]{:S(2)}) copy-start(bf16[512,256]{1,0:T(8,128)(2,1)} %param.28) | copy-start | bytes 786436
  3.1 22.4 %collective-permute-start = (bf16[160,128]{1,0:T(8,128)(2,1)S(1)}, bf16[160,128]{1,0:T(8,128)(2,1)S(1)}, u32[]{:S(2)}, u32[]{:S(2)}) collective-permute-start(bf16[160,128]{1,0:T(8,128)(2,1)S(1)} %get-tuple-element.155), channel_id=1, source_target_pairs={{0,64},{16,80},{32,96},{48,112},{1,65},{17,81},{33,97},{49,113},{2... | collective-permute-start | bytes 122888 | tf_op jit(solution)/shard_map/cond/branch_1_fun/ppermute | solution.py:426
  4.4 20.3 %collective-permute-start.1 = (bf16[8,768]{1,0:T(8,128)(2,1)S(1)}, bf16[8,768]{1,0:T(8,128)(2,1)S(1)}, u32[]{:S(2)}, u32[]{:S(2)}) collective-permute-start(bf16[8,768]{1,0:T(8,128)(2,1)S(1)} %branch_1_fun.14), channel_id=1, source_target_pairs={{0,16},{16,32},{32,48},{48,64},{64,80},{80,96},{96,112},{1,17},{17... | collective-permute-start | bytes 36872 | tf_op jit(solution)/shard_map/cond/branch_1_fun/ppermute | solution.py:446
  25.9 3.5 %collective-permute-start.6 = (bf16[160,128]{1,0:T(8,128)(2,1)S(1)}, bf16[160,128]{1,0:T(8,128)(2,1)S(1)}, u32[]{:S(2)}, u32[]{:S(2)}) collective-permute-start(bf16[160,128]{1,0:T(8,128)(2,1)S(1)} %get-tuple-element.234), channel_id=1, source_target_pairs={{64,192},{80,208},{96,224},{112,240},{65,193},{81,209},{97,225},{1... | collective-permute-start | bytes 122888 | tf_op jit(solution)/shard_map/cond/branch_0_fun/ppermute | solution.py:426
  27.2 3.0 %collective-permute-start.5 = (bf16[160,128]{1,0:T(8,128)(2,1)S(1)}, bf16[160,128]{1,0:T(8,128)(2,1)S(1)}, u32[]{:S(2)}, u32[]{:S(2)}) collective-permute-start(bf16[160,128]{1,0:T(8,128)(2,1)S(1)} %get-tuple-element.234), channel_id=1, source_target_pairs={{64,128},{80,144},{96,160},{112,176},{65,129},{81,145},{97,161},{1... | collective-permute-start | bytes 122888 | tf_op jit(solution)/shard_map/cond/branch_0_fun/ppermute | solution.py:426
  28.5 0.8 %collective-permute-start.4 = (bf16[8,768]{1,0:T(8,128)(2,1)S(1)}, bf16[8,768]{1,0:T(8,128)(2,1)S(1)}, u32[]{:S(2)}, u32[]{:S(2)}) collective-permute-start(bf16[8,768]{1,0:T(8,128)(2,1)S(1)} %branch_0_fun.21), channel_id=1, source_target_pairs={{112,128},{113,129},{114,130},{115,131},{116,132},{117,133},{118,1... | collective-permute-start | bytes 36872 | tf_op jit(solution)/shard_map/cond/branch_0_fun/ppermute | solution.py:446

commit v5 on v4

--- a/solution.py
+++ b/solution.py
@@ -21,7 +21,8 @@
 
 
 def silu(v):
-    return v / (1.0 + jnp.exp(-v))
+    half = 0.5 * v
+    return half + half * jnp.tanh(half)
 
 
 def log1p(u):
@@ -103,13 +104,14 @@
 
     delta = softplus(dt[...].astype(F32) + per_head[0][:, :1])
     scaled = delta * -jnp.exp(per_head[1][:, :1])
-    high = scaled.astype(BF16)
-    mid, low = split(scaled - high.astype(F32))
+    high = scaled.astype(BF16).astype(F32)
+    mid = (scaled - high).astype(BF16).astype(F32)
     size = scaled.shape[1]
     upto = jnp.where(
         lax.broadcasted_iota(jnp.int32, (size, size), 0) <= lax.broadcasted_iota(jnp.int32, (size, size), 1), 1.0, 0.0
     ).astype(BF16)
-    cum = dot(low, upto, 1, 0) + dot(mid, upto, 1, 0) + dot(high, upto, 1, 0)
+    sums = dot(jnp.concatenate([scaled - high - mid, mid, high], axis=0).astype(BF16), upto, 1, 0)
+    cum = sums[:heads] + sums[heads : 2 * heads] + sums[2 * heads :]
     cum_out[...] = cum
     less_out[...] = cum - jnp.log(delta)
     end = cum[:, size - 1 :]
@@ -117,15 +119,11 @@
     total_high, total_low = split(jnp.exp(end))
     total_high, total_low = total_high.astype(F32), total_low.astype(F32)
 
-    spread = jnp.where(
-        lax.broadcasted_iota(jnp.int32, (heads, channels), 1) // width
-        == lax.broadcasted_iota(jnp.int32, (heads, channels), 0),
-        1.0,
-        0.0,
-    ).astype(BF16)
-    gain_high, gain_low = split(gain[:, :128])
+    opening = gain[:, :128].T[:8]
+    gains = jnp.concatenate([jnp.broadcast_to(opening[:, h : h + 1], (8, width)) for h in range(heads)], axis=1)
+    gain_high = gains.astype(BF16).astype(F32)
     lines = lax.broadcasted_iota(jnp.int32, (8, channels), 0)
-    gains = jnp.where(lines < 4, dot(gain_high, spread, 0, 0)[:8], pltpu.roll(dot(gain_low, spread, 0, 0)[:8], 4, 0))
+    gains = jnp.where(lines < 4, gain_high, pltpu.roll(gains - gain_high, 4, 0))
     lines = lax.broadcasted_iota(jnp.int32, last.shape, 0)
     edges = jnp.where(lines < 3, last[...].astype(F32), pltpu.roll(first[...].astype(F32), 3, 0))
 
@@ -277,10 +275,8 @@
         at += block.shape[0]
 
 
-def begin_kernel(kept, inner, later, state, inner_out, later_out):
+def begin_kernel(kept, state):
     state[...] = kept[...].astype(BF16)
-    inner_out[...] = inner[...]
-    later_out[...] = later[...]
 
 
 def blank_kernel(*refs):
@@ -462,10 +458,9 @@
             lambda *kept: gather(block_shape, state_shape),
             *kept,
         )
-        inner = inside(rims)
         (joined,) = run(lambda *refs: join_kernel(*refs, per=per), [block_shape], near, kept[2], own_taps)
         packed = run(pack_kernel, packed_shapes, kept[0], begin, kept[1], joined, near)
-        return (*packed, *inner)
+        return (*packed, *kept_on(rims))
 
     def high_part(*kept):
         rims = shifted(2 * LO, count - 1)
@@ -474,26 +469,28 @@
         kept = lax.cond(far == 3, lambda *kept: gather(), kept_on, *kept[:2])
         return kept_on(*kept, between, rims)
 
-    def later_part(kept, packed, *inner):
+    def later_part(kept, packed, rims_low):
         meta, joined, near = run(unpack_kernel, [kept_shapes[1], block_shape, block_shape], packed)
         over = sent(joined, 1, 3)
         next_one = sent(joined, 1, 2)
         rims_mid = shifted(2 * LO - 1, 2 * LO)
         *kept, between, rims = lax.cond(
-            far >= 2, high_part, lambda *kept: kept_on(*kept) + blank(block_shape, strip), kept, meta
+            far >= 2,
+            high_part,
+            lambda *kept: kept_on(*kept[:2]) + blank(block_shape) + kept_on(kept[2]),
+            kept,
+            meta,
+            rims_low,
         )
-        inner = lax.cond(
-            far >= 2, lambda rims, rims_mid, *inner: inside(rims, rims_mid),
-            lambda rims, rims_mid, *inner: kept_on(*inner), rims, rims_mid, *inner
-        )
+        inner = inside(rims, rims_mid)
         between, *inner = lax.optimization_barrier((between, *inner))
         (state,) = exchange(*kept_on(*kept), own_taps, near, next_one, over, between)
         return (state, *inner)
 
-    parts = lax.cond(far < 2, low_part, lambda: blank(*packed_shapes, *inner_shapes))
+    parts = lax.cond(far < 2, low_part, lambda: blank(*packed_shapes, strip))
     state, inner, later = lax.cond(
         far == 0,
-        lambda kept, packed, *inner: tuple(run(begin_kernel, [state_shape, *inner_shapes], kept, *inner)),
+        lambda kept, packed, rims: tuple(run(begin_kernel, [state_shape], kept)) + inside(rims),
         later_part,
         *parts,
     )

time: 40.6 us -> 41.4 us (1.020)
  blocking collectives: 21 us -> 22 us
    all_to_all x1, blocking collectives: 8.99 us -> 9.99 us  [exchange(): return tuple(rest) + (lax.all_to_all(entering, 'near', 0, 0, tiled=True),)]
    pallas_call x13 -> x14, Pallas kernels: 2.58 us -> 2.49 us  [run(): pl.pallas_call(kernel, out_shape=outs, in_specs=[VMEM] * len(args), out_s...]
  transfers between devices with their start and end apart: 5 -> 5, of which waited for: 2 -> 3; matrix products, arithmetic and copies ran while one was open for 0% -> 0% of each run, Pallas kernels for 3% -> 3%
where the time goes in v5:
time: 41.4 us; the launch traced here: 41.1 us
  blocking collectives  22 us (53%)
  starting transfers between devices  8.82 us (21%)
  Pallas kernels  5.73 us (14%)
  waiting for transfers between devices  4.3 us (10%)
    all_to_all x1, blocking collectives, gather(): got = lax.all_to_all(pay, 'near', 0, 0, tiled=True)  12 us
    all_to_all x1, blocking collectives, exchange(): return tuple(rest) + (lax.all_to_all(entering, 'near', 0, 0, tiled=True),)  9.99 us
    ppermute x2, starting transfers between devices, shifted(): lax.ppermute(kept_on(last)[0], cp, [(i, i + 1) for i in range(begin, end)])  4.94 us
    ppermute x3, starting transfers between devices, sent(): return lax.ppermute(block, cp, route)  3.88 us
    ppermute x2, waiting for transfers between devices, shifted(): lax.ppermute(kept_on(last)[0], cp, [(i, i + 1) for i in range(begin, end)])  3.69 us
    pallas_call x14, Pallas kernels, run(): pl.pallas_call(kernel, out_shape=outs, in_specs=[VMEM] * len(args), out_s...  2.49 us
    pallas_call x1, Pallas kernels, local(): pl.pallas_call(load_kernel, grid_spec=pltpu.PrefetchScalarGridSpec(num_sc...  1.34 us
    pallas_call x1, Pallas kernels, inside(): pl.pallas_call(lambda *refs: intra_kernel(*refs, count=len(rims)), out_sh...  0.97 us
  transfers between devices with their start and end apart: 5, of which 3 were waited for; matrix products, arithmetic and copies ran while one was open for 0% of the time, Pallas kernels for 3%

profile of v5, /device:TPU:256, one launch (start us, length us, event | category | flops | bytes accessed | tf_op | source)
XLA Modules:
  0.0 41.1 jit_solution(4098401079609415084)
XLA Ops:
  0.0 1.3 %load.1 = (bf16[8,768]{1,0:T(8,128)(2,1)S(1)}, bf16[8,768]{1,0:T(8,128)(2,1)S(1)}, bf16[512,256]{1,0:T(8,128)(2,1)S(1)}, bf16[256,256]{1,0:T(8,128)(2,1)S(1)}, b...) custom-call(s32[1]{0:T(128)} %bitcast.2.group, ...), custom_call_target="tpu_custom_call" | custom-call | tf_op jit(solution)/shard_map/load/pallas_call | solution.py:390
  1.3 1.7 %shard_map.109 = (bf16[4,160,128]{2,1,0:T(8,128)(2,1)S(1)}, bf16[512,256]{1,0:T(8,128)(2,1)S(1)}, bf16[256,256]{1,0:T(8,128)(2,1)S(1)}, f32[8,256]{1,0:T(8,128)S(1)}, f32[8,256]{1,0:T(8,128)S(1)}) custom-call(bf16[512,256]{1,0:T(8,128)(2,1)S(1)} %get-tuple-element.212.x, bf16[256,256]{1,0:T(8,128)(2,1)S(1)} %get-tuple-element.213.bc, ...), custom_call_target="tpu_custom_call" | custom-call | tf_op jit(solution)/shard_map/pallas_call | solution.py:362
  3.0 22.4 %conditional.7 = ((f32[4,128,128]{2,1,0:T(8,128)S(1)}, bf16[448,128]{1,0:T(8,128)(2,1)S(1)}, bf16[8,768]{1,0:T(8,128)(2,1)S(1)})) conditional(s32[]{:T(128)} %convert_element_type.20, () %tuple.55, (s32[]{:T(128)}, bf16[4,160,128]{2,1,0:T(8,128)(2,1)S(1)}, f32[2,8,128]{2,1,0:T(8,128)S(1)}, bf16[8,768]{1,0:T(8,128)(2,1)S(1)}) %tuple.56), branch_computations={%region_0.1_spmd, %region_1.6_spmd} | conditional | flops 2 | bytes 868526 | solution.py:490
  3.1 1.3 %collective-permute-start = (bf16[160,128]{1,0:T(8,128)(2,1)S(1)}, bf16[160,128]{1,0:T(8,128)(2,1)S(1)}, u32[]{:S(2)}, u32[]{:S(2)}) collective-permute-start(bf16[160,128]{1,0:T(8,128)(2,1)S(1)} %get-tuple-element.124), channel_id=1, source_target_pairs={{0,64},{16,80},{32,96},{48,112},{1,65},{17,81},{33,97},{49,113},{2... | collective-permute-start | bytes 122888 | tf_op jit(solution)/shard_map/cond/branch_1_fun/ppermute | solution.py:422
  4.4 4.3 %collective-permute-start.1 = (bf16[8,768]{1,0:T(8,128)(2,1)S(1)}, bf16[8,768]{1,0:T(8,128)(2,1)S(1)}, u32[]{:S(2)}, u32[]{:S(2)}) collective-permute-start(bf16[8,768]{1,0:T(8,128)(2,1)S(1)} %branch_1_fun.15), channel_id=1, source_target_pairs={{0,16},{16,32},{32,48},{48,64},{64,80},{80,96},{96,112},{1,17},{17... | collective-permute-start | bytes 36872 | tf_op jit(solution)/shard_map/cond/branch_1_fun/ppermute | solution.py:442
  8.7 12.3 %conditional.1 = ((f32[4,128,128]{2,1,0:T(8,128)S(1)}, bf16[4,32,128]{2,1,0:T(8,128)(2,1)S(1)}, bf16[160,128]{1,0:T(8,128)(2,1)S(1)}, bf16[4,128,128]{2,1,0:T(8,128)(2,1)S(1)})) conditional(s32[]{:T(128)} %convert_element_type.6, (bf16[4,160,128]{2,1,0:T(8,128)(2,1)S(1)}, f32[2,8,128]{2,1,0:T(8,128)S(1)}) %tuple.36, (f32[4,128,128]{2,1,0:T(8,128)S(1)}, ...), branch_computations={%region_4.4_spmd, %region_5.5_spmd} | conditional | bytes 327688 | solution.py:455
  8.7 12.0 %all_to_all.25.refs_0_ = bf16[4,160,128]{2,1,0:T(8,128)(2,1)S(1)} all-to-all(bf16[4,160,128]{2,1,0:T(8,128)(2,1)S(1)} %get-tuple-element.108), channel_id=1, replica_groups=mesh['dp'=4,'far'=4,'near'=4,'tensor'=16] {'near'}, dimensions={0} | all-to-all | bytes 327680 | tf_op jit(solution)/shard_map/cond/branch_1_fun/cond/branch_0_fun/all_to_all | solution.py:408
  20.7 0.2 branch_0_fun.14
  21.0 3.7 %collective-permute-done.1.refs_0_ = bf16[8,768]{1,0:T(8,128)(2,1)S(1)} collective-permute-done((bf16[8,768]{1,0:T(8,128)(2,1)S(1)}, bf16[8,768]{1,0:T(8,128)(2,1)S(1)}, u32[]{:S(2)}, u32[]{:S(2)}) %collective-permute-start.1) | collective-permute-done | bytes 12320 | tf_op jit(solution)/shard_map/cond/branch_1_fun/ppermute | solution.py:442
  24.6 0.5 %collective-permute-done.refs_0_.near = bf16[160,128]{1,0:T(8,128)(2,1)S(1)} collective-permute-done((bf16[160,128]{1,0:T(8,128)(2,1)S(1)}, bf16[160,128]{1,0:T(8,128)(2,1)S(1)}, u32[]{:S(2)}, u32[]{:S(2)}) %collective-permute-start) | collective-permute-done | bytes 40992 | tf_op jit(solution)/shard_map/cond/branch_1_fun/ppermute | solution.py:422
  25.2 0.2 branch_1_fun.13.joined
  25.4 14.7 %conditional.8 = (f32[512,256]{1,0:T(8,128)S(1)}, bf16[640,256]{1,0:T(8,128)(2,1)S(1)}, bf16[512,128]{1,0:T(8,128)(2,1)S(1)}) conditional(s32[]{:T(128)} %convert_element_type.19, (s32[]{:T(128)}, bf16[448,128]{1,0:T(8,128)(2,1)S(1)}, f32[4,128,128]{2,1,0:T(8,128)S(1)}, bf16[8,768]{1,0:T(8,128)(2,1)S(1)}, bf16[4,160,128]{2,1,0:T(8,128)(2,1)S(1)}, ...), branch_computations={%region_6.13_spmd, %region_13.14_spmd} | conditional | flops 6 | bytes 1507706 | solution.py:491
  25.4 1.3 %collective-permute-start.6 = (bf16[160,128]{1,0:T(8,128)(2,1)S(1)}, bf16[160,128]{1,0:T(8,128)(2,1)S(1)}, u32[]{:S(2)}, u32[]{:S(2)}) collective-permute-start(bf16[160,128]{1,0:T(8,128)(2,1)S(1)} %get-tuple-element.177), channel_id=1, source_target_pairs={{64,192},{80,208},{96,224},{112,240},{65,193},{81,209},{97,225},{1... | collective-permute-start | bytes 122888 | tf_op jit(solution)/shard_map/cond/branch_0_fun/ppermute | solution.py:422
  26.7 1.3 %collective-permute-start.5 = (bf16[160,128]{1,0:T(8,128)(2,1)S(1)}, bf16[160,128]{1,0:T(8,128)(2,1)S(1)}, u32[]{:S(2)}, u32[]{:S(2)}) collective-permute-start(bf16[160,128]{1,0:T(8,128)(2,1)S(1)} %get-tuple-element.177), channel_id=1, source_target_pairs={{64,128},{80,144},{96,160},{112,176},{65,129},{81,145},{97,161},{1... | collective-permute-start | bytes 122888 | tf_op jit(solution)/shard_map/cond/branch_0_fun/ppermute | solution.py:422
  28.1 0.7 %collective-permute-start.4 = (bf16[8,768]{1,0:T(8,128)(2,1)S(1)}, bf16[8,768]{1,0:T(8,128)(2,1)S(1)}, u32[]{:S(2)}, u32[]{:S(2)}) collective-permute-start(bf16[8,768]{1,0:T(8,128)(2,1)S(1)} %branch_0_fun.21), channel_id=1, source_target_pairs={{112,128},{113,129},{114,130},{115,131},{116,132},{117,133},{118,1... | collective-permute-start | bytes 36872 | tf_op jit(solution)/shard_map/cond/branch_0_fun/ppermute | solution.py:442
  28.7 0.1 conditional.4
  28.8 0.0 collective-permute-done.4.refs_2_
  28.8 1.0 %intra.2 = (f32[512,256]{1,0:T(8,128)S(1)}, bf16[640,256]{1,0:T(8,128)(2,1)S(1)}) custom-call(bf16[512,256]{1,0:T(8,128)(2,1)} %get-tuple-element.158.refs_0_, bf16[8,768]{1,0:T(8,128)(2,1)S(1)} %get-tuple-element.159.refs_1_, bf16[8,768]{1,0:T(8,128)(2,1)S(1)} %collective-permute-done.4.refs_2_, bf16[512,256]{1,0:T(8,128)(2,1)S(1)} %get-tuple-element.160.refs_3_, ...), custom_call_target="tpu_custom_call" | custom-call | tf_op jit(solution)/shard_map/cond/branch_0_fun/intra/pallas_call | solution.py:430
  29.8 0.0 collective-permute-done.6.refs_5_
  29.8 0.1 collective-permute-done.5.refs_4_
  29.9 0.2 branch_0_fun.23
  30.2 10.0 %all_to_all.29 = bf16[4,128,128]{2,1,0:T(8,128)(2,1)S(1)} all-to-all(bf16[4,128,128]{2,1,0:T(8,128)(2,1)S(1)} %branch_0_fun.23), channel_id=1, replica_groups=mesh['dp'=4,'far'=4,'near'=4,'tensor'=16] {'near'}, dimensions={0} | all-to-all | bytes 262144 | tf_op jit(solution)/shard_map/cond/branch_0_fun/all_to_all | solution.py:418
  40.2 0.9 %gated.1 = bf16[512,256]{1,0:T(8,128)(2,1)} custom-call(f32[512,256]{1,0:T(8,128)S(1)} %get-tuple-element.229.inner, bf16[640,256]{1,0:T(8,128)(2,1)S(1)} %get-tuple-element.230.later, f32[8,256]{1,0:T(8,128)S(1)} %get-tuple-element.227.cum, bf16[512,128]{1,0:T(8,128)(2,1)S(1)} %get-tuple-element.231.state), custom_call_target="tpu_custom_call" | custom-call | tf_op jit(solution)/shard_map/gated/pallas_call | solution.py:498
  (11 shorter events, 0.2 us)
Async XLA Ops:
  3.1 22.1 %collective-permute-start = (bf16[160,128]{1,0:T(8,128)(2,1)S(1)}, bf16[160,128]{1,0:T(8,128)(2,1)S(1)}, u32[]{:S(2)}, u32[]{:S(2)}) collective-permute-start(bf16[160,128]{1,0:T(8,128)(2,1)S(1)} %get-tuple-element.124), channel_id=1, source_target_pairs={{0,64},{16,80},{32,96},{48,112},{1,65},{17,81},{33,97},{49,113},{2... | collective-permute-start | bytes 122888 | tf_op jit(solution)/shard_map/cond/branch_1_fun/ppermute | solution.py:422
  4.4 20.3 %collective-permute-start.1 = (bf16[8,768]{1,0:T(8,128)(2,1)S(1)}, bf16[8,768]{1,0:T(8,128)(2,1)S(1)}, u32[]{:S(2)}, u32[]{:S(2)}) collective-permute-start(bf16[8,768]{1,0:T(8,128)(2,1)S(1)} %branch_1_fun.15), channel_id=1, source_target_pairs={{0,16},{16,32},{32,48},{48,64},{64,80},{80,96},{96,112},{1,17},{17... | collective-permute-start | bytes 36872 | tf_op jit(solution)/shard_map/cond/branch_1_fun/ppermute | solution.py:442
  25.4 4.4 %collective-permute-start.6 = (bf16[160,128]{1,0:T(8,128)(2,1)S(1)}, bf16[160,128]{1,0:T(8,128)(2,1)S(1)}, u32[]{:S(2)}, u32[]{:S(2)}) collective-permute-start(bf16[160,128]{1,0:T(8,128)(2,1)S(1)} %get-tuple-element.177), channel_id=1, source_target_pairs={{64,192},{80,208},{96,224},{112,240},{65,193},{81,209},{97,225},{1... | collective-permute-start | bytes 122888 | tf_op jit(solution)/shard_map/cond/branch_0_fun/ppermute | solution.py:422
  26.7 3.2 %collective-permute-start.5 = (bf16[160,128]{1,0:T(8,128)(2,1)S(1)}, bf16[160,128]{1,0:T(8,128)(2,1)S(1)}, u32[]{:S(2)}, u32[]{:S(2)}) collective-permute-start(bf16[160,128]{1,0:T(8,128)(2,1)S(1)} %get-tuple-element.177), channel_id=1, source_target_pairs={{64,128},{80,144},{96,160},{112,176},{65,129},{81,145},{97,161},{1... | collective-permute-start | bytes 122888 | tf_op jit(solution)/shard_map/cond/branch_0_fun/ppermute | solution.py:422
  28.1 0.8 %collective-permute-start.4 = (bf16[8,768]{1,0:T(8,128)(2,1)S(1)}, bf16[8,768]{1,0:T(8,128)(2,1)S(1)}, u32[]{:S(2)}, u32[]{:S(2)}) collective-permute-start(bf16[8,768]{1,0:T(8,128)(2,1)S(1)} %branch_0_fun.21), channel_id=1, source_target_pairs={{112,128},{113,129},{114,130},{115,131},{116,132},{117,133},{118,1... | collective-permute-start | bytes 36872 | tf_op jit(solution)/shard_map/cond/branch_0_fun/ppermute | solution.py:442

commit v6 on v5

--- a/solution.py
+++ b/solution.py
@@ -96,7 +96,11 @@
     return high, (value - high.astype(F32)).astype(BF16)
 
 
-def state_kernel(x, bc, dt, x_taps, bc_taps, per_head, last, first, pay, xc, bcc, cum_out, less_out):
+def state_kernel(
+    z, x, bc, dt, x_taps, bc_taps, per_head, last, first, pay, xc, bcc, cum_out, less_out, z_out, done
+):
+    fetch = pltpu.make_async_copy(z, z_out, done)
+    fetch.start()
     channels = x.shape[0]
     heads = dt.shape[0]
     width = channels // heads
@@ -147,6 +151,7 @@
         here = slice(quarter * 128, (quarter + 1) * 128)
         rows = jnp.concatenate([tail, edges[:, here], edges[:, channels : channels + 128], gains[:, here]], axis=0)
         pay[quarter, pl.ds(per * width, META), :] = rows.astype(BF16)
+    fetch.wait()
 
 
 def early(series, taps):
@@ -233,14 +238,18 @@
     own = meta[0].astype(F32)
     fresh = kept[0]
     state = jnp.zeros(out.shape[1:], F32)
-    if given:
-        taps, near, next_one, over, between = given
-        (near, rows_near), (next_one, rows_next) = unpack(near[...]), unpack(next_one[...])
+    if len(given) == 2:
+        taps, near = given
+        state, rows = unpack(near[...])
+        fresh = fresh + rim_state(rows, own, taps)
+    elif given:
+        taps, next_one, over, between = given
+        next_one, rows_next = unpack(next_one[...])
         (over, rows_over), (between, rows) = unpack(over[...]), unpack(between[...])
         opening = rim_state(rows_over, rows, taps)
         state = between + spread_rows(rows, 4, per, size) * opening + spread_rows(rows, 0, per, size) * over
-        state = state + near + next_one
-        fresh = fresh + rim_state(rows_near + rows_next + rows, own, taps)
+        state = state + next_one
+        fresh = fresh + rim_state(rows_next + rows, own, taps)
     out[0] = state.astype(BF16)
     for r in range(1, LO):
         state = fresh + spread_rows(meta[r - 1].astype(F32), 0, per, size) * state
@@ -284,11 +293,9 @@
         ref[...] = jnp.zeros(ref.shape, ref.dtype)
 
 
-def intra_kernel(z, *refs, count):
+def intra_kernel(*refs, count):
     rims, refs = refs[:count], refs[count:]
-    xc, bcc, first, x_taps, bc_taps, cum_in, less_in, per_head, out, later, done = refs
-    fetch = pltpu.make_async_copy(z, later.at[pl.ds(bcc.shape[0] // 2, z.shape[0])], done)
-    fetch.start()
+    xc, bcc, first, x_taps, bc_taps, cum_in, less_in, per_head, out, c_out = refs
     heads = cum_in.shape[0]
     channels = xc.shape[0]
     width = channels // heads
@@ -307,7 +314,7 @@
         return jnp.concatenate([jnp.where(lanes < 3, rows, values[:, :128]), values[:, 128:]], axis=1)
 
     both = mended(bcc[...], placed[channels:])
-    later[:states, :] = both[states:]
+    c_out[...] = both[states:]
     gram = dot(both[:states], both[states:], 0, 0)
     keep = lax.broadcasted_iota(jnp.int32, (128, 128), 0) <= lax.broadcasted_iota(jnp.int32, (128, 128), 1)
     for h in range(heads):
@@ -325,22 +332,19 @@
         near = dot(values[:, :128], mix(0, 0, True), 1, 0)
         late = dot(values, jnp.concatenate([mix(0, 128, False), mix(128, 128, True)], axis=0), 1, 0)
         out[at, :] = jnp.concatenate([near, late], axis=1) + skips[h : h + 1] * values.astype(F32)
-    fetch.wait()
-
-
-def output_kernel(inner, later, cum, state, out, held, done):
+
+
+def output_kernel(inner, c_rows, cum, state, z, out, held, done):
     heads = cum.shape[0]
     width = inner.shape[0] // heads
     per = heads // LO
-    states = state.shape[1]
-    c_rows = later[:states, :]
     grown = jnp.exp(cum[...])
     copies = []
     for h in range(heads):
         at = pl.ds(h * width, width)
-        y = inner[at, :] + grown[h : h + 1] * dot(state[at, :], c_rows, 1, 0)
+        y = inner[at, :] + grown[h : h + 1] * dot(state[at, :], c_rows[...], 1, 0)
         y = y.astype(BF16).astype(F32)
-        held[at, :] = (y * silu(later[pl.ds(states + h * width, width), :].astype(F32))).astype(BF16)
+        held[at, :] = (y * silu(z[at, :].astype(F32))).astype(BF16)
         if h % per == per - 1:
             part = pl.ds((h + 1 - per) * width, per * width)
             copies.append(pltpu.make_async_copy(held.at[part], out.at[part], done.at[h // per]))
@@ -401,8 +405,20 @@
         compiler_params=GRANT,
     )(group, member, *[pltpu.with_memory_space_constraint(a, pltpu.HBM) for a in (bc_in, taps, x_in, *small)])
     outs = [shape(LO, quarter + META, states, dtype=BF16), series, pairs]
-    outs += [shape(heads, length), shape(heads, length)]
-    pay, xc, bcc, cum, less = run(state_kernel, outs, x, bc, dt, x_taps, bc_taps, per_head, last, first)
+    outs += [shape(heads, length), shape(heads, length), series]
+    args = [x, bc, dt, x_taps, bc_taps, per_head, last, first]
+    pay, xc, bcc, cum, less, z = pl.pallas_call(
+        state_kernel,
+        out_shape=outs,
+        in_specs=[pl.BlockSpec(memory_space=pl.ANY)] + [VMEM] * len(args),
+        out_specs=[VMEM] * len(outs),
+        scratch_shapes=[pltpu.SemaphoreType.DMA],
+        name="states",
+        compiler_params=GRANT,
+    )(
+        pltpu.with_memory_space_constraint(z_gate, pltpu.HBM),
+        *[pltpu.with_memory_space_constraint(a, pltpu.VMEM) for a in args],
+    )
 
     def gather(*rest, opening=False):
         got = lax.all_to_all(pay, "near", 0, 0, tiled=True)
@@ -426,22 +442,12 @@
 
     def inside(*rims):
         args = [*rims, xc, bcc, first, x_taps, bc_taps, cum, less, per_head]
-        return tuple(
-            pl.pallas_call(
-                lambda *refs: intra_kernel(*refs, count=len(rims)),
-                out_shape=inner_shapes,
-                in_specs=[pl.BlockSpec(memory_space=pl.ANY)] + [VMEM] * len(args),
-                out_specs=[VMEM] * 2,
-                scratch_shapes=[pltpu.SemaphoreType.DMA],
-                name="intra",
-        compiler_params=GRANT,
-            )(pltpu.with_memory_space_constraint(z_gate, pltpu.HBM), *[pltpu.with_memory_space_constraint(a, pltpu.VMEM) for a in args])
-        )
+        return tuple(run(lambda *refs: intra_kernel(*refs, count=len(rims)), inner_shapes, *args))
 
     def shifted(begin, end):
         return lax.ppermute(kept_on(last)[0], cp, [(i, i + 1) for i in range(begin, end)])
 
-    inner_shapes = [shape(channels, length), shape(states + channels, length, dtype=BF16)]
+    inner_shapes = [shape(channels, length), shape(states, length, dtype=BF16)]
 
     packed_rows_count = LO * META + 2 * (quarter + META)
     packed_shapes = [kept_shapes[0], shape(packed_rows_count, states, dtype=BF16)]
@@ -458,8 +464,7 @@
             lambda *kept: gather(block_shape, state_shape),
             *kept,
         )
-        (joined,) = run(lambda *refs: join_kernel(*refs, per=per), [block_shape], near, kept[2], own_taps)
-        packed = run(pack_kernel, packed_shapes, kept[0], begin, kept[1], joined, near)
+        packed = run(pack_kernel, packed_shapes, kept[0], begin, kept[1], kept[2], near)
         return (*packed, *kept_on(rims))
 
     def high_part(*kept):
@@ -467,34 +472,44 @@
         kept = lax.cond(far == 2, lambda *kept: gather(block_shape), lambda *kept: blank(*kept_shapes, block_shape), *kept)
         between = sent(kept[2], 2, 3)
         kept = lax.cond(far == 3, lambda *kept: gather(), kept_on, *kept[:2])
-        return kept_on(*kept, between, rims)
+        return kept_on(*kept, between, rims) + blank(state_shape)
 
     def later_part(kept, packed, rims_low):
-        meta, joined, near = run(unpack_kernel, [kept_shapes[1], block_shape, block_shape], packed)
+        meta, block, near = run(unpack_kernel, [kept_shapes[1], block_shape, block_shape], packed)
+        (joined,) = run(lambda *refs: join_kernel(*refs, per=per), [block_shape], near, block, own_taps)
         over = sent(joined, 1, 3)
         next_one = sent(joined, 1, 2)
         rims_mid = shifted(2 * LO - 1, 2 * LO)
-        *kept, between, rims = lax.cond(
+        *kept, between, rims, state = lax.cond(
             far >= 2,
-            high_part,
-            lambda *kept: kept_on(*kept[:2]) + blank(block_shape) + kept_on(kept[2]),
+            lambda *kept: high_part(*kept),
+            lambda *kept: exchange(*kept, own_taps, near, blanks=(*kept_shapes, block_shape, strip)),
             kept,
             meta,
-            rims_low,
         )
-        inner = inside(rims, rims_mid)
+        inner = inside(rims_low, rims_mid, rims)
         between, *inner = lax.optimization_barrier((between, *inner))
-        (state,) = exchange(*kept_on(*kept), own_taps, near, next_one, over, between)
+        (state,) = lax.cond(
+            far >= 2,
+            lambda state, *given: exchange(*given),
+            lambda state, *given: kept_on(state),
+            state,
+            *kept,
+            own_taps,
+            next_one,
+            over,
+            between,
+        )
         return (state, *inner)
 
     parts = lax.cond(far < 2, low_part, lambda: blank(*packed_shapes, strip))
-    state, inner, later = lax.cond(
+    state, inner, c_rows = lax.cond(
         far == 0,
         lambda kept, packed, rims: tuple(run(begin_kernel, [state_shape], kept)) + inside(rims),
         later_part,
         *parts,
     )
-    inputs = [inner, later, cum, state.reshape(channels, states)]
+    inputs = [inner, c_rows, cum, state.reshape(channels, states), z]
     return pl.pallas_call(
         output_kernel,
         out_shape=jax.ShapeDtypeStruct((channels, length), BF16),

time: 41.4 us -> 39.9 us (0.964)
  blocking collectives: 22 us -> 20.8 us
    all_to_all x1, blocking collectives: 9.99 us -> 8.81 us  [exchange(): return tuple(rest) + (lax.all_to_all(entering, 'near', 0, 0, tiled=True),)]
    pallas_call x14 -> x11, Pallas kernels: 2.49 us -> 1.56 us  [run(): pl.pallas_call(kernel, out_shape=outs, in_specs=[VMEM] * len(args), out_s...]
    pallas_call x1, Pallas kernels: 0.97 us -> 1.7 us  [local(): pl.pallas_call(state_kernel, out_shape=outs, in_specs=[pl.BlockSpec(memor...]
  transfers between devices with their start and end apart: 5 -> 5, of which waited for: 3 -> 2; matrix products, arithmetic and copies ran while one was open for 0% -> 0% of each run, Pallas kernels for 3% -> 3%
where the time goes in v6:
time: 39.9 us; the launch traced here: 39.7 us
  blocking collectives  20.8 us (52%)
  starting transfers between devices  8.82 us (22%)
  Pallas kernels  5.53 us (14%)
  waiting for transfers between devices  4.21 us (11%)
    all_to_all x1, blocking collectives, gather(): got = lax.all_to_all(pay, 'near', 0, 0, tiled=True)  12 us
    all_to_all x1, blocking collectives, exchange(): return tuple(rest) + (lax.all_to_all(entering, 'near', 0, 0, tiled=True),)  8.81 us
    ppermute x2, starting transfers between devices, shifted(): lax.ppermute(kept_on(last)[0], cp, [(i, i + 1) for i in range(begin, end)])  4.94 us
    ppermute x3, starting transfers between devices, sent(): return lax.ppermute(block, cp, route)  3.88 us
    ppermute x2, waiting for transfers between devices, shifted(): lax.ppermute(kept_on(last)[0], cp, [(i, i + 1) for i in range(begin, end)])  3.69 us
    pallas_call x1, Pallas kernels, local(): pl.pallas_call(state_kernel, out_shape=outs, in_specs=[pl.BlockSpec(memor...  1.7 us
    pallas_call x11, Pallas kernels, run(): pl.pallas_call(kernel, out_shape=outs, in_specs=[VMEM] * len(args), out_s...  1.56 us
    pallas_call x1, Pallas kernels, local(): pl.pallas_call(load_kernel, grid_spec=pltpu.PrefetchScalarGridSpec(num_sc...  1.34 us
  transfers between devices with their start and end apart: 5, of which 2 were waited for; matrix products, arithmetic and copies ran while one was open for 0% of the time, Pallas kernels for 3%

profile of v6, /device:TPU:256, one launch (start us, length us, event | category | flops | bytes accessed | tf_op | source)
XLA Modules:
  0.0 39.7 jit_solution(4841053922150698164)
XLA Ops:
  0.0 1.3 %load.1 = (bf16[8,768]{1,0:T(8,128)(2,1)S(1)}, bf16[8,768]{1,0:T(8,128)(2,1)S(1)}, bf16[512,256]{1,0:T(8,128)(2,1)S(1)}, bf16[256,256]{1,0:T(8,128)(2,1)S(1)}, b...) custom-call(s32[1]{0:T(128)} %bitcast.3.group, ...), custom_call_target="tpu_custom_call" | custom-call | tf_op jit(solution)/shard_map/load/pallas_call | solution.py:394
  1.3 1.7 %states.1 = (bf16[4,160,128]{2,1,0:T(8,128)(2,1)S(1)}, bf16[512,256]{1,0:T(8,128)(2,1)S(1)}, bf16[256,256]{1,0:T(8,128)(2,1)S(1)}, f32[8,256]{1,0:T(8,128)S(1)},...) custom-call(bf16[512,256]{1,0:T(8,128)(2,1)} %z.1, bf16[512,256]{1,0:T(8,128)(2,1)S(1)} %get-tuple-element.238.x, ...), custom_call_target="tpu_custom_call" | custom-call | tf_op jit(solution)/shard_map/states/pallas_call | solution.py:410
  3.0 22.2 %conditional.8 = ((f32[4,128,128]{2,1,0:T(8,128)S(1)}, bf16[448,128]{1,0:T(8,128)(2,1)S(1)}, bf16[8,768]{1,0:T(8,128)(2,1)S(1)})) conditional(s32[]{:T(128)} %convert_element_type.21, () %tuple.64, (s32[]{:T(128)}, bf16[4,160,128]{2,1,0:T(8,128)(2,1)S(1)}, f32[2,8,128]{2,1,0:T(8,128)S(1)}, bf16[8,768]{1,0:T(8,128)(2,1)S(1)}) %tuple.65), branch_computations={%region_0.1_spmd, %region_1.6_spmd} | conditional | flops 2 | bytes 868526 | solution.py:505
  3.1 1.3 %collective-permute-start = (bf16[160,128]{1,0:T(8,128)(2,1)S(1)}, bf16[160,128]{1,0:T(8,128)(2,1)S(1)}, u32[]{:S(2)}, u32[]{:S(2)}) collective-permute-start(bf16[160,128]{1,0:T(8,128)(2,1)S(1)} %get-tuple-element.139), channel_id=1, source_target_pairs={{0,64},{16,80},{32,96},{48,112},{1,65},{17,81},{33,97},{49,113},{2... | collective-permute-start | bytes 122888 | tf_op jit(solution)/shard_map/cond/branch_1_fun/ppermute | solution.py:438
  4.4 4.3 %collective-permute-start.1 = (bf16[8,768]{1,0:T(8,128)(2,1)S(1)}, bf16[8,768]{1,0:T(8,128)(2,1)S(1)}, u32[]{:S(2)}, u32[]{:S(2)}) collective-permute-start(bf16[8,768]{1,0:T(8,128)(2,1)S(1)} %branch_1_fun.16), channel_id=1, source_target_pairs={{0,16},{16,32},{32,48},{48,64},{64,80},{80,96},{96,112},{1,17},{17... | collective-permute-start | bytes 36872 | tf_op jit(solution)/shard_map/cond/branch_1_fun/ppermute | solution.py:448
  8.7 12.3 %conditional.1 = ((f32[4,128,128]{2,1,0:T(8,128)S(1)}, bf16[4,32,128]{2,1,0:T(8,128)(2,1)S(1)}, bf16[160,128]{1,0:T(8,128)(2,1)S(1)}, bf16[4,128,128]{2,1,0:T(8,128)(2,1)S(1)})) conditional(s32[]{:T(128)} %convert_element_type.5, (bf16[4,160,128]{2,1,0:T(8,128)(2,1)S(1)}, f32[2,8,128]{2,1,0:T(8,128)S(1)}) %tuple.43, (f32[4,128,128]{2,1,0:T(8,128)S(1)}, ...), branch_computations={%region_4.4_spmd, %region_5.5_spmd} | conditional | bytes 327688 | solution.py:461
  8.7 12.0 %all_to_all.29.refs_0_ = bf16[4,160,128]{2,1,0:T(8,128)(2,1)S(1)} all-to-all(bf16[4,160,128]{2,1,0:T(8,128)(2,1)S(1)} %get-tuple-element.122), channel_id=1, replica_groups=mesh['dp'=4,'far'=4,'near'=4,'tensor'=16] {'near'}, dimensions={0} | all-to-all | bytes 327680 | tf_op jit(solution)/shard_map/cond/branch_1_fun/cond/branch_0_fun/all_to_all | solution.py:424
  20.8 0.2 branch_0_fun.13
  21.0 3.7 %collective-permute-done.1.refs_0_ = bf16[8,768]{1,0:T(8,128)(2,1)S(1)} collective-permute-done((bf16[8,768]{1,0:T(8,128)(2,1)S(1)}, bf16[8,768]{1,0:T(8,128)(2,1)S(1)}, u32[]{:S(2)}, u32[]{:S(2)}) %collective-permute-start.1) | collective-permute-done | bytes 12320 | tf_op jit(solution)/shard_map/cond/branch_1_fun/ppermute | solution.py:448
  24.7 0.5 %collective-permute-done.near = bf16[160,128]{1,0:T(8,128)(2,1)S(1)} collective-permute-done((bf16[160,128]{1,0:T(8,128)(2,1)S(1)}, bf16[160,128]{1,0:T(8,128)(2,1)S(1)}, u32[]{:S(2)}, u32[]{:S(2)}) %collective-permute-start) | collective-permute-done | bytes 40992 | tf_op jit(solution)/shard_map/cond/branch_1_fun/ppermute | solution.py:438
  25.3 13.5 %conditional.9 = (f32[512,256]{1,0:T(8,128)S(1)}, bf16[128,256]{1,0:T(8,128)(2,1)S(1)}, bf16[512,128]{1,0:T(8,128)(2,1)S(1)}) conditional(s32[]{:T(128)} %convert_element_type.20, (s32[]{:T(128)}, bf16[448,128]{1,0:T(8,128)(2,1)S(1)}, f32[4,128,128]{2,1,0:T(8,128)S(1)}, f32[2,8,128]{2,1,0:T(8,128)S(1)}, bf16[4,160,128]{2,1,0:T(8,128)(2,1)S(1)}, ...), branch_computations={%region_6.15_spmd, %region_15.16_spmd} | conditional | flops 6 | bytes 1507802 | solution.py:506
  25.3 0.2 branch_0_fun.19
  25.5 1.3 %collective-permute-start.5 = (bf16[160,128]{1,0:T(8,128)(2,1)S(1)}, bf16[160,128]{1,0:T(8,128)(2,1)S(1)}, u32[]{:S(2)}, u32[]{:S(2)}) collective-permute-start(bf16[160,128]{1,0:T(8,128)(2,1)S(1)} %branch_0_fun.19), channel_id=1, source_target_pairs={{64,192},{80,208},{96,224},{112,240},{65,193},{81,209},{97,225},{1... | collective-permute-start | bytes 122888 | tf_op jit(solution)/shard_map/cond/branch_0_fun/ppermute | solution.py:438
  26.8 1.3 %collective-permute-start.4 = (bf16[160,128]{1,0:T(8,128)(2,1)S(1)}, bf16[160,128]{1,0:T(8,128)(2,1)S(1)}, u32[]{:S(2)}, u32[]{:S(2)}) collective-permute-start(bf16[160,128]{1,0:T(8,128)(2,1)S(1)} %branch_0_fun.19), channel_id=1, source_target_pairs={{64,128},{80,144},{96,160},{112,176},{65,129},{81,145},{97,161},{1... | collective-permute-start | bytes 122888 | tf_op jit(solution)/shard_map/cond/branch_0_fun/ppermute | solution.py:438
  28.1 0.7 %collective-permute-start.6 = (bf16[8,768]{1,0:T(8,128)(2,1)S(1)}, bf16[8,768]{1,0:T(8,128)(2,1)S(1)}, u32[]{:S(2)}, u32[]{:S(2)}) collective-permute-start(bf16[8,768]{1,0:T(8,128)(2,1)S(1)} %branch_0_fun.20), channel_id=1, source_target_pairs={{112,128},{113,129},{114,130},{115,131},{116,132},{117,133},{118,1... | collective-permute-start | bytes 36872 | tf_op jit(solution)/shard_map/cond/branch_0_fun/ppermute | solution.py:448
  28.8 9.0 %conditional.4 = (f32[4,128,128]{2,1,0:T(8,128)S(1)}, bf16[4,32,128]{2,1,0:T(8,128)(2,1)S(1)}, bf16[160,128]{1,0:T(8,128)(2,1)S(1)}, bf16[8,768]{1,0:T(8,128)(2,1)S(1)}, bf16[4,128,128]{2,1,0:T(8,128)(2,1)S(1)}) conditional(s32[]{:T(128)} %convert_element_type.17, (f32[4,128,128]{2,1,0:T(8,128)S(1)}, bf16[4,32,128]{2,1,0:T(8,128)(2,1)S(1)}, ...), branch_computations={%region_7.7_spmd, %region_8.12_spmd} | conditional | flops 4 | bytes 868548 | solution.py:483
  28.8 0.2 branch_0_fun.14
  29.0 8.8 %all_to_all.31 = bf16[4,128,128]{2,1,0:T(8,128)(2,1)S(1)} all-to-all(bf16[4,128,128]{2,1,0:T(8,128)(2,1)S(1)} %get-tuple-element.151), channel_id=1, replica_groups=mesh['dp'=4,'far'=4,'near'=4,'tensor'=16] {'near'}, dimensions={0} | all-to-all | bytes 262144 | tf_op jit(solution)/shard_map/cond/branch_0_fun/cond/branch_0_fun/all_to_all | solution.py:434
  37.8 0.0 collective-permute-done.6.refs_1_
  37.8 0.8 %branch_0_fun.21 = (f32[512,256]{1,0:T(8,128)S(1)}, bf16[128,256]{1,0:T(8,128)(2,1)S(1)}) custom-call(bf16[8,768]{1,0:T(8,128)(2,1)S(1)} %get-tuple-element.190.refs_0_, bf16[8,768]{1,0:T(8,128)(2,1)S(1)} %collective-permute-done.6.refs_1_, bf16[8,768]{1,0:T(8,128)(2,1)S(1)} %get-tuple-element.191.refs_2_, bf16[512,256]{1,0:T(8,128)(2,1)S(1)} %get-tuple-element.192.refs_3_, ...), custom_call_target="tpu_custom_call" | custom-call | tf_op jit(solution)/shard_map/cond/branch_0_fun/pallas_call | solution.py:366
  38.6 0.0 collective-permute-done.5
  38.7 0.0 collective-permute-done.4
  38.7 0.9 %gated.1 = bf16[512,256]{1,0:T(8,128)(2,1)} custom-call(f32[512,256]{1,0:T(8,128)S(1)} %get-tuple-element.255.inner, bf16[128,256]{1,0:T(8,128)(2,1)S(1)} %get-tuple-element.256.c_rows, f32[8,256]{1,0:T(8,128)S(1)} %get-tuple-element.253.cum, bf16[512,128]{1,0:T(8,128)(2,1)S(1)} %get-tuple-element.259.state, bf16[512,256]{1,0:T(8,128)(2,1)S(1)} %get-tuple-element.258.z), custom_call_target="tpu_custom_call" | custom-call | tf_op jit(solution)/shard_map/gated/pallas_call | solution.py:513
  (9 shorter events, 0.2 us)
Async XLA Ops:
  3.1 22.1 %collective-permute-start = (bf16[160,128]{1,0:T(8,128)(2,1)S(1)}, bf16[160,128]{1,0:T(8,128)(2,1)S(1)}, u32[]{:S(2)}, u32[]{:S(2)}) collective-permute-start(bf16[160,128]{1,0:T(8,128)(2,1)S(1)} %get-tuple-element.139), channel_id=1, source_target_pairs={{0,64},{16,80},{32,96},{48,112},{1,65},{17,81},{33,97},{49,113},{2... | collective-permute-start | bytes 122888 | tf_op jit(solution)/shard_map/cond/branch_1_fun/ppermute | solution.py:438
  4.4 20.3 %collective-permute-start.1 = (bf16[8,768]{1,0:T(8,128)(2,1)S(1)}, bf16[8,768]{1,0:T(8,128)(2,1)S(1)}, u32[]{:S(2)}, u32[]{:S(2)}) collective-permute-start(bf16[8,768]{1,0:T(8,128)(2,1)S(1)} %branch_1_fun.16), channel_id=1, source_target_pairs={{0,16},{16,32},{32,48},{48,64},{64,80},{80,96},{96,112},{1,17},{17... | collective-permute-start | bytes 36872 | tf_op jit(solution)/shard_map/cond/branch_1_fun/ppermute | solution.py:448
  25.5 13.2 %collective-permute-start.5 = (bf16[160,128]{1,0:T(8,128)(2,1)S(1)}, bf16[160,128]{1,0:T(8,128)(2,1)S(1)}, u32[]{:S(2)}, u32[]{:S(2)}) collective-permute-start(bf16[160,128]{1,0:T(8,128)(2,1)S(1)} %branch_0_fun.19), channel_id=1, source_target_pairs={{64,192},{80,208},{96,224},{112,240},{65,193},{81,209},{97,225},{1... | collective-permute-start | bytes 122888 | tf_op jit(solution)/shard_map/cond/branch_0_fun/ppermute | solution.py:438
  26.8 11.9 %collective-permute-start.4 = (bf16[160,128]{1,0:T(8,128)(2,1)S(1)}, bf16[160,128]{1,0:T(8,128)(2,1)S(1)}, u32[]{:S(2)}, u32[]{:S(2)}) collective-permute-start(bf16[160,128]{1,0:T(8,128)(2,1)S(1)} %branch_0_fun.19), channel_id=1, source_target_pairs={{64,128},{80,144},{96,160},{112,176},{65,129},{81,145},{97,161},{1... | collective-permute-start | bytes 122888 | tf_op jit(solution)/shard_map/cond/branch_0_fun/ppermute | solution.py:438
  28.1 9.7 %collective-permute-start.6 = (bf16[8,768]{1,0:T(8,128)(2,1)S(1)}, bf16[8,768]{1,0:T(8,128)(2,1)S(1)}, u32[]{:S(2)}, u32[]{:S(2)}) collective-permute-start(bf16[8,768]{1,0:T(8,128)(2,1)S(1)} %branch_0_fun.20), channel_id=1, source_target_pairs={{112,128},{113,129},{114,130},{115,131},{116,132},{117,133},{118,1... | collective-permute-start | bytes 36872 | tf_op jit(solution)/shard_map/cond/branch_0_fun/ppermute | solution.py:448

commit v7 on v6

--- a/solution.py
+++ b/solution.py
@@ -70,14 +70,20 @@
 def filtered(series, taps):
     lanes = lax.broadcasted_iota(jnp.int32, (series.shape[0], 128), 1)
     first, second = series[:, :128].astype(F32), series[:, 128:].astype(F32)
-    a = taps[:, 4:5] + taps[:, 3:4] * first
-    b = taps[:, 4:5] + taps[:, 3:4] * second
+    wide = [taps[:, k * 128 : (k + 1) * 128] for k in range(5)]
+    a = wide[4] + wide[3] * first
+    b = wide[4] + wide[3] * second
     for back in (1, 2, 3):
         moved = pltpu.roll(first, back, 1)
-        tap = taps[:, 3 - back : 4 - back]
-        a = a + tap * moved
-        b = b + tap * jnp.where(lanes < back, moved, pltpu.roll(second, back, 1))
-    return jnp.concatenate([silu(a), silu(b)], axis=1).astype(BF16)
+        a = a + wide[3 - back] * moved
+        b = b + wide[3 - back] * jnp.where(lanes < back, moved, pltpu.roll(second, back, 1))
+    return jnp.concatenate([silu(a), silu(b)], axis=1)
+
+
+def thirds(value):
+    high = value.astype(BF16).astype(F32)
+    mid = (value - high).astype(BF16).astype(F32)
+    return jnp.concatenate([high, mid, value - high - mid], axis=0).astype(BF16)
 
 
 def column(row):
@@ -97,7 +103,7 @@
 
 
 def state_kernel(
-    z, x, bc, dt, x_taps, bc_taps, per_head, last, first, pay, xc, bcc, cum_out, less_out, z_out, done
+    z, x, bc, dt, x_taps, bc_taps, per_head, last, first, pay, xc, bcc, cum_out, less_out, z_out, done, weighted, cols
 ):
     fetch = pltpu.make_async_copy(z, z_out, done)
     fetch.start()
@@ -108,14 +114,12 @@
 
     delta = softplus(dt[...].astype(F32) + per_head[0][:, :1])
     scaled = delta * -jnp.exp(per_head[1][:, :1])
-    high = scaled.astype(BF16).astype(F32)
-    mid = (scaled - high).astype(BF16).astype(F32)
     size = scaled.shape[1]
     upto = jnp.where(
         lax.broadcasted_iota(jnp.int32, (size, size), 0) <= lax.broadcasted_iota(jnp.int32, (size, size), 1), 1.0, 0.0
     ).astype(BF16)
-    sums = dot(jnp.concatenate([scaled - high - mid, mid, high], axis=0).astype(BF16), upto, 1, 0)
-    cum = sums[:heads] + sums[heads : 2 * heads] + sums[2 * heads :]
+    sums = dot(thirds(scaled), upto, 1, 0)
+    cum = sums[2 * heads :] + sums[heads : 2 * heads] + sums[:heads]
     cum_out[...] = cum
     less_out[...] = cum - jnp.log(delta)
     end = cum[:, size - 1 :]
@@ -131,9 +135,12 @@
     lines = lax.broadcasted_iota(jnp.int32, last.shape, 0)
     edges = jnp.where(lines < 3, last[...].astype(F32), pltpu.roll(first[...].astype(F32), 3, 0))
 
-    bcc[...] = filtered(bc[...], bc_taps[...].T)
-    b_rows = bcc[:states, :]
-    x_cols = x_taps[...].T
+    kinds = lax.broadcasted_iota(jnp.int32, (24, 5 * 128), 1) // 128
+    picked = jnp.where(lax.broadcasted_iota(jnp.int32, (24, 5 * 128), 0) % 8 == kinds, 1.0, 0.0).astype(BF16)
+    cols[...] = dot(thirds(jnp.concatenate([x_taps[...], bc_taps[...]], axis=1)), picked, 0, 0)
+    for start in range(0, 2 * states, width):
+        at = pl.ds(start, width)
+        bcc[at, :] = filtered(bc[at, :], cols[pl.ds(channels + start, width), :]).astype(BF16)
     late = jnp.where(lax.broadcasted_iota(jnp.int32, gain.shape, 1) < 3, 0.0, gain)
     lines = lax.broadcasted_iota(jnp.int32, (8, 128), 0)
     per = heads // LO
@@ -142,15 +149,18 @@
         for j in range(per):
             h = quarter * per + j
             at = pl.ds(h * width, width)
-            values = filtered(x[at, :], x_cols[h * width : (h + 1) * width])
-            xc[at, :] = values
-            weighted = (values.astype(F32) * late[h : h + 1]).astype(BF16)
-            pay[quarter, pl.ds(j * width, width), :] = dot(weighted, b_rows, 1, 1).astype(BF16)
+            values = filtered(x[at, :], cols[at, :])
+            xc[at, :] = values.astype(BF16)
+            weighted[at, :] = (values * late[h : h + 1]).astype(BF16)
             tail = jnp.where(lines == 2 * j, total_high[h : h + 1], tail)
             tail = jnp.where(lines == 2 * j + 1, total_low[h : h + 1], tail)
         here = slice(quarter * 128, (quarter + 1) * 128)
         rows = jnp.concatenate([tail, edges[:, here], edges[:, channels : channels + 128], gains[:, here]], axis=0)
         pay[quarter, pl.ds(per * width, META), :] = rows.astype(BF16)
+    fresh = dot(weighted[...], bcc[:states, :], 1, 1).astype(BF16)
+    for quarter in range(LO):
+        size = per * width
+        pay[quarter, pl.ds(0, size), :] = fresh[quarter * size : (quarter + 1) * size]
     fetch.wait()
 
 
@@ -284,8 +294,9 @@
         at += block.shape[0]
 
 
-def begin_kernel(kept, state):
+def begin_kernel(kept, unused, state, *blanks):
     state[...] = kept[...].astype(BF16)
+    blank_kernel(*blanks)
 
 
 def blank_kernel(*refs):
@@ -293,33 +304,20 @@
         ref[...] = jnp.zeros(ref.shape, ref.dtype)
 
 
-def intra_kernel(*refs, count):
-    rims, refs = refs[:count], refs[count:]
-    xc, bcc, first, x_taps, bc_taps, cum_in, less_in, per_head, out, c_out = refs
+def intra_kernel(xc, bcc, cum_in, less_in, per_head, out):
     heads = cum_in.shape[0]
-    channels = xc.shape[0]
-    width = channels // heads
+    width = xc.shape[0] // heads
     states = bcc.shape[0] // 2
     cum, less = cum_in[...], less_in[...]
     less_cols = jnp.concatenate([less[:, :128].T, less[:, 128:].T], axis=0)
     skips = per_head[2][:, :1]
-    lines = lax.broadcasted_iota(jnp.int32, first.shape, 0)
-    given = sum(r[...].astype(F32) for r in rims)
-    edges = jnp.where(lines < 3, given, pltpu.roll(first[...].astype(F32), 3, 0))
-    begun = [early(edges[:, :channels], x_taps[...]), early(edges[:, channels:], bc_taps[...])]
-    placed = dot(jnp.concatenate(begun, axis=1), picks(0), 0, 0).astype(BF16)
-
-    def mended(values, rows):
-        lanes = lax.broadcasted_iota(jnp.int32, rows.shape, 1)
-        return jnp.concatenate([jnp.where(lanes < 3, rows, values[:, :128]), values[:, 128:]], axis=1)
-
-    both = mended(bcc[...], placed[channels:])
-    c_out[...] = both[states:]
-    gram = dot(both[:states], both[states:], 0, 0)
+    gram = dot(bcc[:states, :], bcc[states:, :], 0, 0)
+    gram = jnp.where(lax.broadcasted_iota(jnp.int32, gram.shape, 0) < 3, 0.0, gram)
     keep = lax.broadcasted_iota(jnp.int32, (128, 128), 0) <= lax.broadcasted_iota(jnp.int32, (128, 128), 1)
+    lanes = lax.broadcasted_iota(jnp.int32, (width, 256), 1)
     for h in range(heads):
         at = pl.ds(h * width, width)
-        values = mended(xc[at, :], placed[h * width : (h + 1) * width])
+        values = xc[at, :]
         row = cum[h : h + 1]
         col = less_cols[:, h : h + 1]
 
@@ -331,18 +329,43 @@
 
         near = dot(values[:, :128], mix(0, 0, True), 1, 0)
         late = dot(values, jnp.concatenate([mix(0, 128, False), mix(128, 128, True)], axis=0), 1, 0)
-        out[at, :] = jnp.concatenate([near, late], axis=1) + skips[h : h + 1] * values.astype(F32)
-
-
-def output_kernel(inner, c_rows, cum, state, z, out, held, done):
-    heads = cum.shape[0]
-    width = inner.shape[0] // heads
+        kept = jnp.where(lanes < 3, 0.0, values.astype(F32))
+        out[at, :] = jnp.concatenate([near, late], axis=1) + skips[h : h + 1] * kept
+
+
+def output_kernel(
+    low, high, bcc, rims_low, rims_mid, rims_high, first, x_taps, bc_taps, cum_in, less, per_head, state, z, out, held, done
+):
+    heads = cum_in.shape[0]
+    channels = low.shape[0]
+    width = channels // heads
+    states = state.shape[1]
     per = heads // LO
-    grown = jnp.exp(cum[...])
+    lines = lax.broadcasted_iota(jnp.int32, first.shape, 0)
+    given = rims_low[...].astype(F32) + rims_mid[...].astype(F32) + rims_high[...].astype(F32)
+    edges = jnp.where(lines < 3, given, pltpu.roll(first[...].astype(F32), 3, 0))
+    x_rows = early(edges[:, :channels], x_taps[...])
+    bc_rows = early(edges[:, channels:], bc_taps[...])
+    x_placed = dot(x_rows, picks(0), 0, 0)
+    c_placed = dot(bc_rows[:, states:], picks(0), 0, 0).astype(BF16)
+    lanes = lax.broadcasted_iota(jnp.int32, c_placed.shape, 1)
+    c_rows = bcc[states:, :]
+    c_rows = jnp.concatenate([jnp.where(lanes < 3, c_placed, c_rows[:, :128]), c_rows[:, 128:]], axis=1)
+    gram = dot(bc_rows[:, :states], c_rows, 1, 0)
+    cum = cum_in[...]
+    grown = jnp.exp(cum)
+    less_cols = less[:, :128].T[:8]
+    keep = lax.broadcasted_iota(jnp.int32, gram.shape, 0) <= lax.broadcasted_iota(jnp.int32, gram.shape, 1)
+    skips = per_head[2][:, :1]
     copies = []
     for h in range(heads):
         at = pl.ds(h * width, width)
-        y = inner[at, :] + grown[h : h + 1] * dot(state[at, :], c_rows[...], 1, 0)
+        spread = jnp.where(keep, cum[h : h + 1] - less_cols[:, h : h + 1], -1e30)
+        mixing = (gram * jnp.exp(spread)).astype(BF16)
+        opening = dot(x_rows[:, h * width : (h + 1) * width], mixing, 0, 0)
+        skipped = skips[h : h + 1] * x_placed[h * width : (h + 1) * width]
+        y = low[at, :] + high[at, :] + opening + grown[h : h + 1] * dot(state[at, :], c_rows, 1, 0)
+        y = jnp.concatenate([y[:, :128] + skipped, y[:, 128:]], axis=1)
         y = y.astype(BF16).astype(F32)
         held[at, :] = (y * silu(z[at, :].astype(F32))).astype(BF16)
         if h % per == per - 1:
@@ -412,7 +435,11 @@
         out_shape=outs,
         in_specs=[pl.BlockSpec(memory_space=pl.ANY)] + [VMEM] * len(args),
         out_specs=[VMEM] * len(outs),
-        scratch_shapes=[pltpu.SemaphoreType.DMA],
+        scratch_shapes=[
+            pltpu.SemaphoreType.DMA,
+            pltpu.VMEM((channels, length), BF16),
+            pltpu.VMEM((channels + rows, 5 * 128), F32),
+        ],
         name="states",
         compiler_params=GRANT,
     )(
@@ -440,14 +467,14 @@
     def kept_on(*arrays):
         return tuple(run(copy_kernel, [shape(*a.shape, dtype=a.dtype) for a in arrays], *arrays))
 
-    def inside(*rims):
-        args = [*rims, xc, bcc, first, x_taps, bc_taps, cum, less, per_head]
-        return tuple(run(lambda *refs: intra_kernel(*refs, count=len(rims)), inner_shapes, *args))
+    def inside(after):
+        _, values = lax.optimization_barrier((after, xc))
+        return run(intra_kernel, [inner_shape], values, bcc, cum, less, per_head)[0]
 
     def shifted(begin, end):
         return lax.ppermute(kept_on(last)[0], cp, [(i, i + 1) for i in range(begin, end)])
 
-    inner_shapes = [shape(channels, length), shape(states, length, dtype=BF16)]
+    inner_shape = shape(channels, length)
 
     packed_rows_count = LO * META + 2 * (quarter + META)
     packed_shapes = [kept_shapes[0], shape(packed_rows_count, states, dtype=BF16)]
@@ -464,31 +491,31 @@
             lambda *kept: gather(block_shape, state_shape),
             *kept,
         )
+        inner = inside(begin)
         packed = run(pack_kernel, packed_shapes, kept[0], begin, kept[1], kept[2], near)
-        return (*packed, *kept_on(rims))
+        return (*packed, *kept_on(rims), inner)
 
     def high_part(*kept):
         rims = shifted(2 * LO, count - 1)
         kept = lax.cond(far == 2, lambda *kept: gather(block_shape), lambda *kept: blank(*kept_shapes, block_shape), *kept)
         between = sent(kept[2], 2, 3)
         kept = lax.cond(far == 3, lambda *kept: gather(), kept_on, *kept[:2])
-        return kept_on(*kept, between, rims) + blank(state_shape)
-
-    def later_part(kept, packed, rims_low):
+        inner = inside(kept[0])
+        return kept_on(*kept, between, rims) + (inner,) + blank(state_shape)
+
+    def later_part(kept, packed):
         meta, block, near = run(unpack_kernel, [kept_shapes[1], block_shape, block_shape], packed)
         (joined,) = run(lambda *refs: join_kernel(*refs, per=per), [block_shape], near, block, own_taps)
         over = sent(joined, 1, 3)
         next_one = sent(joined, 1, 2)
         rims_mid = shifted(2 * LO - 1, 2 * LO)
-        *kept, between, rims, state = lax.cond(
+        *kept, between, rims, inner, state = lax.cond(
             far >= 2,
-            lambda *kept: high_part(*kept),
-            lambda *kept: exchange(*kept, own_taps, near, blanks=(*kept_shapes, block_shape, strip)),
+            high_part,
+            lambda *kept: exchange(*kept, own_taps, near, blanks=(*kept_shapes, block_shape, strip, inner_shape)),
             kept,
             meta,
         )
-        inner = inside(rims_low, rims_mid, rims)
-        between, *inner = lax.optimization_barrier((between, *inner))
         (state,) = lax.cond(
             far >= 2,
             lambda state, *given: exchange(*given),
@@ -500,16 +527,18 @@
             over,
             between,
         )
-        return (state, *inner)
-
-    parts = lax.cond(far < 2, low_part, lambda: blank(*packed_shapes, strip))
-    state, inner, c_rows = lax.cond(
+        return (state, inner, rims_mid, rims)
+
+    kept, packed, rims_low, inner_low = lax.cond(far < 2, low_part, lambda: blank(*packed_shapes, strip, inner_shape))
+    state, inner, rims_mid, rims = lax.cond(
         far == 0,
-        lambda kept, packed, rims: tuple(run(begin_kernel, [state_shape], kept)) + inside(rims),
+        lambda kept, packed: tuple(run(begin_kernel, [state_shape, inner_shape, strip, strip], kept, packed)),
         later_part,
-        *parts,
+        kept,
+        packed,
     )
-    inputs = [inner, c_rows, cum, state.reshape(channels, states), z]
+    inputs = [inner_low, inner, bcc, rims_low, rims_mid, rims, first, x_taps, bc_taps, cum, less, per_head]
+    inputs += [state.reshape(channels, states), z]
     return pl.pallas_call(
         output_kernel,
         out_shape=jax.ShapeDtypeStruct((channels, length), BF16),

time: 39.9 us -> 39.1 us (0.980)
  waiting for transfers between devices: 4.21 us -> 3.5 us
    ppermute x2, waiting for transfers between devices: 3.69 us -> 2.98 us  [shifted(): lax.ppermute(kept_on(last)[0], cp, [(i, i + 1) for i in range(begin, end)])]
    pallas_call x1, Pallas kernels: 0.94 us -> 1.35 us  [local(): pl.pallas_call(output_kernel, out_shape=jax.ShapeDtypeStruct((channels, l...]
where the time goes in v7:
time: 39.1 us; the launch traced here: 38.8 us
  blocking collectives  20.8 us (53%)
  starting transfers between devices  8.82 us (23%)
  Pallas kernels  5.51 us (14%)
  waiting for transfers between devices  3.5 us (9%)
    all_to_all x1, blocking collectives, gather(): got = lax.all_to_all(pay, 'near', 0, 0, tiled=True)  12 us
    all_to_all x1, blocking collectives, exchange(): return tuple(rest) + (lax.all_to_all(entering, 'near', 0, 0, tiled=True),)  8.76 us
    ppermute x2, starting transfers between devices, shifted(): lax.ppermute(kept_on(last)[0], cp, [(i, i + 1) for i in range(begin, end)])  4.94 us
    ppermute x3, starting transfers between devices, sent(): return lax.ppermute(block, cp, route)  3.88 us
    ppermute x2, waiting for transfers between devices, shifted(): lax.ppermute(kept_on(last)[0], cp, [(i, i + 1) for i in range(begin, end)])  2.98 us
    pallas_call x11, Pallas kernels, run(): pl.pallas_call(kernel, out_shape=outs, in_specs=[VMEM] * len(args), out_s...  1.46 us
    pallas_call x1, Pallas kernels, local(): pl.pallas_call(state_kernel, out_shape=outs, in_specs=[pl.BlockSpec(memor...  1.36 us
    pallas_call x1, Pallas kernels, local(): pl.pallas_call(output_kernel, out_shape=jax.ShapeDtypeStruct((channels, l...  1.35 us
  transfers between devices with their start and end apart: 5, of which 2 were waited for; matrix products, arithmetic and copies ran while one was open for 0% of the time, Pallas kernels for 3%

profile of v7, /device:TPU:256, one launch (start us, length us, event | category | flops | bytes accessed | tf_op | source)
XLA Modules:
  0.0 38.8 jit_solution(1738992959915751413)
XLA Ops:
  0.0 1.3 %load.1 = (bf16[8,768]{1,0:T(8,128)(2,1)S(1)}, bf16[8,768]{1,0:T(8,128)(2,1)S(1)}, bf16[512,256]{1,0:T(8,128)(2,1)S(1)}, bf16[256,256]{1,0:T(8,128)(2,1)S(1)}, b...) custom-call(s32[1]{0:T(128)} %bitcast.3.group, ...), custom_call_target="tpu_custom_call" | custom-call | tf_op jit(solution)/shard_map/load/pallas_call | solution.py:417
  1.3 1.4 %states.1 = (bf16[4,160,128]{2,1,0:T(8,128)(2,1)S(1)}, bf16[512,256]{1,0:T(8,128)(2,1)S(1)}, bf16[256,256]{1,0:T(8,128)(2,1)S(1)}, f32[8,256]{1,0:T(8,128)S(1)},...) custom-call(bf16[512,256]{1,0:T(8,128)(2,1)} %z.1, bf16[512,256]{1,0:T(8,128)(2,1)S(1)} %get-tuple-element.231.x, ...), custom_call_target="tpu_custom_call" | custom-call | tf_op jit(solution)/shard_map/states/pallas_call | solution.py:433
  2.7 22.2 %conditional.8 = ((f32[4,128,128]{2,1,0:T(8,128)S(1)}, bf16[448,128]{1,0:T(8,128)(2,1)S(1)}, bf16[8,768]{1,0:T(8,128)(2,1)S(1)}, f32[512,256]{1,0:T(8,128)S(1)})) conditional(s32[]{:T(128)} %convert_element_type.20, () %tuple.64, (s32[]{:T(128)}, bf16[4,160,128]{2,1,0:T(8,128)(2,1)S(1)}, f32[2,8,128]{2,1,0:T(8,128)S(1)}, ...), branch_computations={%region_0.1_spmd, %region_1.6_spmd} | conditional | flops 2 | bytes 868534 | solution.py:532
  2.8 1.3 %collective-permute-start = (bf16[160,128]{1,0:T(8,128)(2,1)S(1)}, bf16[160,128]{1,0:T(8,128)(2,1)S(1)}, u32[]{:S(2)}, u32[]{:S(2)}) collective-permute-start(bf16[160,128]{1,0:T(8,128)(2,1)S(1)} %get-tuple-element.135), channel_id=1, source_target_pairs={{0,64},{16,80},{32,96},{48,112},{1,65},{17,81},{33,97},{49,113},{2... | collective-permute-start | bytes 122888 | tf_op jit(solution)/shard_map/cond/branch_1_fun/ppermute | solution.py:465
  4.1 4.3 %collective-permute-start.1 = (bf16[8,768]{1,0:T(8,128)(2,1)S(1)}, bf16[8,768]{1,0:T(8,128)(2,1)S(1)}, u32[]{:S(2)}, u32[]{:S(2)}) collective-permute-start(bf16[8,768]{1,0:T(8,128)(2,1)S(1)} %branch_1_fun.17), channel_id=1, source_target_pairs={{0,16},{16,32},{32,48},{48,64},{64,80},{80,96},{96,112},{1,17},{17... | collective-permute-start | bytes 36872 | tf_op jit(solution)/shard_map/cond/branch_1_fun/ppermute | solution.py:475
  8.4 12.3 %conditional.1 = ((f32[4,128,128]{2,1,0:T(8,128)S(1)}, bf16[4,32,128]{2,1,0:T(8,128)(2,1)S(1)}, bf16[160,128]{1,0:T(8,128)(2,1)S(1)}, bf16[4,128,128]{2,1,0:T(8,128)(2,1)S(1)})) conditional(s32[]{:T(128)} %convert_element_type.5, (bf16[4,160,128]{2,1,0:T(8,128)(2,1)S(1)}, f32[2,8,128]{2,1,0:T(8,128)S(1)}) %tuple.43, (f32[4,128,128]{2,1,0:T(8,128)S(1)}, ...), branch_computations={%region_4.4_spmd, %region_5.5_spmd} | conditional | bytes 327688 | solution.py:488
  8.4 12.0 %all_to_all.29.refs_0_ = bf16[4,160,128]{2,1,0:T(8,128)(2,1)S(1)} all-to-all(bf16[4,160,128]{2,1,0:T(8,128)(2,1)S(1)} %get-tuple-element.118), channel_id=1, replica_groups=mesh['dp'=4,'far'=4,'near'=4,'tensor'=16] {'near'}, dimensions={0} | all-to-all | bytes 327680 | tf_op jit(solution)/shard_map/cond/branch_1_fun/cond/branch_0_fun/all_to_all | solution.py:451
  20.4 0.2 branch_0_fun.12
  20.7 0.7 %branch_1_fun.19 = f32[512,256]{1,0:T(8,128)S(1)} custom-call(bf16[512,256]{1,0:T(8,128)(2,1)S(1)} %get-tuple-element.140.xc, bf16[256,256]{1,0:T(8,128)(2,1)S(1)} %get-tuple-element.141.bcc, f32[8,256]{1,0:T(8,128)S(1)} %get-tuple-element.142.cum_in, f32[8,256]{1,0:T(8,128)S(1)} %get-tuple-element.143.less_in, f32[3,8,128]{2,1,0:T(8,128)S(1)} %get-tuple-element.144.per_head), custom_call_target="tpu_custom_call" | custom-call | tf_op jit(solution)/shard_map/cond/branch_1_fun/pallas_call | solution.py:389
  21.4 3.0 %collective-permute-done.1.refs_0_ = bf16[8,768]{1,0:T(8,128)(2,1)S(1)} collective-permute-done((bf16[8,768]{1,0:T(8,128)(2,1)S(1)}, bf16[8,768]{1,0:T(8,128)(2,1)S(1)}, u32[]{:S(2)}, u32[]{:S(2)}) %collective-permute-start.1) | collective-permute-done | bytes 12320 | tf_op jit(solution)/shard_map/cond/branch_1_fun/ppermute | solution.py:475
  24.4 0.5 %collective-permute-done.near = bf16[160,128]{1,0:T(8,128)(2,1)S(1)} collective-permute-done((bf16[160,128]{1,0:T(8,128)(2,1)S(1)}, bf16[160,128]{1,0:T(8,128)(2,1)S(1)}, u32[]{:S(2)}, u32[]{:S(2)}) %collective-permute-start) | collective-permute-done | bytes 40992 | tf_op jit(solution)/shard_map/cond/branch_1_fun/ppermute | solution.py:465
  24.9 12.6 %conditional.9 = (f32[512,256]{1,0:T(8,128)S(1)}, bf16[8,768]{1,0:T(8,128)(2,1)S(1)}, bf16[8,768]{1,0:T(8,128)(2,1)S(1)}, bf16[512,128]{1,0:T(8,128)(2,1)S(1)}) conditional(s32[]{:T(128)} %convert_element_type.21, (s32[]{:T(128)}, bf16[448,128]{1,0:T(8,128)(2,1)S(1)}, f32[4,128,128]{2,1,0:T(8,128)S(1)}, f32[2,8,128]{2,1,0:T(8,128)S(1)}, ...), branch_computations={%region_6.15_spmd, %region_15.16_spmd} | conditional | flops 6 | bytes 1507858 | solution.py:533
  24.9 0.2 branch_0_fun.18
  25.2 1.3 %collective-permute-start.4 = (bf16[160,128]{1,0:T(8,128)(2,1)S(1)}, bf16[160,128]{1,0:T(8,128)(2,1)S(1)}, u32[]{:S(2)}, u32[]{:S(2)}) collective-permute-start(bf16[160,128]{1,0:T(8,128)(2,1)S(1)} %branch_0_fun.18), channel_id=1, source_target_pairs={{64,128},{80,144},{96,160},{112,176},{65,129},{81,145},{97,161},{1... | collective-permute-start | bytes 122888 | tf_op jit(solution)/shard_map/cond/branch_0_fun/ppermute | solution.py:465
  26.5 1.3 %collective-permute-start.5 = (bf16[160,128]{1,0:T(8,128)(2,1)S(1)}, bf16[160,128]{1,0:T(8,128)(2,1)S(1)}, u32[]{:S(2)}, u32[]{:S(2)}) collective-permute-start(bf16[160,128]{1,0:T(8,128)(2,1)S(1)} %branch_0_fun.18), channel_id=1, source_target_pairs={{64,192},{80,208},{96,224},{112,240},{65,193},{81,209},{97,225},{1... | collective-permute-start | bytes 122888 | tf_op jit(solution)/shard_map/cond/branch_0_fun/ppermute | solution.py:465
  27.8 0.7 %collective-permute-start.6 = (bf16[8,768]{1,0:T(8,128)(2,1)S(1)}, bf16[8,768]{1,0:T(8,128)(2,1)S(1)}, u32[]{:S(2)}, u32[]{:S(2)}) collective-permute-start(bf16[8,768]{1,0:T(8,128)(2,1)S(1)} %branch_0_fun.19), channel_id=1, source_target_pairs={{112,128},{113,129},{114,130},{115,131},{116,132},{117,133},{118,1... | collective-permute-start | bytes 36872 | tf_op jit(solution)/shard_map/cond/branch_0_fun/ppermute | solution.py:475
  28.5 9.0 %conditional.4 = (f32[4,128,128]{2,1,0:T(8,128)S(1)}, bf16[4,32,128]{2,1,0:T(8,128)(2,1)S(1)}, bf16[160,128]{1,0:T(8,128)(2,1)S(1)}, bf16[8,768]{1,0:T(8,128)(2,...) conditional(s32[]{:T(128)} %convert_element_type.17, (f32[4,128,128]{2,1,0:T(8,128)S(1)}, ...), branch_computations={%region_7.7_spmd, %region_8.12_spmd} | conditional | flops 4 | bytes 868556 | solution.py:512
  28.5 0.2 branch_0_fun.13
  28.7 8.8 %all_to_all.31 = bf16[4,128,128]{2,1,0:T(8,128)(2,1)S(1)} all-to-all(bf16[4,128,128]{2,1,0:T(8,128)(2,1)S(1)} %get-tuple-element.154), channel_id=1, replica_groups=mesh['dp'=4,'far'=4,'near'=4,'tensor'=16] {'near'}, dimensions={0} | all-to-all | bytes 262144 | tf_op jit(solution)/shard_map/cond/branch_0_fun/cond/branch_0_fun/all_to_all | solution.py:461
  37.4 0.0 collective-permute-done.4
  37.4 0.0 collective-permute-done.5
  37.5 0.0 collective-permute-done.6
  37.5 1.4 %gated.1 = bf16[512,256]{1,0:T(8,128)(2,1)} custom-call(f32[512,256]{1,0:T(8,128)S(1)} %get-tuple-element.245.low, f32[512,256]{1,0:T(8,128)S(1)} %get-tuple-element.248.high, bf16[256,256]{1,0:T(8,128)(2,1)S(1)} %get-tuple-element.242.bcc, bf16[8,768]{1,0:T(8,128)(2,1)S(1)} %get-tuple-element.249.rims_low, bf16[8,768]{1,0:T(8,128)(2,1)S(1)} %get-tuple-element.250.rims_mid, ...), custom_call_target="tpu_custom_call" | custom-call | tf_op jit(solution)/shard_map/gated/pallas_call | solution.py:542
  (9 shorter events, 0.2 us)
Async XLA Ops:
  2.8 22.1 %collective-permute-start = (bf16[160,128]{1,0:T(8,128)(2,1)S(1)}, bf16[160,128]{1,0:T(8,128)(2,1)S(1)}, u32[]{:S(2)}, u32[]{:S(2)}) collective-permute-start(bf16[160,128]{1,0:T(8,128)(2,1)S(1)} %get-tuple-element.135), channel_id=1, source_target_pairs={{0,64},{16,80},{32,96},{48,112},{1,65},{17,81},{33,97},{49,113},{2... | collective-permute-start | bytes 122888 | tf_op jit(solution)/shard_map/cond/branch_1_fun/ppermute | solution.py:465
  4.1 20.3 %collective-permute-start.1 = (bf16[8,768]{1,0:T(8,128)(2,1)S(1)}, bf16[8,768]{1,0:T(8,128)(2,1)S(1)}, u32[]{:S(2)}, u32[]{:S(2)}) collective-permute-start(bf16[8,768]{1,0:T(8,128)(2,1)S(1)} %branch_1_fun.17), channel_id=1, source_target_pairs={{0,16},{16,32},{32,48},{48,64},{64,80},{80,96},{96,112},{1,17},{17... | collective-permute-start | bytes 36872 | tf_op jit(solution)/shard_map/cond/branch_1_fun/ppermute | solution.py:475
  25.2 12.3 %collective-permute-start.4 = (bf16[160,128]{1,0:T(8,128)(2,1)S(1)}, bf16[160,128]{1,0:T(8,128)(2,1)S(1)}, u32[]{:S(2)}, u32[]{:S(2)}) collective-permute-start(bf16[160,128]{1,0:T(8,128)(2,1)S(1)} %branch_0_fun.18), channel_id=1, source_target_pairs={{64,128},{80,144},{96,160},{112,176},{65,129},{81,145},{97,161},{1... | collective-permute-start | bytes 122888 | tf_op jit(solution)/shard_map/cond/branch_0_fun/ppermute | solution.py:465
  26.5 11.0 %collective-permute-start.5 = (bf16[160,128]{1,0:T(8,128)(2,1)S(1)}, bf16[160,128]{1,0:T(8,128)(2,1)S(1)}, u32[]{:S(2)}, u32[]{:S(2)}) collective-permute-start(bf16[160,128]{1,0:T(8,128)(2,1)S(1)} %branch_0_fun.18), channel_id=1, source_target_pairs={{64,192},{80,208},{96,224},{112,240},{65,193},{81,209},{97,225},{1... | collective-permute-start | bytes 122888 | tf_op jit(solution)/shard_map/cond/branch_0_fun/ppermute | solution.py:465
  27.8 9.7 %collective-permute-start.6 = (bf16[8,768]{1,0:T(8,128)(2,1)S(1)}, bf16[8,768]{1,0:T(8,128)(2,1)S(1)}, u32[]{:S(2)}, u32[]{:S(2)}) collective-permute-start(bf16[8,768]{1,0:T(8,128)(2,1)S(1)} %branch_0_fun.19), channel_id=1, source_target_pairs={{112,128},{113,129},{114,130},{115,131},{116,132},{117,133},{118,1... | collective-permute-start | bytes 36872 | tf_op jit(solution)/shard_map/cond/branch_0_fun/ppermute | solution.py:475

commit v8 on v7

--- a/solution.py
+++ b/solution.py
@@ -40,13 +40,14 @@
 
 
 def load_kernel(
-    group, member, bc, bw, x, dt, xw, xb, bb, bias, a_log, skip,
+    group, member, bc_0, bc_1, x_0, x_1, x_2, x_3, bw, dt, xw, xb, bb, bias, a_log, skip,
     last, first, x_out, bc_out, dt_out, x_taps, bc_taps, own_taps, per_head,
 ):
-    channels = x.shape[0]
+    channels = x_out.shape[0]
     heads = dt.shape[0]
     begin, finish = picks(0), picks(125)
-    series, mine = x[...], bc[0]
+    series = jnp.concatenate([x_0[...], x_1[...], x_2[...], x_3[...]], axis=0)
+    mine = jnp.concatenate([bc_0[0], bc_1[0]], axis=0)
     last[:, :channels] = dot(finish, series[:, 128:], 1, 1).astype(BF16)
     last[:, channels:] = dot(finish, mine[:, 128:], 1, 1).astype(BF16)
     first[:, :channels] = dot(begin, series[:, :128], 1, 1).astype(BF16)
@@ -419,14 +420,16 @@
         grid_spec=pltpu.PrefetchScalarGridSpec(
             num_scalar_prefetch=2,
             grid=(1,),
-            in_specs=[pl.BlockSpec((1,) + a.shape[1:], lambda i, g, m: (g[0], 0, 0)) for a in (bc_in, taps)]
-            + [pl.BlockSpec(a.shape, lambda i, g, m: (0, 0)) for a in [x_in] + small],
+            in_specs=[pl.BlockSpec((1, states, length), lambda i, g, m, p=p: (g[0], p, 0)) for p in range(2)]
+            + [pl.BlockSpec((quarter, length), lambda i, g, m, p=p: (p, 0)) for p in range(LO)]
+            + [pl.BlockSpec((1,) + taps.shape[1:], lambda i, g, m: (g[0], 0, 0))]
+            + [pl.BlockSpec(a.shape, lambda i, g, m: (0, 0)) for a in small],
             out_specs=[VMEM] * len(outs),
         ),
         out_shape=outs,
         name="load",
         compiler_params=GRANT,
-    )(group, member, *[pltpu.with_memory_space_constraint(a, pltpu.HBM) for a in (bc_in, taps, x_in, *small)])
+    )(group, member, *[pltpu.with_memory_space_constraint(a, pltpu.HBM) for a in (bc_in, bc_in, *[x_in] * LO, taps, *small)])
     outs = [shape(LO, quarter + META, states, dtype=BF16), series, pairs]
     outs += [shape(heads, length), shape(heads, length), series]
     args = [x, bc, dt, x_taps, bc_taps, per_head, last, first]

time: 39.1 us -> 39.1 us (level)
  no operation moved by 1% of the time
where the time goes in v8:
time: 39.1 us; the launch traced here: 38.8 us
  blocking collectives  20.8 us (53%)
  starting transfers between devices  8.82 us (23%)
  Pallas kernels  5.46 us (14%)
  waiting for transfers between devices  3.5 us (9%)
    all_to_all x1, blocking collectives, gather(): got = lax.all_to_all(pay, 'near', 0, 0, tiled=True)  12 us
    all_to_all x1, blocking collectives, exchange(): return tuple(rest) + (lax.all_to_all(entering, 'near', 0, 0, tiled=True),)  8.76 us
    ppermute x2, starting transfers between devices, shifted(): lax.ppermute(kept_on(last)[0], cp, [(i, i + 1) for i in range(begin, end)])  4.94 us
    ppermute x3, starting transfers between devices, sent(): return lax.ppermute(block, cp, route)  3.88 us
    ppermute x2, waiting for transfers between devices, shifted(): lax.ppermute(kept_on(last)[0], cp, [(i, i + 1) for i in range(begin, end)])  2.98 us
    pallas_call x11, Pallas kernels, run(): pl.pallas_call(kernel, out_shape=outs, in_specs=[VMEM] * len(args), out_s...  1.46 us
    pallas_call x1, Pallas kernels, local(): pl.pallas_call(output_kernel, out_shape=jax.ShapeDtypeStruct((channels, l...  1.35 us
    pallas_call x1, Pallas kernels, local(): pl.pallas_call(state_kernel, out_shape=outs, in_specs=[pl.BlockSpec(memor...  1.35 us
  transfers between devices with their start and end apart: 5, of which 2 were waited for; matrix products, arithmetic and copies ran while one was open for 0% of the time, Pallas kernels for 3%

profile of v8, /device:TPU:256, one launch (start us, length us, event | category | flops | bytes accessed | tf_op | source)
XLA Modules:
  0.0 38.8 jit_solution(11835541024471623682)
XLA Ops:
  0.0 1.3 %load.1 = (bf16[8,768]{1,0:T(8,128)(2,1)S(1)}, bf16[8,768]{1,0:T(8,128)(2,1)S(1)}, bf16[512,256]{1,0:T(8,128)(2,1)S(1)}, bf16[256,256]{1,0:T(8,128)(2,1)S(1)}, b...) custom-call(s32[1]{0:T(128)} %bitcast.3.group, ...), custom_call_target="tpu_custom_call" | custom-call | tf_op jit(solution)/shard_map/load/pallas_call | solution.py:418
  1.3 1.4 %states.1 = (bf16[4,160,128]{2,1,0:T(8,128)(2,1)S(1)}, bf16[512,256]{1,0:T(8,128)(2,1)S(1)}, bf16[256,256]{1,0:T(8,128)(2,1)S(1)}, f32[8,256]{1,0:T(8,128)S(1)},...) custom-call(bf16[512,256]{1,0:T(8,128)(2,1)} %z.1, bf16[512,256]{1,0:T(8,128)(2,1)S(1)} %get-tuple-element.231.x, ...), custom_call_target="tpu_custom_call" | custom-call | tf_op jit(solution)/shard_map/states/pallas_call | solution.py:436
  2.7 22.2 %conditional.8 = ((f32[4,128,128]{2,1,0:T(8,128)S(1)}, bf16[448,128]{1,0:T(8,128)(2,1)S(1)}, bf16[8,768]{1,0:T(8,128)(2,1)S(1)}, f32[512,256]{1,0:T(8,128)S(1)})) conditional(s32[]{:T(128)} %convert_element_type.20, () %tuple.64, (s32[]{:T(128)}, bf16[4,160,128]{2,1,0:T(8,128)(2,1)S(1)}, f32[2,8,128]{2,1,0:T(8,128)S(1)}, ...), branch_computations={%region_0.1_spmd, %region_1.6_spmd} | conditional | flops 2 | bytes 868534 | solution.py:535
  2.7 1.3 %collective-permute-start = (bf16[160,128]{1,0:T(8,128)(2,1)S(1)}, bf16[160,128]{1,0:T(8,128)(2,1)S(1)}, u32[]{:S(2)}, u32[]{:S(2)}) collective-permute-start(bf16[160,128]{1,0:T(8,128)(2,1)S(1)} %get-tuple-element.135), channel_id=1, source_target_pairs={{0,64},{16,80},{32,96},{48,112},{1,65},{17,81},{33,97},{49,113},{2... | collective-permute-start | bytes 122888 | tf_op jit(solution)/shard_map/cond/branch_1_fun/ppermute | solution.py:468
  4.1 4.3 %collective-permute-start.1 = (bf16[8,768]{1,0:T(8,128)(2,1)S(1)}, bf16[8,768]{1,0:T(8,128)(2,1)S(1)}, u32[]{:S(2)}, u32[]{:S(2)}) collective-permute-start(bf16[8,768]{1,0:T(8,128)(2,1)S(1)} %branch_1_fun.17), channel_id=1, source_target_pairs={{0,16},{16,32},{32,48},{48,64},{64,80},{80,96},{96,112},{1,17},{17... | collective-permute-start | bytes 36872 | tf_op jit(solution)/shard_map/cond/branch_1_fun/ppermute | solution.py:478
  8.3 12.3 %conditional.1 = ((f32[4,128,128]{2,1,0:T(8,128)S(1)}, bf16[4,32,128]{2,1,0:T(8,128)(2,1)S(1)}, bf16[160,128]{1,0:T(8,128)(2,1)S(1)}, bf16[4,128,128]{2,1,0:T(8,128)(2,1)S(1)})) conditional(s32[]{:T(128)} %convert_element_type.5, (bf16[4,160,128]{2,1,0:T(8,128)(2,1)S(1)}, f32[2,8,128]{2,1,0:T(8,128)S(1)}) %tuple.43, (f32[4,128,128]{2,1,0:T(8,128)S(1)}, ...), branch_computations={%region_4.4_spmd, %region_5.5_spmd} | conditional | bytes 327688 | solution.py:491
  8.4 12.0 %all_to_all.29.refs_0_ = bf16[4,160,128]{2,1,0:T(8,128)(2,1)S(1)} all-to-all(bf16[4,160,128]{2,1,0:T(8,128)(2,1)S(1)} %get-tuple-element.118), channel_id=1, replica_groups=mesh['dp'=4,'far'=4,'near'=4,'tensor'=16] {'near'}, dimensions={0} | all-to-all | bytes 327680 | tf_op jit(solution)/shard_map/cond/branch_1_fun/cond/branch_0_fun/all_to_all | solution.py:454
  20.4 0.2 branch_0_fun.12
  20.6 0.7 %branch_1_fun.19 = f32[512,256]{1,0:T(8,128)S(1)} custom-call(bf16[512,256]{1,0:T(8,128)(2,1)S(1)} %get-tuple-element.140.xc, bf16[256,256]{1,0:T(8,128)(2,1)S(1)} %get-tuple-element.141.bcc, f32[8,256]{1,0:T(8,128)S(1)} %get-tuple-element.142.cum_in, f32[8,256]{1,0:T(8,128)S(1)} %get-tuple-element.143.less_in, f32[3,8,128]{2,1,0:T(8,128)S(1)} %get-tuple-element.144.per_head), custom_call_target="tpu_custom_call" | custom-call | tf_op jit(solution)/shard_map/cond/branch_1_fun/pallas_call | solution.py:390
  21.3 3.0 %collective-permute-done.1.refs_0_ = bf16[8,768]{1,0:T(8,128)(2,1)S(1)} collective-permute-done((bf16[8,768]{1,0:T(8,128)(2,1)S(1)}, bf16[8,768]{1,0:T(8,128)(2,1)S(1)}, u32[]{:S(2)}, u32[]{:S(2)}) %collective-permute-start.1) | collective-permute-done | bytes 12320 | tf_op jit(solution)/shard_map/cond/branch_1_fun/ppermute | solution.py:478
  24.3 0.5 %collective-permute-done.near = bf16[160,128]{1,0:T(8,128)(2,1)S(1)} collective-permute-done((bf16[160,128]{1,0:T(8,128)(2,1)S(1)}, bf16[160,128]{1,0:T(8,128)(2,1)S(1)}, u32[]{:S(2)}, u32[]{:S(2)}) %collective-permute-start) | collective-permute-done | bytes 40992 | tf_op jit(solution)/shard_map/cond/branch_1_fun/ppermute | solution.py:468
  24.9 12.6 %conditional.9 = (f32[512,256]{1,0:T(8,128)S(1)}, bf16[8,768]{1,0:T(8,128)(2,1)S(1)}, bf16[8,768]{1,0:T(8,128)(2,1)S(1)}, bf16[512,128]{1,0:T(8,128)(2,1)S(1)}) conditional(s32[]{:T(128)} %convert_element_type.21, (s32[]{:T(128)}, bf16[448,128]{1,0:T(8,128)(2,1)S(1)}, f32[4,128,128]{2,1,0:T(8,128)S(1)}, f32[2,8,128]{2,1,0:T(8,128)S(1)}, ...), branch_computations={%region_6.15_spmd, %region_15.16_spmd} | conditional | flops 6 | bytes 1507858 | solution.py:536
  24.9 0.2 branch_0_fun.18
  25.1 1.3 %collective-permute-start.4 = (bf16[160,128]{1,0:T(8,128)(2,1)S(1)}, bf16[160,128]{1,0:T(8,128)(2,1)S(1)}, u32[]{:S(2)}, u32[]{:S(2)}) collective-permute-start(bf16[160,128]{1,0:T(8,128)(2,1)S(1)} %branch_0_fun.18), channel_id=1, source_target_pairs={{64,128},{80,144},{96,160},{112,176},{65,129},{81,145},{97,161},{1... | collective-permute-start | bytes 122888 | tf_op jit(solution)/shard_map/cond/branch_0_fun/ppermute | solution.py:468
  26.4 1.3 %collective-permute-start.5 = (bf16[160,128]{1,0:T(8,128)(2,1)S(1)}, bf16[160,128]{1,0:T(8,128)(2,1)S(1)}, u32[]{:S(2)}, u32[]{:S(2)}) collective-permute-start(bf16[160,128]{1,0:T(8,128)(2,1)S(1)} %branch_0_fun.18), channel_id=1, source_target_pairs={{64,192},{80,208},{96,224},{112,240},{65,193},{81,209},{97,225},{1... | collective-permute-start | bytes 122888 | tf_op jit(solution)/shard_map/cond/branch_0_fun/ppermute | solution.py:468
  27.7 0.7 %collective-permute-start.6 = (bf16[8,768]{1,0:T(8,128)(2,1)S(1)}, bf16[8,768]{1,0:T(8,128)(2,1)S(1)}, u32[]{:S(2)}, u32[]{:S(2)}) collective-permute-start(bf16[8,768]{1,0:T(8,128)(2,1)S(1)} %branch_0_fun.19), channel_id=1, source_target_pairs={{112,128},{113,129},{114,130},{115,131},{116,132},{117,133},{118,1... | collective-permute-start | bytes 36872 | tf_op jit(solution)/shard_map/cond/branch_0_fun/ppermute | solution.py:478
  28.4 9.0 %conditional.4 = (f32[4,128,128]{2,1,0:T(8,128)S(1)}, bf16[4,32,128]{2,1,0:T(8,128)(2,1)S(1)}, bf16[160,128]{1,0:T(8,128)(2,1)S(1)}, bf16[8,768]{1,0:T(8,128)(2,...) conditional(s32[]{:T(128)} %convert_element_type.17, (f32[4,128,128]{2,1,0:T(8,128)S(1)}, ...), branch_computations={%region_7.7_spmd, %region_8.12_spmd} | conditional | flops 4 | bytes 868556 | solution.py:515
  28.4 0.2 branch_0_fun.13
  28.6 8.8 %all_to_all.31 = bf16[4,128,128]{2,1,0:T(8,128)(2,1)S(1)} all-to-all(bf16[4,128,128]{2,1,0:T(8,128)(2,1)S(1)} %get-tuple-element.154), channel_id=1, replica_groups=mesh['dp'=4,'far'=4,'near'=4,'tensor'=16] {'near'}, dimensions={0} | all-to-all | bytes 262144 | tf_op jit(solution)/shard_map/cond/branch_0_fun/cond/branch_0_fun/all_to_all | solution.py:464
  37.4 0.0 collective-permute-done.4
  37.4 0.0 collective-permute-done.5
  37.4 0.0 collective-permute-done.6
  37.4 1.4 %gated.1 = bf16[512,256]{1,0:T(8,128)(2,1)} custom-call(f32[512,256]{1,0:T(8,128)S(1)} %get-tuple-element.245.low, f32[512,256]{1,0:T(8,128)S(1)} %get-tuple-element.248.high, bf16[256,256]{1,0:T(8,128)(2,1)S(1)} %get-tuple-element.242.bcc, bf16[8,768]{1,0:T(8,128)(2,1)S(1)} %get-tuple-element.249.rims_low, bf16[8,768]{1,0:T(8,128)(2,1)S(1)} %get-tuple-element.250.rims_mid, ...), custom_call_target="tpu_custom_call" | custom-call | tf_op jit(solution)/shard_map/gated/pallas_call | solution.py:545
  (9 shorter events, 0.2 us)
Async XLA Ops:
  2.7 22.1 %collective-permute-start = (bf16[160,128]{1,0:T(8,128)(2,1)S(1)}, bf16[160,128]{1,0:T(8,128)(2,1)S(1)}, u32[]{:S(2)}, u32[]{:S(2)}) collective-permute-start(bf16[160,128]{1,0:T(8,128)(2,1)S(1)} %get-tuple-element.135), channel_id=1, source_target_pairs={{0,64},{16,80},{32,96},{48,112},{1,65},{17,81},{33,97},{49,113},{2... | collective-permute-start | bytes 122888 | tf_op jit(solution)/shard_map/cond/branch_1_fun/ppermute | solution.py:468
  4.1 20.3 %collective-permute-start.1 = (bf16[8,768]{1,0:T(8,128)(2,1)S(1)}, bf16[8,768]{1,0:T(8,128)(2,1)S(1)}, u32[]{:S(2)}, u32[]{:S(2)}) collective-permute-start(bf16[8,768]{1,0:T(8,128)(2,1)S(1)} %branch_1_fun.17), channel_id=1, source_target_pairs={{0,16},{16,32},{32,48},{48,64},{64,80},{80,96},{96,112},{1,17},{17... | collective-permute-start | bytes 36872 | tf_op jit(solution)/shard_map/cond/branch_1_fun/ppermute | solution.py:478
  25.1 12.3 %collective-permute-start.4 = (bf16[160,128]{1,0:T(8,128)(2,1)S(1)}, bf16[160,128]{1,0:T(8,128)(2,1)S(1)}, u32[]{:S(2)}, u32[]{:S(2)}) collective-permute-start(bf16[160,128]{1,0:T(8,128)(2,1)S(1)} %branch_0_fun.18), channel_id=1, source_target_pairs={{64,128},{80,144},{96,160},{112,176},{65,129},{81,145},{97,161},{1... | collective-permute-start | bytes 122888 | tf_op jit(solution)/shard_map/cond/branch_0_fun/ppermute | solution.py:468
  26.4 11.0 %collective-permute-start.5 = (bf16[160,128]{1,0:T(8,128)(2,1)S(1)}, bf16[160,128]{1,0:T(8,128)(2,1)S(1)}, u32[]{:S(2)}, u32[]{:S(2)}) collective-permute-start(bf16[160,128]{1,0:T(8,128)(2,1)S(1)} %branch_0_fun.18), channel_id=1, source_target_pairs={{64,192},{80,208},{96,224},{112,240},{65,193},{81,209},{97,225},{1... | collective-permute-start | bytes 122888 | tf_op jit(solution)/shard_map/cond/branch_0_fun/ppermute | solution.py:468
  27.7 9.7 %collective-permute-start.6 = (bf16[8,768]{1,0:T(8,128)(2,1)S(1)}, bf16[8,768]{1,0:T(8,128)(2,1)S(1)}, u32[]{:S(2)}, u32[]{:S(2)}) collective-permute-start(bf16[8,768]{1,0:T(8,128)(2,1)S(1)} %branch_0_fun.19), channel_id=1, source_target_pairs={{112,128},{113,129},{114,130},{115,131},{116,132},{117,133},{118,1... | collective-permute-start | bytes 36872 | tf_op jit(solution)/shard_map/cond/branch_0_fun/ppermute | solution.py:478

commit v9 on v8

--- a/solution.py
+++ b/solution.py
@@ -450,8 +450,8 @@
         *[pltpu.with_memory_space_constraint(a, pltpu.VMEM) for a in args],
     )
 
-    def gather(*rest, opening=False):
-        got = lax.all_to_all(pay, "near", 0, 0, tiled=True)
+    def gather(*rest, opening=False, source=pay):
+        got = lax.all_to_all(source, "near", 0, 0, tiled=True)
         kernel = lambda *refs: group_kernel(*refs, per=per, opening=opening)
         return tuple(run(kernel, [*kept_shapes, *rest], got, own_taps))
 
@@ -483,8 +483,14 @@
     packed_shapes = [kept_shapes[0], shape(packed_rows_count, states, dtype=BF16)]
 
     def low_part():
+        ahead = jnp.logical_and(far == 0, member[0] > 0)
+        (begun,) = lax.cond(ahead, lambda: (inside(less),), lambda: blank(inner_shape))
+        ready, begun = lax.optimization_barrier((pay, begun))
         kept = lax.cond(
-            far == 0, lambda: gather(block_shape, opening=True), lambda: blank(*kept_shapes, block_shape)
+            far == 0,
+            lambda ready: gather(block_shape, opening=True, source=ready),
+            lambda ready: blank(*kept_shapes, block_shape),
+            ready,
         )
         near = sent(kept[2], 0, 1)
         rims = shifted(0, 2 * LO - 1)
@@ -494,9 +500,10 @@
             lambda *kept: gather(block_shape, state_shape),
             *kept,
         )
-        inner = inside(begin)
+        begin, begun = lax.optimization_barrier((begin, begun))
+        (inner,) = lax.cond(ahead, lambda begun: kept_on(begun), lambda begun: (inside(less),), begun)
         packed = run(pack_kernel, packed_shapes, kept[0], begin, kept[1], kept[2], near)
-        return (*packed, *kept_on(rims), inner)
+        return (*packed, *kept_on(rims, inner))
 
     def high_part(*kept):
         rims = shifted(2 * LO, count - 1)

time: 39.1 us -> 39.2 us (level)
    pallas_call x11 -> x12, Pallas kernels: 1.46 us -> 1.53 us  [run(): pl.pallas_call(kernel, out_shape=outs, in_specs=[VMEM] * len(args), out_s...]
where the time goes in v9:
time: 39.2 us; the launch traced here: 38.9 us
  blocking collectives  20.8 us (53%)
  starting transfers between devices  8.82 us (22%)
  Pallas kernels  5.52 us (14%)
  waiting for transfers between devices  3.44 us (9%)
    all_to_all x1, blocking collectives, gather(): got = lax.all_to_all(source, 'near', 0, 0, tiled=True)  12 us
    all_to_all x1, blocking collectives, exchange(): return tuple(rest) + (lax.all_to_all(entering, 'near', 0, 0, tiled=True),)  8.78 us
    ppermute x2, starting transfers between devices, shifted(): lax.ppermute(kept_on(last)[0], cp, [(i, i + 1) for i in range(begin, end)])  4.94 us
    ppermute x3, starting transfers between devices, sent(): return lax.ppermute(block, cp, route)  3.88 us
    ppermute x2, waiting for transfers between devices, shifted(): lax.ppermute(kept_on(last)[0], cp, [(i, i + 1) for i in range(begin, end)])  2.89 us
    pallas_call x12, Pallas kernels, run(): pl.pallas_call(kernel, out_shape=outs, in_specs=[VMEM] * len(args), out_s...  1.53 us
    pallas_call x1, Pallas kernels, local(): pl.pallas_call(state_kernel, out_shape=outs, in_specs=[pl.BlockSpec(memor...  1.35 us
    pallas_call x1, Pallas kernels, local(): pl.pallas_call(output_kernel, out_shape=jax.ShapeDtypeStruct((channels, l...  1.35 us
  transfers between devices with their start and end apart: 5, of which 2 were waited for; matrix products, arithmetic and copies ran while one was open for 0% of the time, Pallas kernels for 3%

profile of v9, /device:TPU:256, one launch (start us, length us, event | category | flops | bytes accessed | tf_op | source)
XLA Modules:
  0.0 38.9 jit_solution(17897561281814858135)
XLA Ops:
  0.0 1.3 %load.1 = (bf16[8,768]{1,0:T(8,128)(2,1)S(1)}, bf16[8,768]{1,0:T(8,128)(2,1)S(1)}, bf16[512,256]{1,0:T(8,128)(2,1)S(1)}, bf16[256,256]{1,0:T(8,128)(2,1)S(1)}, b...) custom-call(s32[1]{0:T(128)} %bitcast.3.group, ...), custom_call_target="tpu_custom_call" | custom-call | tf_op jit(solution)/shard_map/load/pallas_call | solution.py:418
  1.3 1.4 %states.1 = (bf16[4,160,128]{2,1,0:T(8,128)(2,1)S(1)}, bf16[512,256]{1,0:T(8,128)(2,1)S(1)}, bf16[256,256]{1,0:T(8,128)(2,1)S(1)}, f32[8,256]{1,0:T(8,128)S(1)},...) custom-call(bf16[512,256]{1,0:T(8,128)(2,1)} %z.1, bf16[512,256]{1,0:T(8,128)(2,1)S(1)} %get-tuple-element.278.x, ...), custom_call_target="tpu_custom_call" | custom-call | tf_op jit(solution)/shard_map/states/pallas_call | solution.py:436
  2.7 22.3 %conditional.10 = ((f32[4,128,128]{2,1,0:T(8,128)S(1)}, bf16[448,128]{1,0:T(8,128)(2,1)S(1)}, bf16[8,768]{1,0:T(8,128)(2,1)S(1)}, f32[512,256]{1,0:T(8,128)S(1)})) conditional(s32[]{:T(128)} %convert_element_type.24, () %tuple.79, (s32[]{:T(128)}, s32[]{:T(128)}, f32[8,256]{1,0:T(8,128)S(1)}, bf16[512,256]{1,0:T(8,128)(2,1)S(1)}, ...), branch_computations={%region_0.1_spmd, %region_1.10_spmd} | conditional | flops 5 | bytes 868623 | solution.py:542
  2.7 0.1 conditional
  2.8 0.1 conditional.1
  2.8 1.3 %collective-permute-start = (bf16[160,128]{1,0:T(8,128)(2,1)S(1)}, bf16[160,128]{1,0:T(8,128)(2,1)S(1)}, u32[]{:S(2)}, u32[]{:S(2)}) collective-permute-start(bf16[160,128]{1,0:T(8,128)(2,1)S(1)} %get-tuple-element.185), channel_id=1, source_target_pairs={{0,64},{16,80},{32,96},{48,112},{1,65},{17,81},{33,97},{49,113},{2... | collective-permute-start | bytes 122888 | tf_op jit(solution)/shard_map/cond/branch_1_fun/ppermute | solution.py:468
  4.1 4.3 %collective-permute-start.1 = (bf16[8,768]{1,0:T(8,128)(2,1)S(1)}, bf16[8,768]{1,0:T(8,128)(2,1)S(1)}, u32[]{:S(2)}, u32[]{:S(2)}) collective-permute-start(bf16[8,768]{1,0:T(8,128)(2,1)S(1)} %branch_1_fun.20), channel_id=1, source_target_pairs={{0,16},{16,32},{32,48},{48,64},{64,80},{80,96},{96,112},{1,17},{17... | collective-permute-start | bytes 36872 | tf_op jit(solution)/shard_map/cond/branch_1_fun/ppermute | solution.py:478
  8.4 12.3 %conditional.2 = ((f32[4,128,128]{2,1,0:T(8,128)S(1)}, bf16[4,32,128]{2,1,0:T(8,128)(2,1)S(1)}, bf16[160,128]{1,0:T(8,128)(2,1)S(1)}, bf16[4,128,128]{2,1,0:T(8,128)(2,1)S(1)})) conditional(s32[]{:T(128)} %convert_element_type.1, (bf16[4,160,128]{2,1,0:T(8,128)(2,1)S(1)}, f32[2,8,128]{2,1,0:T(8,128)S(1)}) %tuple.54, (f32[4,128,128]{2,1,0:T(8,128)S(1)}, ...), branch_computations={%region_6.6_spmd, %region_7.7_spmd} | conditional | bytes 327688 | solution.py:497
  8.4 12.0 %all_to_all.29.refs_0_ = bf16[4,160,128]{2,1,0:T(8,128)(2,1)S(1)} all-to-all(bf16[4,160,128]{2,1,0:T(8,128)(2,1)S(1)} %get-tuple-element.153), channel_id=1, replica_groups=mesh['dp'=4,'far'=4,'near'=4,'tensor'=16] {'near'}, dimensions={0} | all-to-all | bytes 327680 | tf_op jit(solution)/shard_map/cond/branch_1_fun/cond/branch_0_fun/all_to_all | solution.py:454
  20.4 0.2 branch_0_fun.15
  20.7 0.7 %conditional.3 = (f32[512,256]{1,0:T(8,128)S(1)}) conditional(s32[]{:T(128)} %convert_element_type.2, (f32[8,256]{1,0:T(8,128)S(1)}, bf16[512,256]{1,0:T(8,128)(2,1)S(1)}, bf16[256,256]{1,0:T(8,128)(2,1)S(1)}, f32[8,256]{1,0:T(8,128)S(1)}, f32[3,8,128]{2,1,0:T(8,128)S(1)}) %tuple.57, f32[512,256]{1,0:T(8,128)S(1)} %get-tuple-element.361), branch_computations={%region_8.8_spmd, %region_9.9_spmd} | conditional | bytes 8 | solution.py:504
  20.7 0.7 %branch_0_fun.16 = f32[512,256]{1,0:T(8,128)S(1)} custom-call(bf16[512,256]{1,0:T(8,128)(2,1)S(1)} %get-tuple-element.163.xc, bf16[256,256]{1,0:T(8,128)(2,1)S(1)} %get-tuple-element.164.bcc, f32[8,256]{1,0:T(8,128)S(1)} %get-tuple-element.165.cum_in, f32[8,256]{1,0:T(8,128)S(1)} %get-tuple-element.161.less_in, f32[3,8,128]{2,1,0:T(8,128)S(1)} %get-tuple-element.166.per_head), custom_call_target="tpu_custom_call" | custom-call | tf_op jit(solution)/shard_map/cond/branch_1_fun/cond/branch_0_fun/pallas_call | solution.py:390
  21.4 2.9 %collective-permute-done.1.refs_0_ = bf16[8,768]{1,0:T(8,128)(2,1)S(1)} collective-permute-done((bf16[8,768]{1,0:T(8,128)(2,1)S(1)}, bf16[8,768]{1,0:T(8,128)(2,1)S(1)}, u32[]{:S(2)}, u32[]{:S(2)}) %collective-permute-start.1) | collective-permute-done | bytes 12320 | tf_op jit(solution)/shard_map/cond/branch_1_fun/ppermute | solution.py:478
  24.3 0.6 %collective-permute-done.near = bf16[160,128]{1,0:T(8,128)(2,1)S(1)} collective-permute-done((bf16[160,128]{1,0:T(8,128)(2,1)S(1)}, bf16[160,128]{1,0:T(8,128)(2,1)S(1)}, u32[]{:S(2)}, u32[]{:S(2)}) %collective-permute-start) | collective-permute-done | bytes 40992 | tf_op jit(solution)/shard_map/cond/branch_1_fun/ppermute | solution.py:468
  24.9 12.6 %conditional.11 = (f32[512,256]{1,0:T(8,128)S(1)}, bf16[8,768]{1,0:T(8,128)(2,1)S(1)}, bf16[8,768]{1,0:T(8,128)(2,1)S(1)}, bf16[512,128]{1,0:T(8,128)(2,1)S(1)}) conditional(s32[]{:T(128)} %convert_element_type.25, (s32[]{:T(128)}, bf16[448,128]{1,0:T(8,128)(2,1)S(1)}, f32[4,128,128]{2,1,0:T(8,128)S(1)}, f32[2,8,128]{2,1,0:T(8,128)S(1)}, ...), branch_computations={%region_10.19_spmd, %region_19.20_spmd} | conditional | flops 6 | bytes 1507858 | solution.py:543
  25.0 0.2 branch_0_fun.22
  25.2 1.3 %collective-permute-start.4 = (bf16[160,128]{1,0:T(8,128)(2,1)S(1)}, bf16[160,128]{1,0:T(8,128)(2,1)S(1)}, u32[]{:S(2)}, u32[]{:S(2)}) collective-permute-start(bf16[160,128]{1,0:T(8,128)(2,1)S(1)} %branch_0_fun.22), channel_id=1, source_target_pairs={{64,128},{80,144},{96,160},{112,176},{65,129},{81,145},{97,161},{1... | collective-permute-start | bytes 122888 | tf_op jit(solution)/shard_map/cond/branch_0_fun/ppermute | solution.py:468
  26.5 1.3 %collective-permute-start.5 = (bf16[160,128]{1,0:T(8,128)(2,1)S(1)}, bf16[160,128]{1,0:T(8,128)(2,1)S(1)}, u32[]{:S(2)}, u32[]{:S(2)}) collective-permute-start(bf16[160,128]{1,0:T(8,128)(2,1)S(1)} %branch_0_fun.22), channel_id=1, source_target_pairs={{64,192},{80,208},{96,224},{112,240},{65,193},{81,209},{97,225},{1... | collective-permute-start | bytes 122888 | tf_op jit(solution)/shard_map/cond/branch_0_fun/ppermute | solution.py:468
  27.8 0.7 %collective-permute-start.6 = (bf16[8,768]{1,0:T(8,128)(2,1)S(1)}, bf16[8,768]{1,0:T(8,128)(2,1)S(1)}, u32[]{:S(2)}, u32[]{:S(2)}) collective-permute-start(bf16[8,768]{1,0:T(8,128)(2,1)S(1)} %branch_0_fun.23), channel_id=1, source_target_pairs={{112,128},{113,129},{114,130},{115,131},{116,132},{117,133},{118,1... | collective-permute-start | bytes 36872 | tf_op jit(solution)/shard_map/cond/branch_0_fun/ppermute | solution.py:478
  28.5 9.0 %conditional.6 = (f32[4,128,128]{2,1,0:T(8,128)S(1)}, bf16[4,32,128]{2,1,0:T(8,128)(2,1)S(1)}, bf16[160,128]{1,0:T(8,128)(2,1)S(1)}, bf16[8,768]{1,0:T(8,128)(2,...) conditional(s32[]{:T(128)} %convert_element_type.21, (f32[4,128,128]{2,1,0:T(8,128)S(1)}, ...), branch_computations={%region_11.11_spmd, %region_12.16_spmd} | conditional | flops 4 | bytes 868556 | solution.py:522
  28.5 0.2 branch_0_fun.17
  28.7 8.8 %all_to_all.31 = bf16[4,128,128]{2,1,0:T(8,128)(2,1)S(1)} all-to-all(bf16[4,128,128]{2,1,0:T(8,128)(2,1)S(1)} %get-tuple-element.201), channel_id=1, replica_groups=mesh['dp'=4,'far'=4,'near'=4,'tensor'=16] {'near'}, dimensions={0} | all-to-all | bytes 262144 | tf_op jit(solution)/shard_map/cond/branch_0_fun/cond/branch_0_fun/all_to_all | solution.py:464
  37.5 0.0 collective-permute-done.4
  37.5 0.0 collective-permute-done.5
  37.5 0.0 collective-permute-done.6
  37.5 1.4 %gated.1 = bf16[512,256]{1,0:T(8,128)(2,1)} custom-call(f32[512,256]{1,0:T(8,128)S(1)} %get-tuple-element.292.low, f32[512,256]{1,0:T(8,128)S(1)} %get-tuple-element.295.high, bf16[256,256]{1,0:T(8,128)(2,1)S(1)} %get-tuple-element.288.bcc, bf16[8,768]{1,0:T(8,128)(2,1)S(1)} %get-tuple-element.296.rims_low, bf16[8,768]{1,0:T(8,128)(2,1)S(1)} %get-tuple-element.297.rims_mid, ...), custom_call_target="tpu_custom_call" | custom-call | tf_op jit(solution)/shard_map/gated/pallas_call | solution.py:552
  (9 shorter events, 0.2 us)
Async XLA Ops:
  2.8 22.1 %collective-permute-start = (bf16[160,128]{1,0:T(8,128)(2,1)S(1)}, bf16[160,128]{1,0:T(8,128)(2,1)S(1)}, u32[]{:S(2)}, u32[]{:S(2)}) collective-permute-start(bf16[160,128]{1,0:T(8,128)(2,1)S(1)} %get-tuple-element.185), channel_id=1, source_target_pairs={{0,64},{16,80},{32,96},{48,112},{1,65},{17,81},{33,97},{49,113},{2... | collective-permute-start | bytes 122888 | tf_op jit(solution)/shard_map/cond/branch_1_fun/ppermute | solution.py:468
  4.1 20.2 %collective-permute-start.1 = (bf16[8,768]{1,0:T(8,128)(2,1)S(1)}, bf16[8,768]{1,0:T(8,128)(2,1)S(1)}, u32[]{:S(2)}, u32[]{:S(2)}) collective-permute-start(bf16[8,768]{1,0:T(8,128)(2,1)S(1)} %branch_1_fun.20), channel_id=1, source_target_pairs={{0,16},{16,32},{32,48},{48,64},{64,80},{80,96},{96,112},{1,17},{17... | collective-permute-start | bytes 36872 | tf_op jit(solution)/shard_map/cond/branch_1_fun/ppermute | solution.py:478
  25.2 12.3 %collective-permute-start.4 = (bf16[160,128]{1,0:T(8,128)(2,1)S(1)}, bf16[160,128]{1,0:T(8,128)(2,1)S(1)}, u32[]{:S(2)}, u32[]{:S(2)}) collective-permute-start(bf16[160,128]{1,0:T(8,128)(2,1)S(1)} %branch_0_fun.22), channel_id=1, source_target_pairs={{64,128},{80,144},{96,160},{112,176},{65,129},{81,145},{97,161},{1... | collective-permute-start | bytes 122888 | tf_op jit(solution)/shard_map/cond/branch_0_fun/ppermute | solution.py:468
  26.5 11.0 %collective-permute-start.5 = (bf16[160,128]{1,0:T(8,128)(2,1)S(1)}, bf16[160,128]{1,0:T(8,128)(2,1)S(1)}, u32[]{:S(2)}, u32[]{:S(2)}) collective-permute-start(bf16[160,128]{1,0:T(8,128)(2,1)S(1)} %branch_0_fun.22), channel_id=1, source_target_pairs={{64,192},{80,208},{96,224},{112,240},{65,193},{81,209},{97,225},{1... | collective-permute-start | bytes 122888 | tf_op jit(solution)/shard_map/cond/branch_0_fun/ppermute | solution.py:468
  27.8 9.7 %collective-permute-start.6 = (bf16[8,768]{1,0:T(8,128)(2,1)S(1)}, bf16[8,768]{1,0:T(8,128)(2,1)S(1)}, u32[]{:S(2)}, u32[]{:S(2)}) collective-permute-start(bf16[8,768]{1,0:T(8,128)(2,1)S(1)} %branch_0_fun.23), channel_id=1, source_target_pairs={{112,128},{113,129},{114,130},{115,131},{116,132},{117,133},{118,1... | collective-permute-start | bytes 36872 | tf_op jit(solution)/shard_map/cond/branch_0_fun/ppermute | solution.py:478
